TPU v7x, 256 devices: a whole 4x4x8 slice. The times are simulated.
256 devices in a mesh: dom: 256 (over z, x, y, core).
Axes of the slice: x: 4, y: 4, z: 8, core: 2. Of those that a mesh axis runs over, the one named last changes fastest.
Arguments:
- entities: float32 [262144, 200], P('dom'), may hold values from -3 to 3
- entity_state: float32 [262144], P('dom'), may hold values from 1e-05 to 0.1
- relations: float32 [1345, 200], replicated, may hold values from -3 to 3
- relation_state: float32 [1345], replicated, may hold values from 1 to 100
- edges: int32 [2, 3, 131072], P(None, None, 'dom'), may hold values from 0 to 1344, as said below
- negatives: int32 [2, 1024, 1000], P(None, 'dom'), may hold values from 0 to 1023
- counts: int32 [2, 256], P(None, 'dom'), may hold values from 1 to 512, as said below
Outputs:
- entities_after: float32 [262144, 200], P('dom')
- entity_state_after: float32 [262144], P('dom')
- relations_after: float32 [1345, 200], replicated
- relation_state_after: float32 [1345], replicated
Inputs may be any that keep to these rules, and one draw needn't show every extreme that they name: `edges`: rows 0 and 2 are local entity ids below 1024; row 1 holds relation ids below 1345. `negatives`: local ids in the partner's partition. `counts`: in every round some bucket is full.
All inputs are finite; a program needn't handle non-finite values.
Results may differ from a plain program's by a relative error of at most 0.0003.
Values sent between devices are 32-bit elements; how exact they have to be, the bound alone decides.
A program may use at most 64 MiB of HBM per device.

v0:
```python
import jax
import jax.numpy as jnp
from jax import lax
from jax.sharding import Mesh
from jax.sharding import PartitionSpec as P

DOM = ("dom_0", "dom_1", "dom_2", "dom_3")


RATE = 0.2
HIGH = lax.Precision.HIGHEST


def swapped(block, axis, apart):
    count = lax.axis_size(axis)
    route = []
    for low in range(count):
        high = low | 1 << apart
        if high != low and high < count:
            route += [(low, high), (high, low)]
    return lax.ppermute(block, axis, route)


def padded_to(lines, count):
    spare = -len(lines) % count
    return jnp.pad(lines, [(0, spare)] + [(0, 0)] * (lines.ndim - 1))


def from_everyone(value, axis):
    count = lax.axis_size(axis)
    return lax.all_to_all(
        jnp.broadcast_to(value[None], (count, *value.shape)), axis, 0, 0, tiled=True
    )


def in_order(pieces, dim):
    pieces = jnp.moveaxis(pieces, 0, dim)
    shape = pieces.shape
    return pieces.reshape(*shape[:dim], shape[dim] * shape[dim + 1], *shape[dim + 2 :])


def whole_of(value, axes, dim):
    far, near = axes
    pieces = from_everyone(from_everyone(value, far), near)
    return in_order(pieces.swapaxes(0, 1).reshape(-1, *value.shape), dim)


def split_up(value, dim, count):
    shape = value.shape
    pieces = value.reshape(*shape[:dim], count, shape[dim] // count, *shape[dim + 1 :])
    return jnp.moveaxis(pieces, dim, 0)


def summed_on_arrival(value, axis, dim):
    count = lax.axis_size(axis)
    pieces = lax.all_to_all(split_up(value, dim, count), axis, 0, 0, tiled=True)
    return jnp.sum(pieces, axis=0)


def sum_in_two_steps(value, axes, dim):
    far, near = axes
    pieces = split_up(value, dim, lax.axis_size(far))
    nearer = summed_on_arrival(pieces, near, dim + 1)
    arrived = lax.all_to_all(nearer, far, split_axis=0, concat_axis=0, tiled=True)
    return arrived.sum(axis=0)


def total_of(value, axes):
    lines = value.reshape(-1)
    padded = padded_to(lines, lax.axis_size(axes[0]) * lax.axis_size(axes[1]))
    whole = whole_of(sum_in_two_steps(padded, axes, 0), axes, 0)
    return lax.slice_in_dim(whole, 0, len(lines)).reshape(value.shape)


def block_terms(carry, table, relations, source, relation, target, negative_ids, live):
    grad_table, grad_relation = carry
    half = table.shape[1] // 2
    src_rows = table[source]
    tgt_rows = table[target]
    neg_rows = table[negative_ids]
    rel_rows = relations[relation]
    src_real, src_imag = (src_rows[:, :half], src_rows[:, half:])
    rel_real, rel_imag = (rel_rows[:, :half], rel_rows[:, half:])
    product = jnp.concatenate(
        [src_real * rel_real - src_imag * rel_imag, src_real * rel_imag + src_imag * rel_real],
        axis=1,
    )
    positive = jnp.sum(product * tgt_rows, axis=1)
    negative = lax.dot_general(
        product,
        neg_rows,
        (((1,), (1,)), ((), ())),
        precision=HIGH,
        preferred_element_type=jnp.float32,
    )
    pos_weight = -jax.nn.sigmoid(-positive) * live
    neg_weight = jax.nn.sigmoid(negative) * (live[:, None] / negative.shape[1])
    upstream = pos_weight[:, None] * tgt_rows + jnp.dot(
        neg_weight, neg_rows, precision=HIGH, preferred_element_type=jnp.float32
    )
    target_grad = pos_weight[:, None] * product
    negative_grad = lax.dot_general(
        neg_weight,
        product,
        (((0,), (0,)), ((), ())),
        precision=HIGH,
        preferred_element_type=jnp.float32,
    )
    up_real, up_imag = (upstream[:, :half], upstream[:, half:])
    source_grad = jnp.concatenate(
        [up_real * rel_real + up_imag * rel_imag, up_imag * rel_real - up_real * rel_imag], axis=1
    )
    relation_grad = jnp.concatenate(
        [up_real * src_real + up_imag * src_imag, up_imag * src_real - up_real * src_imag], axis=1
    )
    grad_table = (
        grad_table.at[source]
        .add(source_grad)
        .at[target]
        .add(target_grad)
        .at[negative_ids]
        .add(negative_grad)
    )
    grad_relation = grad_relation.at[relation].add(relation_grad)
    return (grad_table, grad_relation)


def bucket_pass(
    carry,
    table,
    relations,
    edge_pair,
    negative_pair,
    count_pair,
    source_shift,
    target_shift,
    block,
    first,
    last,
):
    block_pair = (count_pair + block - 1) // block

    def visit(index, inner):
        which = (index >= block_pair[0]).astype(jnp.int32)
        number = index - which * block_pair[0]
        edge_list = lax.dynamic_index_in_dim(edge_pair, which, 0, keepdims=False)
        start = number * block
        window = lax.dynamic_slice_in_dim(edge_list, start, block, 1)
        negative_list = lax.dynamic_index_in_dim(negative_pair, which, 0, keepdims=False)
        negative_ids = (
            lax.dynamic_index_in_dim(negative_list, number, 0, keepdims=False) + target_shift[which]
        )
        live = (start + jnp.arange(block, dtype=jnp.int32) < count_pair[which]).astype(jnp.float32)
        return block_terms(
            inner,
            table,
            relations,
            window[0] + source_shift[which],
            window[1],
            window[2] + target_shift[which],
            negative_ids,
            live,
        )

    return lax.fori_loop(first, last, visit, carry)


def adagrad(param, state, grad):
    new_state = state + jnp.mean(grad * grad, axis=1)
    return (param - RATE * grad / jnp.sqrt(new_state)[:, None], new_state)


def body(entities, entity_state, relations, relation_state, edges, negatives, counts):
    rows = entities.shape[0]
    blocks_dev = negatives.shape[1]
    block = edges.shape[2] // blocks_dev
    levels = lax.axis_size(DOM).bit_length() - 1
    for round_index, bit in enumerate((levels - 1, 0)):
        partner = swapped(entities, DOM, bit)
        table = jnp.concatenate([entities, partner], axis=0)
        own_edges = edges[round_index]
        own_negatives = negatives[round_index]
        own_count = counts[round_index]
        edge_pair = jnp.stack([own_edges, own_edges])
        negative_pair = jnp.stack([own_negatives, own_negatives])
        count_pair = jnp.concatenate([own_count, own_count])
        source_shift = jnp.array([0, 0], dtype=jnp.int32)
        target_shift = jnp.array([rows, rows], dtype=jnp.int32)
        first = jnp.int32(0)
        last = (own_count[0] + block - 1) // block
        empty = (
            jnp.zeros((2 * rows, entities.shape[1]), jnp.float32),
            jnp.zeros(relations.shape, jnp.float32),
        )
        grads, relation_grads = bucket_pass(
            empty,
            table,
            relations,
            edge_pair,
            negative_pair,
            count_pair,
            source_shift,
            target_shift,
            block,
            first,
            last,
        )
        returned = swapped(grads[rows:], DOM, bit)
        relation_total = total_of(relation_grads, (("dom_0", "dom_1"), ("dom_2", "dom_3")))
        entities, entity_state = adagrad(entities, entity_state, grads[:rows] + returned)
        relations, relation_state = adagrad(relations, relation_state, relation_total)
    return (entities, entity_state, relations, relation_state)


def solution(mesh):
    finer = Mesh(mesh.devices.reshape(8, 4, 4, 2), ("dom_0", "dom_1", "dom_2", "dom_3"))
    return jax.shard_map(
        body,
        mesh=finer,
        in_specs=(
            P(DOM, None),
            P(DOM),
            P(),
            P(),
            P(None, None, DOM),
            P(None, DOM, None),
            P(None, DOM),
        ),
        out_specs=(P(DOM, None), P(DOM), P(), P()),
        check_vma=False,
    )
```

profile of v0, /device:TPU:1, one launch (start us, length us, event | category | flops | bytes accessed | tf_op | source)
XLA Modules:
  0.0 654.6 jit_solution(750336269881493213)
XLA Ops:
  0.7 7.8 %collective-permute-start = (f32[1024,200]{0,1:T(8,128)}, f32[1024,200]{0,1:T(8,128)}, u32[]{:S(2)}, u32[]{:S(2)}) collective-permute-start(f32[1024,200]{0,1:T(8,128)} %param.15), channel_id=1, source_target_pairs={{0,128},{128,0},{1,129},{129,1},{2,130},{130,2},{3,131},{131,3},{4... | collective-permute-start | bytes 2457608 | tf_op jit(solution)/shard_map/ppermute | solution.py:21
  15.8 13.8 %collective-permute-done = f32[1024,200]{0,1:T(8,128)} collective-permute-done((f32[1024,200]{0,1:T(8,128)}, f32[1024,200]{0,1:T(8,128)}, u32[]{:S(2)}, u32[]{:S(2)}) %collective-permute-start) | collective-permute-done | bytes 819232 | tf_op jit(solution)/shard_map/ppermute | solution.py:21
  34.3 47.7 %while.32 = (s32[]{:T(128)}, f32[2048,200]{1,0:T(8,128)S(1)}, f32[1345,200]{1,0:T(8,128)}, s32[]{:T(128)}, s32[2]{0:T(128)S(1)}, /*index=5*/s32[2,3,512]{2,1,0:T...) while((s32[]{:T(128)}, f32[2048,200]{1,0:T(8,128)S(1)}, ...), condition=%wide.region_6.7_spmd.clone, body=%wide.region_0.6_spmd.sunk.clone.sunk | while | flops 922910976 | bytes 24684976 | solution.py:165
  35.2 3.0 gather_fusion
  52.7 5.2 gather_fusion.1
  67.8 6.8 %scatter_fusion.2 = f32[2048,200]{1,0:T(8,128)S(1)} fusion(f32[2048,200]{1,0:T(8,128)S(1)} %scatter_fusion.1, s32[1000]{0:T(1024)S(1)} %bitcast.105, f32[1000,200]{1,0:T(8,128)S(1)} %fusion.65), kind=kCustom, calls=%fused_computation.10.clone.1 | custom fusion | flops 200000 | bytes 2404000 | tf_op jit(solution)/shard_map/while/body/scatter-add | solution.py:122
  77.9 4.0 scatter_fusion.3
  82.0 3.6 reshape.328
  87.9 3.1 reshape_reshape.12
  93.5 114.1 %all-to-all-start = ((f32[8,32,1051]{2,1,0:T(8,128)}), f32[8,32,1051]{2,1,0:T(8,128)}, u32[]{:S(2)}, u32[]{:S(2)}) async-start(f32[8,32,1051]{2,1,0:T(8,128)} %copy.129), calls=%async_computation | async-start | bytes 2359296 | tf_op jit(solution)/shard_map/all_to_all | solution.py:56
  211.5 12.5 %all-to-all-done = f32[8,32,1051]{2,1,0:T(8,128)} async-done(((f32[8,32,1051]{2,1,0:T(8,128)}), f32[8,32,1051]{2,1,0:T(8,128)}, u32[]{:S(2)}, u32[]{:S(2)}) %all-to-all-start) | async-done | bytes 1076256 | tf_op jit(solution)/shard_map/all_to_all | solution.py:56
  226.2 55.7 %all-to-all-start.1 = ((f32[32,1,1051]{2,1,0:T(1,128)}), f32[32,1,1051]{2,1,0:T(1,128)S(1)}, u32[]{:S(2)}, u32[]{:S(2)}) async-start(f32[32,1,1051]{2,1,0:T(1,128)} %all_to_all.33), calls=%async_computation.1 | async-start | bytes 294912 | tf_op jit(solution)/shard_map/all_to_all | solution.py:64
  283.3 21.5 %all-to-all-done.1 = f32[32,1,1051]{2,1,0:T(1,128)S(1)} async-done(((f32[32,1,1051]{2,1,0:T(1,128)}), f32[32,1,1051]{2,1,0:T(1,128)S(1)}, u32[]{:S(2)}, u32[]{:S(2)}) %all-to-all-start.1) | async-done | bytes 134560 | tf_op jit(solution)/shard_map/all_to_all | solution.py:64
  305.6 8.3 %all-to-all-start.2 = ((f32[32,1,1051]{2,1,0:T(1,128)}), f32[32,1,1051]{2,1,0:T(1,128)S(1)}, u32[]{:S(2)}, u32[]{:S(2)}) async-start(f32[32,1,1051]{2,1,0:T(1,128)} %broadcast_in_dim.23), calls=%async_computation.2 | async-start | bytes 294912 | tf_op jit(solution)/shard_map/all_to_all | solution.py:31
  317.7 5.7 all-to-all-done.2
  324.5 7.1 %all-to-all-start.3 = ((f32[8,32,1051]{2,1,0:T(8,128)}), f32[8,32,1051]{2,1,0:T(8,128)}, u32[]{:S(2)}, u32[]{:S(2)}) async-start(f32[8,32,1051]{2,1,0:T(8,128)} %broadcast_in_dim.25), calls=%async_computation.3 | async-start | bytes 2359296 | tf_op jit(solution)/shard_map/all_to_all | solution.py:31
  338.1 10.0 %all-to-all-done.3 = f32[8,32,1051]{2,1,0:T(8,128)} async-done(((f32[8,32,1051]{2,1,0:T(8,128)}), f32[8,32,1051]{2,1,0:T(8,128)}, u32[]{:S(2)}, u32[]{:S(2)}) %all-to-all-start.3) | async-done | bytes 1076256 | tf_op jit(solution)/shard_map/all_to_all | solution.py:31
  354.1 3.1 mul.337
  357.2 3.2 mul.335
  365.2 186.6 %while.33 = (s32[]{:T(128)}, f32[2048,200]{1,0:T(8,128)S(1)}, f32[1345,200]{1,0:T(8,128)}, s32[]{:T(128)}, s32[2]{0:T(128)}, /*index=5*/s32[2,3,512]{2,1,0:T(4,1...) while((s32[]{:T(128)}, f32[2048,200]{1,0:T(8,128)S(1)}, ...), condition=%wide.region_17.18_spmd.clone, body=%wide.region_11.17_spmd.sunk.clone.sunk | while | flops 922910976 | bytes 20380956 | solution.py:165
  367.5 3.0 gather_fusion.4
  382.8 5.2 gather_fusion.5
  397.9 6.8 %scatter_fusion.6 = f32[2048,200]{1,0:T(8,128)S(1)} fusion(f32[2048,200]{1,0:T(8,128)S(1)} %scatter_fusion.5, s32[1000]{0:T(1024)S(1)} %bitcast.107, f32[1000,200]{1,0:T(8,128)S(1)} %fusion.74), kind=kCustom, calls=%fused_computation.14.clone.1 | custom fusion | flops 200000 | bytes 2404000 | tf_op jit(solution)/shard_map/while/body/scatter-add | solution.py:122
  407.9 4.0 scatter_fusion.7
  414.1 3.0 gather_fusion.4
  429.3 5.2 gather_fusion.5
  444.4 6.8 %scatter_fusion.6 = f32[2048,200]{1,0:T(8,128)S(1)} fusion(f32[2048,200]{1,0:T(8,128)S(1)} %scatter_fusion.5, s32[1000]{0:T(1024)S(1)} %bitcast.107, f32[1000,200]{1,0:T(8,128)S(1)} %fusion.74), kind=kCustom, calls=%fused_computation.14.clone.1 | custom fusion | flops 200000 | bytes 2404000 | tf_op jit(solution)/shard_map/while/body/scatter-add | solution.py:122
  454.5 4.0 scatter_fusion.7
  460.6 3.0 gather_fusion.4
  475.9 5.2 gather_fusion.5
  491.0 6.8 %scatter_fusion.6 = f32[2048,200]{1,0:T(8,128)S(1)} fusion(f32[2048,200]{1,0:T(8,128)S(1)} %scatter_fusion.5, s32[1000]{0:T(1024)S(1)} %bitcast.107, f32[1000,200]{1,0:T(8,128)S(1)} %fusion.74), kind=kCustom, calls=%fused_computation.14.clone.1 | custom fusion | flops 200000 | bytes 2404000 | tf_op jit(solution)/shard_map/while/body/scatter-add | solution.py:122
  501.0 4.0 scatter_fusion.7
  507.1 3.0 gather_fusion.4
  522.4 5.2 gather_fusion.5
  537.5 6.8 %scatter_fusion.6 = f32[2048,200]{1,0:T(8,128)S(1)} fusion(f32[2048,200]{1,0:T(8,128)S(1)} %scatter_fusion.5, s32[1000]{0:T(1024)S(1)} %bitcast.107, f32[1000,200]{1,0:T(8,128)S(1)} %fusion.74), kind=kCustom, calls=%fused_computation.14.clone.1 | custom fusion | flops 200000 | bytes 2404000 | tf_op jit(solution)/shard_map/while/body/scatter-add | solution.py:122
  547.6 4.0 scatter_fusion.7
  551.7 3.6 reshape.329
  557.6 3.1 reshape_reshape.14
  563.3 4.2 all-to-all-start.4
  571.3 10.6 %all-to-all-done.4 = f32[8,32,1051]{2,1,0:T(8,128)} async-done(((f32[8,32,1051]{2,1,0:T(8,128)}), f32[8,32,1051]{2,1,0:T(8,128)}, u32[]{:S(2)}, u32[]{:S(2)}) %all-to-all-start.4) | async-done | bytes 1076256 | tf_op jit(solution)/shard_map/all_to_all | solution.py:56
  583.4 14.5 %all_to_all.51 = f32[32,1,1051]{2,1,0:T(1,128)S(1)} all-to-all(f32[32,1,1051]{2,1,0:T(1,128)S(1)} %all_to_all.38), channel_id=1, replica_groups=mesh['dom_0'=8,'dom_1'=4,'dom_2'=4,'dom_3'=2] {'dom_0','dom_1'}, dimensions={0} | all-to-all | bytes 269056 | tf_op jit(solution)/shard_map/all_to_all | solution.py:64
  598.0 12.9 %all_to_all.50 = f32[32,1,1051]{2,1,0:T(1,128)S(1)} all-to-all(f32[32,1,1051]{2,1,0:T(1,128)S(1)} %broadcast_in_dim.26), channel_id=1, replica_groups=mesh['dom_0'=8,'dom_1'=4,'dom_2'=4,'dom_3'=2] {'dom_0','dom_1'}, dimensions={0} | all-to-all | bytes 269056 | tf_op jit(solution)/shard_map/all_to_all | solution.py:31
  612.1 7.7 %all-to-all-start.7 = ((f32[8,32,1051]{2,1,0:T(8,128)}), f32[8,32,1051]{2,1,0:T(8,128)}, u32[]{:S(2)}, u32[]{:S(2)}) async-start(f32[8,32,1051]{2,1,0:T(8,128)} %broadcast_in_dim.28), calls=%async_computation.7 | async-start | bytes 2359296 | tf_op jit(solution)/shard_map/all_to_all | solution.py:31
  624.2 12.1 %all-to-all-done.7 = f32[8,32,1051]{2,1,0:T(8,128)} async-done(((f32[8,32,1051]{2,1,0:T(8,128)}), f32[8,32,1051]{2,1,0:T(8,128)}, u32[]{:S(2)}, u32[]{:S(2)}) %all-to-all-start.7) | async-done | bytes 1076256 | tf_op jit(solution)/shard_map/all_to_all | solution.py:31
  639.9 2.7 slice_multiply_fusion
  642.7 3.2 mul.343
  646.8 3.2 mul.341
  651.4 2.8 copy.137
  (321 shorter events, 199.6 us)
Async XLA Ops:
  0.6 11.5 %copy-start.25 = (s32[2,3,512]{2,0,1:T(2,128)S(1)}, s32[2,3,512]{2,0,1:T(2,128)}, u32[]{:S(2)}) copy-start(s32[2,3,512]{2,0,1:T(2,128)} %param.19) | copy-start | bytes 36868
  0.6 14.0 %copy-start.21 = (s32[2,4,1000]{2,1,0:T(4,128)S(1)}, s32[2,4,1000]{2,1,0:T(4,128)}, u32[]{:S(2)}) copy-start(s32[2,4,1000]{2,1,0:T(4,128)} %param.20) | copy-start | bytes 96004
  0.7 29.0 %collective-permute-start = (f32[1024,200]{0,1:T(8,128)}, f32[1024,200]{0,1:T(8,128)}, u32[]{:S(2)}, u32[]{:S(2)}) collective-permute-start(f32[1024,200]{0,1:T(8,128)} %param.15), channel_id=1, source_target_pairs={{0,128},{128,0},{1,129},{129,1},{2,130},{130,2},{3,131},{131,3},{4... | collective-permute-start | bytes 2457608 | tf_op jit(solution)/shard_map/ppermute | solution.py:21
  34.3 9.5 %copy-start.2 = (f32[1345,200]{1,0:T(8,128)}, f32[1345,200]{1,0:T(8,128)S(1)}, u32[]{:S(2)}) copy-start(f32[1345,200]{1,0:T(8,128)S(1)} %get-tuple-element.864) | copy-start | bytes 3228004 | tf_op jit(solution)/shard_map/while
  45.4 5.2 copy-start.27
  47.3 10.6 %copy-start.8 = (f32[128,100]{0,1:T(8,128)}, f32[128,100]{0,1:T(8,128)S(1)}, u32[]{:S(2)}) copy-start(f32[128,100]{0,1:T(8,128)S(1)} %copy.176) | copy-start | bytes 153604 | tf_op jit(solution)/shard_map/while
  58.9 1.8 copy-start
  58.9 1.8 copy-start.6
  58.9 1.8 copy-start.9
  67.8 6.9 %copy-start.14 = (f32[128,100]{0,1:T(8,128)S(1)}, f32[128,100]{0,1:T(8,128)}, u32[]{:S(2)}) copy-start(f32[128,100]{0,1:T(8,128)} %get-tuple-element.794) | copy-start | bytes 153604 | tf_op jit(solution)/shard_map/while
  74.6 7.2 %copy-start.3 = (f32[1345,200]{1,0:T(8,128)S(1)}, f32[1345,200]{1,0:T(8,128)}, u32[]{:S(2)}) copy-start(f32[1345,200]{1,0:T(8,128)} %copy-done.2) | copy-start | bytes 3228004 | tf_op jit(solution)/shard_map/while
  93.5 130.6 %all-to-all-start = ((f32[8,32,1051]{2,1,0:T(8,128)}), f32[8,32,1051]{2,1,0:T(8,128)}, u32[]{:S(2)}, u32[]{:S(2)}) async-start(f32[8,32,1051]{2,1,0:T(8,128)} %copy.129), calls=%async_computation | async-start | bytes 2359296 | tf_op jit(solution)/shard_map/all_to_all | solution.py:56
  209.3 72.7 %copy-start.13 = (f32[2048,200]{0,1:T(8,128)S(1)}, f32[2048,200]{0,1:T(8,128)}, u32[]{:S(2)}) copy-start(f32[2048,200]{0,1:T(8,128)} %copy.126) | copy-start | bytes 4915204
  211.5 70.4 %collective-permute-start.1 = (f32[1024,200]{0,1:T(8,128)}, f32[1024,200]{0,1:T(8,128)}, u32[]{:S(2)}, u32[]{:S(2)}) collective-permute-start(f32[1024,200]{0,1:T(8,128)} %slice.265), channel_id=1, source_target_pairs={{0,128},{128,0},{1,129},{129,1},{2,130},{130,2},{3,131},{131,3},{4... | collective-permute-start | bytes 2457608 | tf_op jit(solution)/shard_map/ppermute | solution.py:21
  225.4 57.8 %copy-start.23 = (f32[1024]{0:T(1024)S(1)}, f32[1024]{0:T(1024)}, u32[]{:S(2)}) copy-start(f32[1024]{0:T(1024)} %param.16) | copy-start | bytes 12292
  226.2 78.5 %all-to-all-start.1 = ((f32[32,1,1051]{2,1,0:T(1,128)}), f32[32,1,1051]{2,1,0:T(1,128)S(1)}, u32[]{:S(2)}, u32[]{:S(2)}) async-start(f32[32,1,1051]{2,1,0:T(1,128)} %all_to_all.33), calls=%async_computation.1 | async-start | bytes 294912 | tf_op jit(solution)/shard_map/all_to_all | solution.py:64
  305.6 17.8 %all-to-all-start.2 = ((f32[32,1,1051]{2,1,0:T(1,128)}), f32[32,1,1051]{2,1,0:T(1,128)S(1)}, u32[]{:S(2)}, u32[]{:S(2)}) async-start(f32[32,1,1051]{2,1,0:T(1,128)} %broadcast_in_dim.23), calls=%async_computation.2 | async-start | bytes 294912 | tf_op jit(solution)/shard_map/all_to_all | solution.py:31
  316.3 18.4 %collective-permute-start.2 = (f32[1024,200]{0,1:T(8,128)}, f32[1024,200]{0,1:T(8,128)}, u32[]{:S(2)}, u32[]{:S(2)}) collective-permute-start(f32[1024,200]{0,1:T(8,128)} %divide_subtract_fusion.3), channel_id=1, source_target_pairs={{0,1},{1,0},{2,3},{3,2},{4,5},{5,4},{6,7},{7,6},{8,9},{9,8},{10,11... | collective-permute-start | bytes 2457608 | tf_op jit(solution)/shard_map/ppermute | solution.py:21
  324.5 7.8 %copy-start.22 = (s32[1,3,512]{2,0,1:T(1,128)S(1)}, s32[1,3,512]{2,0,1:T(1,128)}, u32[]{:S(2)}) copy-start(s32[1,3,512]{2,0,1:T(1,128)} %get-tuple-element.628) | copy-start | bytes 18436
  324.5 9.7 %copy-start.18 = (s32[1,4,1000]{2,1,0:T(4,128)S(1)}, s32[1,4,1000]{2,1,0:T(4,128)}, u32[]{:S(2)}) copy-start(s32[1,4,1000]{2,1,0:T(4,128)} %get-tuple-element.626) | copy-start | bytes 48004
  324.5 23.6 %all-to-all-start.3 = ((f32[8,32,1051]{2,1,0:T(8,128)}), f32[8,32,1051]{2,1,0:T(8,128)}, u32[]{:S(2)}, u32[]{:S(2)}) async-start(f32[8,32,1051]{2,1,0:T(8,128)} %broadcast_in_dim.25), calls=%async_computation.3 | async-start | bytes 2359296 | tf_op jit(solution)/shard_map/all_to_all | solution.py:31
  357.2 4.9 copy-start.19
  376.1 4.6 copy-start.26
  377.4 10.6 %copy-start.10 = (f32[128,100]{0,1:T(8,128)}, f32[128,100]{0,1:T(8,128)S(1)}, u32[]{:S(2)}) copy-start(f32[128,100]{0,1:T(8,128)S(1)} %copy.184) | copy-start | bytes 153604 | tf_op jit(solution)/shard_map/while
  389.0 1.8 copy-start.1
  397.9 6.9 %copy-start.15 = (f32[128,100]{0,1:T(8,128)S(1)}, f32[128,100]{0,1:T(8,128)}, u32[]{:S(2)}) copy-start(f32[128,100]{0,1:T(8,128)} %get-tuple-element.819) | copy-start | bytes 153604 | tf_op jit(solution)/shard_map/while
  404.7 7.2 %copy-start.5 = (f32[1345,200]{1,0:T(8,128)S(1)}, f32[1345,200]{1,0:T(8,128)}, u32[]{:S(2)}) copy-start(f32[1345,200]{1,0:T(8,128)} %get-tuple-element.947) | copy-start | bytes 3228004 | tf_op jit(solution)/shard_map/while
  422.7 4.6 copy-start.26
  423.9 10.6 %copy-start.10 = (f32[128,100]{0,1:T(8,128)}, f32[128,100]{0,1:T(8,128)S(1)}, u32[]{:S(2)}) copy-start(f32[128,100]{0,1:T(8,128)S(1)} %copy.184) | copy-start | bytes 153604 | tf_op jit(solution)/shard_map/while
  435.5 1.8 copy-start.1
  444.4 6.9 %copy-start.15 = (f32[128,100]{0,1:T(8,128)S(1)}, f32[128,100]{0,1:T(8,128)}, u32[]{:S(2)}) copy-start(f32[128,100]{0,1:T(8,128)} %get-tuple-element.819) | copy-start | bytes 153604 | tf_op jit(solution)/shard_map/while
  451.2 7.2 %copy-start.5 = (f32[1345,200]{1,0:T(8,128)S(1)}, f32[1345,200]{1,0:T(8,128)}, u32[]{:S(2)}) copy-start(f32[1345,200]{1,0:T(8,128)} %get-tuple-element.947) | copy-start | bytes 3228004 | tf_op jit(solution)/shard_map/while
  469.2 4.6 copy-start.26
  470.5 10.6 %copy-start.10 = (f32[128,100]{0,1:T(8,128)}, f32[128,100]{0,1:T(8,128)S(1)}, u32[]{:S(2)}) copy-start(f32[128,100]{0,1:T(8,128)S(1)} %copy.184) | copy-start | bytes 153604 | tf_op jit(solution)/shard_map/while
  482.0 1.8 copy-start.1
  490.9 6.9 %copy-start.15 = (f32[128,100]{0,1:T(8,128)S(1)}, f32[128,100]{0,1:T(8,128)}, u32[]{:S(2)}) copy-start(f32[128,100]{0,1:T(8,128)} %get-tuple-element.819) | copy-start | bytes 153604 | tf_op jit(solution)/shard_map/while
  497.8 7.2 %copy-start.5 = (f32[1345,200]{1,0:T(8,128)S(1)}, f32[1345,200]{1,0:T(8,128)}, u32[]{:S(2)}) copy-start(f32[1345,200]{1,0:T(8,128)} %get-tuple-element.947) | copy-start | bytes 3228004 | tf_op jit(solution)/shard_map/while
  515.7 4.6 copy-start.26
  517.0 10.6 %copy-start.10 = (f32[128,100]{0,1:T(8,128)}, f32[128,100]{0,1:T(8,128)S(1)}, u32[]{:S(2)}) copy-start(f32[128,100]{0,1:T(8,128)S(1)} %copy.184) | copy-start | bytes 153604 | tf_op jit(solution)/shard_map/while
  528.6 1.8 copy-start.1
  537.5 6.9 %copy-start.15 = (f32[128,100]{0,1:T(8,128)S(1)}, f32[128,100]{0,1:T(8,128)}, u32[]{:S(2)}) copy-start(f32[128,100]{0,1:T(8,128)} %get-tuple-element.819) | copy-start | bytes 153604 | tf_op jit(solution)/shard_map/while
  544.3 7.2 %copy-start.5 = (f32[1345,200]{1,0:T(8,128)S(1)}, f32[1345,200]{1,0:T(8,128)}, u32[]{:S(2)}) copy-start(f32[1345,200]{1,0:T(8,128)} %get-tuple-element.947) | copy-start | bytes 3228004 | tf_op jit(solution)/shard_map/while
  563.3 18.6 %all-to-all-start.4 = ((f32[8,32,1051]{2,1,0:T(8,128)}), f32[8,32,1051]{2,1,0:T(8,128)}, u32[]{:S(2)}, u32[]{:S(2)}) async-start(f32[8,32,1051]{2,1,0:T(8,128)} %copy.135), calls=%async_computation.4 | async-start | bytes 2359296 | tf_op jit(solution)/shard_map/all_to_all | solution.py:56
  571.3 48.5 %collective-permute-start.3 = (f32[1024,200]{0,1:T(8,128)}, f32[1024,200]{0,1:T(8,128)}, u32[]{:S(2)}, u32[]{:S(2)}) collective-permute-start(f32[1024,200]{0,1:T(8,128)} %slice.268), channel_id=1, source_target_pairs={{0,1},{1,0},{2,3},{3,2},{4,5},{5,4},{6,7},{7,6},{8,9},{9,8},{10,11... | collective-permute-start | bytes 2457608 | tf_op jit(solution)/shard_map/ppermute | solution.py:21
  612.1 7.8 %copy-start.12 = (f32[2048,200]{0,1:T(8,128)S(1)}, f32[2048,200]{0,1:T(8,128)}, u32[]{:S(2)}) copy-start(f32[2048,200]{0,1:T(8,128)} %copy.133) | copy-start | bytes 4915204
  612.1 24.3 %all-to-all-start.7 = ((f32[8,32,1051]{2,1,0:T(8,128)}), f32[8,32,1051]{2,1,0:T(8,128)}, u32[]{:S(2)}, u32[]{:S(2)}) async-start(f32[8,32,1051]{2,1,0:T(8,128)} %broadcast_in_dim.28), calls=%async_computation.7 | async-start | bytes 2359296 | tf_op jit(solution)/shard_map/all_to_all | solution.py:31
  642.7 3.5 copy-start.17
  642.7 3.5 copy-start.20
  (11 other events, 19.0 us)
where the time goes:
time: 668 us; the launch traced here: 655 us
  starting transfers between devices  206 us (31%)
  local copies, waits for them, and re-layouts  174 us (26%)
  other arithmetic  127 us (19%)
  waiting for transfers between devices  86.1 us (13%)
  blocking collectives  27.4 us (4%)
  matrix products  23.9 us (4%)
  loops' own time  7.36 us (1%)
    all_to_all x2, starting transfers between devices, summed_on_arrival(): pieces = lax.all_to_all(split_up(value, dim, count), axis, 0, 0, tiled=True)  118 us
    all_to_all x1, starting transfers between devices, sum_in_two_steps(): lax.all_to_all(nearer, far, split_axis=0, concat_axis=0, tiled=True)  55.7 us
    scatter-add x15, other arithmetic, block_terms(): grad_table = grad_table.at[source].add(source_grad).at[target].add(target...  54.6 us
    all_to_all x3, waiting for transfers between devices, from_everyone(): lax.all_to_all(jnp.broadcast_to(value[None], (count, *value.shape)), axis...  27.7 us
    gather x5, local copies, waits for them, and re-layouts, block_terms(): neg_rows = table[negative_ids]  25.9 us
    all_to_all x3, starting transfers between devices, from_everyone(): lax.all_to_all(jnp.broadcast_to(value[None], (count, *value.shape)), axis...  23.2 us
    all_to_all x2, waiting for transfers between devices, summed_on_arrival(): pieces = lax.all_to_all(split_up(value, dim, count), axis, 0, 0, tiled=True)  23.1 us
    all_to_all x1, waiting for transfers between devices, sum_in_two_steps(): lax.all_to_all(nearer, far, split_axis=0, concat_axis=0, tiled=True)  21.5 us
  transfers between devices with their start and end apart: 10, of which 7 were waited for; matrix products, arithmetic and copies ran while one was open for 5% of the time, Pallas kernels for 0%

commit v1 on v0

v1 whole, which is shorter than its diff:
```python
import jax
import jax.numpy as jnp
from jax import lax
from jax.experimental import pallas as pl
from jax.experimental.pallas import tpu as pltpu
from jax.sharding import PartitionSpec as P

RATE = 0.2
F32 = jnp.float32
BF16 = jnp.bfloat16
VMEM = pl.BlockSpec(memory_space=pltpu.VMEM)
SMEM = pl.BlockSpec(memory_space=pltpu.SMEM)
NN = (((1,), (0,)), ((), ()))
NT = (((1,), (1,)), ((), ()))
LANES = 128


def split(value):
    high = value.astype(BF16)
    return high, (value - high.astype(F32)).astype(BF16)


def dot(left, right, dims=NN):
    return lax.dot_general(left, right, dims, preferred_element_type=F32)


def dot3(left, right, dims=NN):
    return (
        dot(left[0], right[0], dims) + dot(left[0], right[1], dims) + dot(left[1], right[0], dims)
    )


def dot_exact(left, right, dims=NN):
    return dot(left[0], right, dims) + dot(left[1], right, dims)


def spots(ids, count):
    rows = lax.broadcasted_iota(jnp.int32, (count, ids.shape[1]), 0)
    return jnp.where(rows == ids, 1.0, 0.0).astype(BF16)


def call(kernel, outs, args, scratch=(), name=None):
    specs = [SMEM if kind == "smem" else VMEM for kind, _ in args]
    return pl.pallas_call(
        kernel,
        out_shape=[jax.ShapeDtypeStruct(*out) for out in outs],
        in_specs=specs,
        out_specs=[VMEM] * len(outs),
        scratch_shapes=list(scratch),
        name=name,
    )(*[value for _, value in args])


def prep_kernel(e_ref, edges_ref, et_ref, st_ref, wide):
    rows, dim = e_ref.shape
    wide[...] = jnp.zeros_like(wide)
    wide[:, :dim] = e_ref[...]
    et_ref[...] = wide[...].T[:dim]
    source = edges_ref[0, 0:1, :]
    st_ref[...] = dot_exact(split(et_ref[...]), spots(source, rows))


def rel_prep_kernel(r_ref, rt_ref, wide):
    rows, dim = r_ref.shape
    wide[...] = jnp.zeros_like(wide)
    wide[:rows, :dim] = r_ref[...]
    rt_ref[...] = wide[...].T[:dim]


def hist_kernel(neg_ref, c_ref):
    blocks, draws = neg_ref.shape
    rows = c_ref.shape[0]
    ones = jnp.ones((draws, LANES), BF16)
    for b in range(blocks):
        hits = spots(neg_ref[b : b + 1, :], rows)
        c_ref[:, b * LANES : (b + 1) * LANES] = dot(hits, ones) * (1.0 / draws)


def main_kernel(
    e_ref, et_ref, rt_ref, st_ref, edges_ref, c_ref, count_ref, gt_ref, gs_ref, h_ref, q, tmp
):
    rows, dim = e_ref.shape
    half = dim // 2
    wide = edges_ref.shape[1]
    rels = rt_ref.shape[1]
    relation = edges_ref[1:2, :]
    live = lax.broadcasted_iota(jnp.int32, (1, wide), 1) < count_ref[0]
    target = jnp.where(live, edges_ref[2:3, :], -1)
    alive = live.astype(F32)
    rel_spots = spots(relation, rels)
    tmp[...] = dot_exact(split(rt_ref[...]), rel_spots)
    s_re, s_im = st_ref[0:half, :], st_ref[half:dim, :]
    w_re, w_im = tmp[0:half, :], tmp[half:dim, :]
    q[0:half, :] = s_re * w_re - s_im * w_im
    q[half:dim, :] = s_re * w_im + s_im * w_re
    q_parts = split(q[...])
    up = jnp.zeros((dim, wide), F32)
    step = 256
    for j in range(0, rows, step):
        scores = dot3(split(e_ref[j : j + step, :]), q_parts)
        sig = 0.5 * jnp.tanh(0.5 * scores) + 0.5
        number = lax.broadcasted_iota(jnp.int32, (step, wide), 0) + j
        mark = jnp.where(number == target, 1.0, 0.0)
        weight = split(sig * (c_ref[j : j + step, :] * alive + mark) - mark)
        up = up + dot3(split(et_ref[:, j : j + step]), weight)
        gt_ref[:, j : j + step] = dot3(q_parts, weight, NT)
    q[...] = up
    u_re, u_im = q[0:half, :], q[half:dim, :]
    gs_ref[0:half, :] = u_re * w_re + u_im * w_im
    gs_ref[half:dim, :] = u_im * w_re - u_re * w_im
    tmp[0:half, :] = u_re * s_re + u_im * s_im
    tmp[half:dim, :] = u_im * s_re - u_re * s_im
    h_ref[...] = dot_exact(split(tmp[...]), rel_spots, NT)


def stepped(param, state, grad):
    new_state = state + jnp.sum(grad * grad, axis=0, keepdims=True) * (1.0 / grad.shape[0])
    return param - RATE * grad / jnp.sqrt(new_state), new_state


def update_kernel(number, et_ref, state_ref, gt_ref, gs_ref, edges_ref, e_out, state_out, et_out, *more):
    dim, rows = et_ref.shape
    source = spots(edges_ref[number, 0:1, :], rows)
    grad = gt_ref[...] + dot_exact(split(gs_ref[...]), source, NT)
    after, state = stepped(et_ref[...], state_ref[...], grad)
    state_out[...] = state
    wide = more[-1]
    wide[0:dim, :] = after
    wide[dim:, :] = jnp.zeros((wide.shape[0] - dim, rows), F32)
    e_out[...] = wide[...].T[:, :dim]
    et_out[...] = after
    if len(more) > 1:
        more[0][...] = dot_exact(split(after), spots(edges_ref[number + 1, 0:1, :], rows))


def rel_update_kernel(rt_ref, state_ref, h_ref, rt_out, state_out):
    rt_out[...], state_out[...] = stepped(rt_ref[...], state_ref[...], h_ref[...])


def rel_final_kernel(rt_ref, state_ref, h_ref, r_out, state_out, wide):
    dim = rt_ref.shape[0]
    after, state_out[...] = stepped(rt_ref[...], state_ref[...], h_ref[...])
    wide[0:dim, :] = after
    wide[dim:, :] = jnp.zeros((wide.shape[0] - dim, wide.shape[1]), F32)
    r_out[...] = wide[...].T[: r_out.shape[0], :dim]


def swapped(value, apart):
    count = lax.axis_size("dom")
    return lax.ppermute(value, "dom", [(low, low ^ (1 << apart)) for low in range(count)])


def body(entities, entity_state, relations, relation_state, edges, negatives, counts):
    rows, dim = entities.shape
    rels = relations.shape[0]
    rels_pad = -(-rels // LANES) * LANES
    rounds, _, slots = edges.shape
    levels = lax.axis_size("dom").bit_length() - 1
    dim_pad = -(-dim // LANES) * LANES
    et, st = call(
        prep_kernel,
        [((dim, rows), F32), ((dim, slots), F32)],
        [("v", entities), ("v", edges)],
        [pltpu.VMEM((rows, dim_pad), F32)],
        name="prep",
    )
    (rt,) = call(
        rel_prep_kernel,
        [((dim, rels_pad), F32)],
        [("v", relations)],
        [pltpu.VMEM((rels_pad, dim_pad), F32)],
        name="rel_prep",
    )
    state = entity_state.reshape(1, rows)
    rel_state = jnp.pad(relation_state.reshape(1, rels), ((0, 0), (0, rels_pad - rels)), constant_values=1.0)
    table = entities
    for number, bit in enumerate((levels - 1, 0)):
        their_edges = swapped(edges[number], bit)
        their_negatives = swapped(negatives[number], bit)
        their_count = swapped(counts[number], bit)
        their_rows = swapped(st, bit)
        (c,) = call(hist_kernel, [((rows, slots), F32)], [("v", their_negatives)], name=f"hist{number}")
        gt, gs, h = call(
            main_kernel,
            [((dim, rows), F32), ((dim, slots), F32), ((dim, rels_pad), F32)],
            [
                ("v", table),
                ("v", et),
                ("v", rt),
                ("v", their_rows),
                ("v", their_edges),
                ("v", c),
                ("smem", their_count),
            ],
            [pltpu.VMEM((dim, slots), F32), pltpu.VMEM((dim, slots), F32)],
            name=f"main{number}",
        )
        gs = swapped(gs, bit)
        h = lax.psum(h, "dom")
        last = number == rounds - 1
        outs = call(
            lambda *refs, number=number: update_kernel(number, *refs),
            [((rows, dim), F32), ((1, rows), F32), ((dim, rows), F32)]
            + ([] if last else [((dim, slots), F32)]),
            [("v", et), ("v", state), ("v", gt), ("v", gs), ("v", edges)],
            [pltpu.VMEM((dim_pad, rows), F32)],
            name=f"update{number}",
        )
        table, state, et = outs[:3]
        if last:
            relations, rel_state = call(
                rel_final_kernel,
                [((rels, dim), F32), ((1, rels_pad), F32)],
                [("v", rt), ("v", rel_state), ("v", h)],
                [pltpu.VMEM((dim_pad, rels_pad), F32)],
                name=f"rel_update{number}",
            )
        else:
            st = outs[3]
            rt, rel_state = call(
                rel_update_kernel,
                [((dim, rels_pad), F32), ((1, rels_pad), F32)],
                [("v", rt), ("v", rel_state), ("v", h)],
                name=f"rel_update{number}",
            )
    return table, state.reshape(rows), relations, rel_state[0, :rels]


def solution(mesh):
    return jax.shard_map(
        body,
        mesh=mesh,
        in_specs=(
            P("dom", None),
            P("dom"),
            P(),
            P(),
            P(None, None, "dom"),
            P(None, "dom", None),
            P(None, "dom"),
        ),
        out_specs=(P("dom", None), P("dom"), P(), P()),
        check_vma=False,
    )
```

time: 668 us -> 604 us (0.904); the launches traced: 655 us -> 603 us
  waiting for transfers between devices: 86.1 us -> 484 us
  starting transfers between devices: 206 us -> 38.7 us
  local copies, waits for them, and re-layouts: 174 us -> 17.7 us
  other arithmetic: 127 us -> 0 us
  Pallas kernels: 0 us -> 47.8 us
  blocking collectives: 27.4 us -> 0 us
  matrix products: 23.9 us -> 0 us
  between operations: 2.68 us -> 14.1 us
  loops' own time: 7.36 us -> 0 us
    psum x0 -> x2, waiting for transfers between devices: none -> 477 us  [body(): h = lax.psum(h, 'dom')]
    all_to_all x6 -> x0, starting transfers between devices: 197 us -> none  [the longest x2 118 us: summed_on_arrival(): pieces = lax.all_to_all(split_up(value, dim, count), axis, 0, 0, tiled=True)]
    scatter-add x20 -> x0, other arithmetic: 74.4 us -> none  [the longest x15 54.6 us: block_terms(): grad_table = grad_table.at[source].add(source_grad).at[target].add(target...]
    all_to_all x6 -> x0, waiting for transfers between devices: 72.3 us -> none  [the longest x3 27.7 us: from_everyone(): lax.all_to_all(jnp.broadcast_to(value[None], (count, *value.shape)), axis...]
    gather x25 -> x0, local copies, waits for them, and re-layouts: 60 us -> none  [the longest x5 25.9 us: block_terms(): neg_rows = table[negative_ids]]
    pallas_call x0 -> x10, Pallas kernels: none -> 47.8 us  [call(): pl.pallas_call(kernel, out_shape=[jax.ShapeDtypeStruct(*out) for out in o...]
    ppermute x4 -> x10, starting transfers between devices: 9.18 us -> 38.4 us  [swapped(): lax.ppermute(value, 'dom', [(low, low ^ 1 << apart) for low in range(coun...]
    all_to_all x2 -> x0, blocking collectives: 27.4 us -> none  [the longest x1 14.5 us: sum_in_two_steps(): lax.all_to_all(nearer, far, split_axis=0, concat_axis=0, tiled=True)]
  transfers between devices with their start and end apart: 10 -> 12, of which waited for: 7 -> 5; matrix products, arithmetic and copies ran while one was open for 5% -> 1% of each run, Pallas kernels for 0% -> 4%
where the time goes in v1:
time: 604 us; the launch traced here: 603 us
  waiting for transfers between devices  484 us (80%)
  Pallas kernels  47.8 us (8%)
  starting transfers between devices  38.7 us (6%)
  local copies, waits for them, and re-layouts  17.7 us (3%)
  between operations  14.1 us (2%)
    psum x2, waiting for transfers between devices, body(): h = lax.psum(h, 'dom')  477 us
    pallas_call x10, Pallas kernels, call(): pl.pallas_call(kernel, out_shape=[jax.ShapeDtypeStruct(*out) for out in o...  47.8 us
    ppermute x10, starting transfers between devices, swapped(): lax.ppermute(value, 'dom', [(low, low ^ 1 << apart) for low in range(coun...  38.4 us
    unnamed x35, local copies, waits for them, and re-layouts  15.9 us
  transfers between devices with their start and end apart: 12, of which 5 were waited for; matrix products, arithmetic and copies ran while one was open for 1% of the time, Pallas kernels for 4%

profile of v1, /device:TPU:1, one launch (start us, length us, event | category | flops | bytes accessed | tf_op | source)
XLA Modules:
  0.0 602.8 jit_solution(18074026592841037235)
XLA Ops:
  7.2 0.0 all-reduce.4.cloned.1.call-start
  7.2 1.3 copy.12.edges_ref.refs_4_
  8.5 2.6 copy.11.e_ref
  11.1 2.8 prep.1
  13.9 7.7 %collective-permute-start = (f32[200,512]{1,0:T(8,128)}, f32[200,512]{1,0:T(8,128)S(1)}, u32[]{:S(2)}, u32[]{:S(2)}) collective-permute-start(f32[200,512]{1,0:T(8,128)} %get-tuple-element.23), channel_id=1, source_target_pairs={{0,128},{1,129},{2,130},{3,131},{4,132},{5,133},{6,134},{7,135},{8... | collective-permute-start | bytes 1228808 | tf_op jit(solution)/shard_map/ppermute | solution.py:150
  21.7 0.1 collective-permute-start.1
  21.8 5.3 collective-permute-start.2
  27.0 0.6 fusion
  27.6 0.1 collective-permute-start.3
  27.8 1.5 copy.13.r_ref
  29.3 2.8 rel_prep.1.rt_ref
  32.1 0.0 collective-permute-done.2.neg_ref
  32.1 0.6 copy-done.8
  32.7 4.4 hist0.1.c_ref
  37.1 0.0 collective-permute-done.3.count_ref
  37.2 0.6 copy-done.10
  37.8 0.2 copy-done.3
  37.9 9.5 %main0.1 = (f32[200,1024]{1,0:T(8,128)}, f32[200,512]{1,0:T(8,128)}, f32[200,1408]{1,0:T(8,128)}) custom-call(f32[1024,200]{1,0:T(8,128)} %copy.11.e_ref, f32[200,1024]{1,0:T(8,128)} %get-tuple-element.22.et_ref.refs_0_, f32[200,1408]{1,0:T(8,128)} %rel_prep.1.rt_ref, f32[200,512]{1,0:T(8,128)} %copy-done.3, s32[3,512]{1,0:T(4,128)} %copy-done.10, ...), custom_call_target="tpu_custom_call" | custom-call | tf_op jit(solution)/shard_map/main0/pallas_call | solution.py:44
  47.5 5.6 collective-permute-start.4
  53.1 0.0 all-reduce.4.cloned.1.call-update
  53.1 0.0 copy-start.11
  53.1 0.2 all-reduce.6.cloned.1.call-start
  53.3 5.3 collective-permute-done.4.refs_3_
  58.6 0.8 copy-done.4
  59.4 4.3 update0.1
  63.7 17.3 %collective-permute-start.5 = (f32[200,512]{1,0:T(8,128)}, f32[200,512]{1,0:T(8,128)S(1)}, u32[]{:S(2)}, u32[]{:S(2)}) collective-permute-start(f32[200,512]{1,0:T(8,128)} %get-tuple-element.31), channel_id=1, source_target_pairs={{0,1},{1,0},{2,3},{3,2},{4,5},{5,4},{6,7},{7,6},{8,9},{9,8},{10,11... | collective-permute-start | bytes 1228808 | tf_op jit(solution)/shard_map/ppermute | solution.py:150
  81.0 0.5 collective-permute-start.6
  81.5 0.6 pad.4.state_ref
  82.1 0.5 collective-permute-done.7.neg_ref
  82.6 0.6 copy-done.7
  83.2 4.4 hist1.1.c_ref
  87.6 231.6 %all-reduce.4.cloned.1.call-done.h_ref = f32[200,1408]{1,0:T(8,128)} async-done(((f32[200,1408]{1,0:T(8,128)}), f32[200,1408]{1,0:T(8,128)}) %all-reduce.4.cloned.1.call-update) | async-done | bytes 1126416 | tf_op jit(solution)/shard_map/psum | solution.py:199
  319.3 2.9 rel_update0.1
  322.2 0.0 copy-start.9
  322.2 0.6 copy-done.9
  322.8 0.2 copy-done.2
  323.0 9.5 %main1.1 = (f32[200,1024]{1,0:T(8,128)}, f32[200,512]{1,0:T(8,128)}, f32[200,1408]{1,0:T(8,128)}) custom-call(f32[1024,200]{1,0:T(8,128)} %get-tuple-element.28.e_ref, f32[200,1024]{1,0:T(8,128)} %get-tuple-element.26.et_ref.refs_0_, f32[200,1408]{1,0:T(8,128)} %get-tuple-element.30.rt_ref, f32[200,512]{1,0:T(8,128)} %copy-done.2, s32[3,512]{1,0:T(4,128)} %copy-done.9, ...), custom_call_target="tpu_custom_call" | custom-call | tf_op jit(solution)/shard_map/main1/pallas_call | solution.py:44
  332.5 0.0 all-reduce.6.cloned.1.call-update
  332.5 1.0 copy-done.14
  333.5 1.8 collective-permute-start.9
  335.3 1.4 collective-permute-done.9.refs_3_
  336.7 0.8 copy-done.5
  337.5 3.8 update1.1
  341.3 2.5 copy.19
  343.8 245.5 %all-reduce.6.cloned.1.call-done.h_ref = f32[200,1408]{1,0:T(8,128)} async-done(((f32[200,1408]{1,0:T(8,128)}), f32[200,1408]{1,0:T(8,128)}) %all-reduce.6.cloned.1.call-update) | async-done | bytes 1126416 | tf_op jit(solution)/shard_map/psum | solution.py:199
  589.3 3.2 rel_update1.1
  592.5 2.8 copy.20
  595.3 0.6 slice_reduce_fusion
  (29 shorter events, 0.1 us)
Async XLA Ops:
  7.2 312.1 %all-reduce.4.cloned.1.call-start = ((), (), s32[]{:S(2)}) async-start(), calls=%async_computation | async-start | bytes 2252800 | tf_op jit(solution)/shard_map/psum | solution.py:199
  8.5 13.1 %copy-start.1 = (s32[2,3,512]{2,1,0:T(4,128)S(1)}, s32[2,3,512]{2,1,0:T(4,128)}, u32[]{:S(2)}) copy-start(s32[2,3,512]{2,1,0:T(4,128)} %copy.12.edges_ref.refs_4_) | copy-start | bytes 36868
  8.5 13.2 %copy-start.6 = (s32[2,4,1000]{2,1,0:T(4,128)S(1)}, s32[2,4,1000]{2,1,0:T(4,128)}, u32[]{:S(2)}) copy-start(s32[2,4,1000]{2,1,0:T(4,128)} %param.12) | copy-start | bytes 96004
  8.5 18.5 %copy-start.13 = (s32[2,1]{0,1:T(1,128)S(1)}, s32[2,1]{0,1:T(1,128)}, u32[]{:S(2)}) copy-start(s32[2,1]{0,1:T(1,128)} %param.13) | copy-start | bytes 28
  8.5 19.2 %copy-start = (f32[1345,200]{0,1:T(8,128)S(1)}, f32[1345,200]{0,1:T(8,128)}, u32[]{:S(2)}) copy-start(f32[1345,200]{0,1:T(8,128)} %param.9) | copy-start | bytes 3228004
  13.9 23.2 %collective-permute-start = (f32[200,512]{1,0:T(8,128)}, f32[200,512]{1,0:T(8,128)S(1)}, u32[]{:S(2)}, u32[]{:S(2)}) collective-permute-start(f32[200,512]{1,0:T(8,128)} %get-tuple-element.23), channel_id=1, source_target_pairs={{0,128},{1,129},{2,130},{3,131},{4,132},{5,133},{6,134},{7,135},{8... | collective-permute-start | bytes 1228808 | tf_op jit(solution)/shard_map/ppermute | solution.py:150
  21.7 15.5 %collective-permute-start.1 = (s32[3,512]{1,0:T(4,128)S(1)}, s32[3,512]{1,0:T(4,128)S(1)}, u32[]{:S(2)}, u32[]{:S(2)}) collective-permute-start(s32[3,512]{1,0:T(4,128)S(1)} %get-tuple-element.47), channel_id=1, source_target_pairs={{0,128},{1,129},{2,130},{3,131},{4,132},{5,133},{6,134},{7,135},{8... | collective-permute-start | bytes 18440 | tf_op jit(solution)/shard_map/ppermute | solution.py:150
  21.8 10.4 %collective-permute-start.2 = (s32[4,1000]{1,0:T(4,128)S(1)}, s32[4,1000]{1,0:T(4,128)S(1)}, u32[]{:S(2)}, u32[]{:S(2)}) collective-permute-start(s32[4,1000]{1,0:T(4,128)S(1)} %get-tuple-element.45), channel_id=1, source_target_pairs={{0,128},{1,129},{2,130},{3,131},{4,132},{5,133},{6,134},{7,135},{8... | collective-permute-start | bytes 48008 | tf_op jit(solution)/shard_map/ppermute | solution.py:150
  27.6 9.5 %collective-permute-start.3 = (s32[1]{0:T(128)}, s32[1]{0:T(128)}, u32[]{:S(2)}, u32[]{:S(2)}) collective-permute-start(s32[1]{0:T(128)} %bitcast.3), channel_id=1, source_target_pairs={{0,128},{1,129},{2,130},{3,131},{4,132},{5,133},{6,134},{7,135},{8... | collective-permute-start | bytes 20 | tf_op jit(solution)/shard_map/ppermute | solution.py:150
  32.1 0.6 copy-start.8
  37.1 0.6 copy-start.10
  37.2 0.8 copy-start.3
  47.5 11.1 %collective-permute-start.4 = (f32[200,512]{1,0:T(8,128)}, f32[200,512]{1,0:T(8,128)S(1)}, u32[]{:S(2)}, u32[]{:S(2)}) collective-permute-start(f32[200,512]{1,0:T(8,128)} %get-tuple-element.25), channel_id=1, source_target_pairs={{0,128},{1,129},{2,130},{3,131},{4,132},{5,133},{6,134},{7,135},{8... | collective-permute-start | bytes 1228808 | tf_op jit(solution)/shard_map/ppermute | solution.py:150
  53.1 28.4 %copy-start.11 = (f32[1345]{0:T(1024)S(1)}, f32[1345]{0:T(1024)}, u32[]{:S(2)}) copy-start(f32[1345]{0:T(1024)} %param.10) | copy-start | bytes 16144
  53.1 536.2 %all-reduce.6.cloned.1.call-start = ((), (), s32[]{:S(2)}) async-start(), calls=%async_computation.1 | async-start | bytes 2252800 | tf_op jit(solution)/shard_map/psum | solution.py:199
  58.6 0.8 copy-start.4
  63.7 258.5 %collective-permute-start.5 = (f32[200,512]{1,0:T(8,128)}, f32[200,512]{1,0:T(8,128)S(1)}, u32[]{:S(2)}, u32[]{:S(2)}) collective-permute-start(f32[200,512]{1,0:T(8,128)} %get-tuple-element.31), channel_id=1, source_target_pairs={{0,1},{1,0},{2,3},{3,2},{4,5},{5,4},{6,7},{7,6},{8,9},{9,8},{10,11... | collective-permute-start | bytes 1228808 | tf_op jit(solution)/shard_map/ppermute | solution.py:150
  81.0 1.6 collective-permute-start.7
  81.0 241.2 %collective-permute-start.6 = (s32[3,512]{1,0:T(4,128)S(1)}, s32[3,512]{1,0:T(4,128)S(1)}, u32[]{:S(2)}, u32[]{:S(2)}) collective-permute-start(s32[3,512]{1,0:T(4,128)S(1)} %get-tuple-element.46), channel_id=1, source_target_pairs={{0,1},{1,0},{2,3},{3,2},{4,5},{5,4},{6,7},{7,6},{8,9},{9,8},{10,11... | collective-permute-start | bytes 18440 | tf_op jit(solution)/shard_map/ppermute | solution.py:150
  81.5 240.6 %collective-permute-start.8 = (s32[1]{0:T(128)}, s32[1]{0:T(128)}, u32[]{:S(2)}, u32[]{:S(2)}) collective-permute-start(s32[1]{0:T(128)} %bitcast.6), channel_id=1, source_target_pairs={{0,1},{1,0},{2,3},{3,2},{4,5},{5,4},{6,7},{7,6},{8,9},{9,8},{10,11... | collective-permute-start | bytes 20 | tf_op jit(solution)/shard_map/ppermute | solution.py:150
  82.6 0.6 copy-start.7
  322.2 0.6 copy-start.9
  322.2 0.8 copy-start.2
  332.5 1.0 copy-start.14
  333.5 3.2 collective-permute-start.9
  336.7 0.8 copy-start.5
  592.5 2.8 copy-start.12
Sparse Core Ops, SparseCore 0:
  53.2 266.0 all-reduce.3
  332.7 256.5 all-reduce.5

commit v2 on v1

--- a/solution.py
+++ b/solution.py
@@ -13,6 +13,10 @@
 NN = (((1,), (0,)), ((), ()))
 NT = (((1,), (1,)), ((), ()))
 LANES = 128
+SUBLANES = 8
+ZS, XS, YS, CORES = 8, 4, 4, 2
+PLANE = XS * YS
+MESH = pl.DeviceIdType.MESH
 
 
 def split(value):
@@ -39,14 +43,18 @@
     return jnp.where(rows == ids, 1.0, 0.0).astype(BF16)
 
 
-def call(kernel, outs, args, scratch=(), name=None):
+def call(kernel, outs, args, scratch=(), name=None, collective=None):
     specs = [SMEM if kind == "smem" else VMEM for kind, _ in args]
+    params = None
+    if collective is not None:
+        params = pltpu.CompilerParams(collective_id=collective, has_side_effects=True)
     return pl.pallas_call(
         kernel,
         out_shape=[jax.ShapeDtypeStruct(*out) for out in outs],
         in_specs=specs,
         out_specs=[VMEM] * len(outs),
         scratch_shapes=list(scratch),
+        compiler_params=params,
         name=name,
     )(*[value for _, value in args])
 
@@ -110,7 +118,165 @@
     gs_ref[half:dim, :] = u_im * w_re - u_re * w_im
     tmp[0:half, :] = u_re * s_re + u_im * s_im
     tmp[half:dim, :] = u_im * s_re - u_re * s_im
-    h_ref[...] = dot_exact(split(tmp[...]), rel_spots, NT)
+    total = dot_exact(split(tmp[...]), rel_spots, NT)
+    places, tiles = tile_places(h_ref.shape, total.shape)
+    for place, (row, lane) in zip(places, tiles):
+        h_ref[place] = total[row : row + SUBLANES, lane : lane + LANES]
+    for place in places[len(tiles) :]:
+        h_ref[place] = jnp.zeros((SUBLANES, LANES), F32)
+
+
+def tile_places(shape, flat):
+    places = [(c, k, t) for c in range(shape[0]) for k in range(shape[1]) for t in range(shape[2])]
+    tiles = [(r, l) for r in range(0, flat[0], SUBLANES) for l in range(0, flat[1], LANES)]
+    return places, tiles
+
+
+def join_tiles(h_ref, whole):
+    places, tiles = tile_places(h_ref.shape, whole.shape)
+    for place, (row, lane) in zip(places, tiles):
+        whole[row : row + SUBLANES, lane : lane + LANES] = h_ref[place]
+
+
+def places_of():
+    me = lax.axis_index("dom")
+    return me % CORES, me // CORES % YS, me // (CORES * YS) % XS, me // (CORES * YS * XS)
+
+
+def device(z, x, y, c):
+    return (((z * XS + x) * YS + y) * CORES + c,)
+
+
+def remote(src, dst, sems, k, to):
+    return pltpu.make_async_remote_copy(
+        src_ref=src,
+        dst_ref=dst,
+        send_sem=sems[0].at[k],
+        recv_sem=sems[1].at[k],
+        device_id=to,
+        device_id_type=MESH,
+    )
+
+
+def meet(peers):
+    barrier = pltpu.get_barrier_semaphore()
+    for peer in peers:
+        pl.semaphore_signal(barrier, inc=1, device_id=peer, device_id_type=MESH)
+    pl.semaphore_wait(barrier, len(peers))
+
+
+def other_core():
+    c, y, x, z = places_of()
+    return device(z, x, y, 1 - c)
+
+
+def in_plane():
+    c, y, x, z = places_of()
+    plane = []
+    for k in range(PLANE):
+        px, py = (x + k // YS) % XS, (y + k % YS) % YS
+        fx, fy = (x + XS - k // YS) % XS, (y + YS - k % YS) % YS
+        plane.append((device(z, px, py, c), px * YS + py, fx * YS + fy))
+    return plane
+
+
+def in_column():
+    c, y, x, z = places_of()
+    return [device((z + k) % ZS, x, y, c) for k in range(ZS)]
+
+
+def core_sum_kernel(h_ref, out_ref, got, *sems):
+    other = other_core()
+    c = places_of()[0]
+    meet([other])
+    one = remote(h_ref.at[1 - c], got, sems, 0, other)
+    one.start()
+    one.wait()
+    out_ref[...] = h_ref[c] + got[...]
+
+
+def plane_sum_kernel(h_ref, out_ref, *more):
+    got, sems = more[:-2], more[-2:]
+    plane = in_plane()
+    meet([p[0] for p in plane[1:]])
+    sends = [remote(h_ref.at[plane[k][1]], got[k], sems, k, plane[k][0]) for k in range(1, PLANE)]
+    for one in sends[::-1]:
+        one.start()
+    total = h_ref[plane[0][1]]
+    for k in range(PLANE - 1, 0, -1):
+        sends[k - 1].wait_recv()
+        total = total + got[k][...]
+    out_ref[...] = total
+    for one in sends:
+        one.wait_send()
+
+
+def column_sum_kernel(h_ref, out_ref, level, *more):
+    got, sems = more[:-2], more[-2:]
+    column = in_column()
+    z = places_of()[3]
+    meet(column[1:])
+    sends = [remote(h_ref, got[k], sems, k, column[k]) for k in range(1, ZS)]
+    for k in (4, 3, 5, 2, 6, 1, 7):
+        sends[k - 1].start()
+    level[z] = h_ref[...]
+    for k in range(1, ZS):
+        sends[k - 1].wait_recv()
+        level[(z + ZS - k) % ZS] = got[k][...]
+    total = level[0]
+    for k in range(1, ZS):
+        total = total + level[k]
+    out_ref[...] = total
+    for one in sends:
+        one.wait_send()
+
+
+def plane_share_kernel(h_ref, out_ref, *more):
+    got, sems = more[:-2], more[-2:]
+    plane = in_plane()
+    meet([p[0] for p in plane[1:]])
+    sends = [remote(h_ref, got[k], sems, k, plane[k][0]) for k in range(1, PLANE)]
+    for one in sends[::-1]:
+        one.start()
+    out_ref[plane[0][1]] = h_ref[...]
+    for k in range(PLANE - 1, 0, -1):
+        sends[k - 1].wait_recv()
+        out_ref[plane[k][2]] = got[k][...]
+    for one in sends:
+        one.wait_send()
+
+
+def core_share_kernel(h_ref, out_ref, got, *sems):
+    other = other_core()
+    c = places_of()[0]
+    meet([other])
+    one = remote(h_ref, got, sems, 0, other)
+    one.start()
+    out_ref[c] = h_ref[...]
+    one.wait()
+    out_ref[1 - c] = got[...]
+
+
+def settings(shape, scratch, count, number):
+    return dict(
+        out_shape=jax.ShapeDtypeStruct(shape, F32),
+        in_specs=[VMEM],
+        out_specs=VMEM,
+        scratch_shapes=[*scratch, pltpu.SemaphoreType.DMA((count,)), pltpu.SemaphoreType.DMA((count,))],
+        compiler_params=pltpu.CompilerParams(collective_id=number, has_side_effects=True),
+    )
+
+
+def reduced(h, number):
+    pieces = h.shape
+    half, piece = pieces[1:], pieces[2:]
+    base = 5 * number
+    one = pltpu.VMEM(piece, F32)
+    h = pl.pallas_call(core_sum_kernel, **settings(half, [pltpu.VMEM(half, F32)], 1, base))(h)
+    h = pl.pallas_call(plane_sum_kernel, **settings(piece, [one] * PLANE, PLANE, base + 1))(h)
+    h = pl.pallas_call(column_sum_kernel, **settings(piece, [pltpu.VMEM((ZS, *piece), F32)] + [one] * ZS, ZS, base + 2))(h)
+    h = pl.pallas_call(plane_share_kernel, **settings(half, [one] * PLANE, PLANE, base + 3))(h)
+    return pl.pallas_call(core_share_kernel, **settings(pieces, [pltpu.VMEM(half, F32)], 1, base + 4))(h)
 
 
 def stepped(param, state, grad):
@@ -133,13 +299,15 @@
         more[0][...] = dot_exact(split(after), spots(edges_ref[number + 1, 0:1, :], rows))
 
 
-def rel_update_kernel(rt_ref, state_ref, h_ref, rt_out, state_out):
-    rt_out[...], state_out[...] = stepped(rt_ref[...], state_ref[...], h_ref[...])
-
-
-def rel_final_kernel(rt_ref, state_ref, h_ref, r_out, state_out, wide):
+def rel_update_kernel(rt_ref, state_ref, h_ref, rt_out, state_out, whole):
+    join_tiles(h_ref, whole)
+    rt_out[...], state_out[...] = stepped(rt_ref[...], state_ref[...], whole[...])
+
+
+def rel_final_kernel(rt_ref, state_ref, h_ref, r_out, state_out, wide, whole):
     dim = rt_ref.shape[0]
-    after, state_out[...] = stepped(rt_ref[...], state_ref[...], h_ref[...])
+    join_tiles(h_ref, whole)
+    after, state_out[...] = stepped(rt_ref[...], state_ref[...], whole[...])
     wide[0:dim, :] = after
     wide[dim:, :] = jnp.zeros((wide.shape[0] - dim, wide.shape[1]), F32)
     r_out[...] = wide[...].T[: r_out.shape[0], :dim]
@@ -171,6 +339,8 @@
         [pltpu.VMEM((rels_pad, dim_pad), F32)],
         name="rel_prep",
     )
+    tiles = dim // SUBLANES * (rels_pad // LANES)
+    pieces = (CORES, PLANE, -(-tiles // (CORES * PLANE)), SUBLANES, LANES)
     state = entity_state.reshape(1, rows)
     rel_state = jnp.pad(relation_state.reshape(1, rels), ((0, 0), (0, rels_pad - rels)), constant_values=1.0)
     table = entities
@@ -182,7 +352,7 @@
         (c,) = call(hist_kernel, [((rows, slots), F32)], [("v", their_negatives)], name=f"hist{number}")
         gt, gs, h = call(
             main_kernel,
-            [((dim, rows), F32), ((dim, slots), F32), ((dim, rels_pad), F32)],
+            [((dim, rows), F32), ((dim, slots), F32), (pieces, F32)],
             [
                 ("v", table),
                 ("v", et),
@@ -196,7 +366,7 @@
             name=f"main{number}",
         )
         gs = swapped(gs, bit)
-        h = lax.psum(h, "dom")
+        h = reduced(h, number)
         last = number == rounds - 1
         outs = call(
             lambda *refs, number=number: update_kernel(number, *refs),
@@ -212,7 +382,7 @@
                 rel_final_kernel,
                 [((rels, dim), F32), ((1, rels_pad), F32)],
                 [("v", rt), ("v", rel_state), ("v", h)],
-                [pltpu.VMEM((dim_pad, rels_pad), F32)],
+                [pltpu.VMEM((dim_pad, rels_pad), F32), pltpu.VMEM((dim, rels_pad), F32)],
                 name=f"rel_update{number}",
             )
         else:
@@ -221,6 +391,7 @@
                 rel_update_kernel,
                 [((dim, rels_pad), F32), ((1, rels_pad), F32)],
                 [("v", rt), ("v", rel_state), ("v", h)],
+                [pltpu.VMEM((dim, rels_pad), F32)],
                 name=f"rel_update{number}",
             )
     return table, state.reshape(rows), relations, rel_state[0, :rels]

time: 604 us -> 215 us (0.36)
  waiting for transfers between devices: 484 us -> 6.11 us
  Pallas kernels: 47.8 us -> 154 us
  between operations: 14.1 us -> 0.79 us
    psum x2 -> x0, waiting for transfers between devices: 477 us -> none  [body(): h = lax.psum(h, 'dom')]
    pallas_call x0 -> x10, Pallas kernels: none -> 106 us  [the longest x2 30.4 us: reduced(): pl.pallas_call(column_sum_kernel, **settings(piece, [pltpu.VMEM((ZS, *pie...]
    unnamed x35 -> x33, local copies, waits for them, and re-layouts: 15.9 us -> 14.8 us
  transfers between devices with their start and end apart: 12 -> 10, of which waited for: 5 -> 3; matrix products, arithmetic and copies ran while one was open for 1% -> 3% of each run, Pallas kernels for 4% -> 58%
where the time goes in v2:
time: 215 us; the launch traced here: 214 us
  Pallas kernels  154 us (72%)
  starting transfers between devices  36.8 us (17%)
  local copies, waits for them, and re-layouts  16.6 us (8%)
  waiting for transfers between devices  6.11 us (3%)
    pallas_call x10, Pallas kernels, call(): pl.pallas_call(kernel, out_shape=[jax.ShapeDtypeStruct(*out) for out in o...  48 us
    ppermute x10, starting transfers between devices, swapped(): lax.ppermute(value, 'dom', [(low, low ^ 1 << apart) for low in range(coun...  36.8 us
    pallas_call x2, Pallas kernels, reduced(): pl.pallas_call(column_sum_kernel, **settings(piece, [pltpu.VMEM((ZS, *pie...  30.4 us
    pallas_call x2, Pallas kernels, reduced(): pl.pallas_call(plane_sum_kernel, **settings(piece, [one] * PLANE, PLANE,...  30 us
    pallas_call x2, Pallas kernels, reduced(): pl.pallas_call(plane_share_kernel, **settings(half, [one] * PLANE, PLANE,...  26.8 us
    unnamed x33, local copies, waits for them, and re-layouts  14.8 us
    pallas_call x2, Pallas kernels, reduced(): pl.pallas_call(core_share_kernel, **settings(pieces, [pltpu.VMEM(half, F3...  10 us
    pallas_call x2, Pallas kernels, reduced(): pl.pallas_call(core_sum_kernel, **settings(half, [pltpu.VMEM(half, F32)],...  8.37 us
  transfers between devices with their start and end apart: 10, of which 3 were waited for; matrix products, arithmetic and copies ran while one was open for 3% of the time, Pallas kernels for 58%

profile of v2, /device:TPU:1, one launch (start us, length us, event | category | flops | bytes accessed | tf_op | source)
XLA Modules:
  0.0 213.9 jit_solution(928655821282987552)
XLA Ops:
  0.6 1.3 copy.12.edges_ref.refs_4_
  1.9 2.6 %copy.11.e_ref = f32[1024,200]{1,0:T(8,128)} copy(f32[1024,200]{0,1:T(8,128)} %param.7) | data formatting | bytes 1638400 | tf_op args[0]
  4.5 2.8 %prep.1 = (f32[200,1024]{1,0:T(8,128)}, f32[200,512]{1,0:T(8,128)}) custom-call(f32[1024,200]{1,0:T(8,128)} %copy.11.e_ref, s32[2,3,512]{2,1,0:T(4,128)} %copy.12.edges_ref.refs_4_), custom_call_target="tpu_custom_call" | custom-call | tf_op jit(solution)/shard_map/prep/pallas_call | solution.py:51
  7.3 7.7 %collective-permute-start = (f32[200,512]{1,0:T(8,128)}, f32[200,512]{1,0:T(8,128)S(1)}, u32[]{:S(2)}, u32[]{:S(2)}) collective-permute-start(f32[200,512]{1,0:T(8,128)} %get-tuple-element.23), channel_id=1, source_target_pairs={{0,128},{1,129},{2,130},{3,131},{4,132},{5,133},{6,134},{7,135},{8... | collective-permute-start | bytes 1228808 | tf_op jit(solution)/shard_map/ppermute | solution.py:318
  15.1 0.1 collective-permute-start.1
  15.2 5.3 %collective-permute-start.2 = (s32[4,1000]{1,0:T(4,128)S(1)}, s32[4,1000]{1,0:T(4,128)S(1)}, u32[]{:S(2)}, u32[]{:S(2)}) collective-permute-start(s32[4,1000]{1,0:T(4,128)S(1)} %get-tuple-element.45), channel_id=1, source_target_pairs={{0,128},{1,129},{2,130},{3,131},{4,132},{5,133},{6,134},{7,135},{8... | collective-permute-start | bytes 48008 | tf_op jit(solution)/shard_map/ppermute | solution.py:318
  20.5 0.6 fusion
  21.0 0.1 collective-permute-start.3
  21.2 1.5 copy.13.r_ref
  22.7 2.8 %rel_prep.1.rt_ref = f32[200,1408]{1,0:T(8,128)} custom-call(f32[1345,200]{1,0:T(8,128)} %copy.13.r_ref), custom_call_target="tpu_custom_call" | custom-call | tf_op jit(solution)/shard_map/rel_prep/pallas_call | solution.py:51
  25.5 0.1 collective-permute-done.2.neg_ref
  25.6 0.6 copy-done.8
  26.2 4.4 %hist0.1.c_ref = f32[1024,512]{1,0:T(8,128)} custom-call(s32[4,1000]{1,0:T(4,128)} %copy-done.8), custom_call_target="tpu_custom_call" | custom-call | tf_op jit(solution)/shard_map/hist0/pallas_call | solution.py:51
  30.6 0.6 copy-done.10
  31.2 0.2 copy-done.3
  31.3 9.6 %main0.1 = (f32[200,1024]{1,0:T(8,128)}, f32[200,512]{1,0:T(8,128)}, f32[2,16,9,8,128]{4,3,2,1,0:T(8,128)}) custom-call(f32[1024,200]{1,0:T(8,128)} %copy.11.e_ref, f32[200,1024]{1,0:T(8,128)} %get-tuple-element.22.et_ref.refs_0_, f32[200,1408]{1,0:T(8,128)} %rel_prep.1.rt_ref, f32[200,512]{1,0:T(8,128)} %copy-done.3, s32[3,512]{1,0:T(4,128)} %copy-done.10, ...), custom_call_target="tpu_custom_call" | custom-call | tf_op jit(solution)/shard_map/main0/pallas_call | solution.py:51
  40.9 5.6 %collective-permute-start.4 = (f32[200,512]{1,0:T(8,128)}, f32[200,512]{1,0:T(8,128)S(1)}, u32[]{:S(2)}, u32[]{:S(2)}) collective-permute-start(f32[200,512]{1,0:T(8,128)} %get-tuple-element.25), channel_id=1, source_target_pairs={{0,128},{1,129},{2,130},{3,131},{4,132},{5,133},{6,134},{7,135},{8... | collective-permute-start | bytes 1228808 | tf_op jit(solution)/shard_map/ppermute | solution.py:318
  46.5 5.5 %collective-permute-done.4.refs_3_ = f32[200,512]{1,0:T(8,128)S(1)} collective-permute-done((f32[200,512]{1,0:T(8,128)}, f32[200,512]{1,0:T(8,128)S(1)}, u32[]{:S(2)}, u32[]{:S(2)}) %collective-permute-start.4) | collective-permute-done | bytes 409632 | tf_op jit(solution)/shard_map/ppermute | solution.py:318
  52.1 0.8 copy-done.5
  52.8 4.3 %update0.1 = (f32[1024,200]{1,0:T(8,128)}, f32[1,1024]{1,0:T(1,128)}, f32[200,1024]{1,0:T(8,128)}, f32[200,512]{1,0:T(8,128)}) custom-call(f32[200,1024]{1,0:T(8,128)} %get-tuple-element.22.et_ref.refs_0_, f32[1,1024]{1,0:T(1,128)} %bitcast.12, f32[200,1024]{1,0:T(8,128)} %get-tuple-element.24.refs_2_, f32[200,512]{1,0:T(8,128)} %copy-done.5, ...), custom_call_target="tpu_custom_call" | custom-call | tf_op jit(solution)/shard_map/update0/pallas_call | solution.py:51
  57.1 17.1 %collective-permute-start.5 = (f32[200,512]{1,0:T(8,128)}, f32[200,512]{1,0:T(8,128)S(1)}, u32[]{:S(2)}, u32[]{:S(2)}) collective-permute-start(f32[200,512]{1,0:T(8,128)} %get-tuple-element.31), channel_id=1, source_target_pairs={{0,1},{1,0},{2,3},{3,2},{4,5},{5,4},{6,7},{7,6},{8,9},{9,8},{10,11... | collective-permute-start | bytes 1228808 | tf_op jit(solution)/shard_map/ppermute | solution.py:318
  74.2 0.5 collective-permute-start.6
  74.7 0.6 pad.4.state_ref
  75.3 0.5 collective-permute-done.7.neg_ref
  75.8 0.6 copy-done.7
  76.4 4.4 %hist1.1.c_ref = f32[1024,512]{1,0:T(8,128)} custom-call(s32[4,1000]{1,0:T(4,128)} %copy-done.7), custom_call_target="tpu_custom_call" | custom-call | tf_op jit(solution)/shard_map/hist1/pallas_call | solution.py:51
  80.8 4.2 %shard_map.102.h_ref = f32[16,9,8,128]{3,2,1,0:T(8,128)} custom-call(f32[2,16,9,8,128]{4,3,2,1,0:T(8,128)} %get-tuple-element.29.h_ref), custom_call_target="tpu_custom_call" | custom-call | tf_op jit(solution)/shard_map/pallas_call | solution.py:275
  85.0 15.8 %shard_map.103.h_ref = f32[9,8,128]{2,1,0:T(8,128)} custom-call(f32[16,9,8,128]{3,2,1,0:T(8,128)} %shard_map.102.h_ref), custom_call_target="tpu_custom_call" | custom-call | tf_op jit(solution)/shard_map/pallas_call | solution.py:276
  100.8 17.3 %shard_map.104.h_ref = f32[9,8,128]{2,1,0:T(8,128)} custom-call(f32[9,8,128]{2,1,0:T(8,128)} %shard_map.103.h_ref), custom_call_target="tpu_custom_call" | custom-call | tf_op jit(solution)/shard_map/pallas_call | solution.py:277
  118.1 13.6 %shard_map.105.h_ref = f32[16,9,8,128]{3,2,1,0:T(8,128)} custom-call(f32[9,8,128]{2,1,0:T(8,128)} %shard_map.104.h_ref), custom_call_target="tpu_custom_call" | custom-call | tf_op jit(solution)/shard_map/pallas_call | solution.py:278
  131.7 4.9 %shard_map.106.h_ref = f32[2,16,9,8,128]{4,3,2,1,0:T(8,128)} custom-call(f32[16,9,8,128]{3,2,1,0:T(8,128)} %shard_map.105.h_ref), custom_call_target="tpu_custom_call" | custom-call | tf_op jit(solution)/shard_map/pallas_call | solution.py:279
  136.6 2.9 %rel_update0.1 = (f32[200,1408]{1,0:T(8,128)}, f32[1,1408]{1,0:T(1,128)}) custom-call(f32[200,1408]{1,0:T(8,128)} %rel_prep.1.rt_ref, f32[1,1408]{1,0:T(1,128)} %pad.4.state_ref, f32[2,16,9,8,128]{4,3,2,1,0:T(8,128)} %shard_map.106.h_ref), custom_call_target="tpu_custom_call" | custom-call | tf_op jit(solution)/shard_map/rel_update0/pallas_call | solution.py:51
  139.5 0.0 copy-start.9
  139.5 0.6 copy-done.9
  140.1 0.2 copy-done.2
  140.3 9.6 %main1.1 = (f32[200,1024]{1,0:T(8,128)}, f32[200,512]{1,0:T(8,128)}, f32[2,16,9,8,128]{4,3,2,1,0:T(8,128)}) custom-call(f32[1024,200]{1,0:T(8,128)} %get-tuple-element.28.e_ref, f32[200,1024]{1,0:T(8,128)} %get-tuple-element.26.et_ref.refs_0_, f32[200,1408]{1,0:T(8,128)} %get-tuple-element.30.rt_ref, f32[200,512]{1,0:T(8,128)} %copy-done.2, ...), custom_call_target="tpu_custom_call" | custom-call | tf_op jit(solution)/shard_map/main1/pallas_call | solution.py:51
  149.9 0.4 collective-permute-start.9
  150.3 4.2 %shard_map.107.h_ref = f32[16,9,8,128]{3,2,1,0:T(8,128)} custom-call(f32[2,16,9,8,128]{4,3,2,1,0:T(8,128)} %get-tuple-element.37.h_ref), custom_call_target="tpu_custom_call" | custom-call | tf_op jit(solution)/shard_map/pallas_call | solution.py:275
  154.5 14.2 %shard_map.108.h_ref = f32[9,8,128]{2,1,0:T(8,128)} custom-call(f32[16,9,8,128]{3,2,1,0:T(8,128)} %shard_map.107.h_ref), custom_call_target="tpu_custom_call" | custom-call | tf_op jit(solution)/shard_map/pallas_call | solution.py:276
  168.7 13.1 %shard_map.109.h_ref = f32[9,8,128]{2,1,0:T(8,128)} custom-call(f32[9,8,128]{2,1,0:T(8,128)} %shard_map.108.h_ref), custom_call_target="tpu_custom_call" | custom-call | tf_op jit(solution)/shard_map/pallas_call | solution.py:277
  181.8 13.3 %shard_map.110.h_ref = f32[16,9,8,128]{3,2,1,0:T(8,128)} custom-call(f32[9,8,128]{2,1,0:T(8,128)} %shard_map.109.h_ref), custom_call_target="tpu_custom_call" | custom-call | tf_op jit(solution)/shard_map/pallas_call | solution.py:278
  195.1 5.1 %shard_map.111.h_ref = f32[2,16,9,8,128]{4,3,2,1,0:T(8,128)} custom-call(f32[16,9,8,128]{3,2,1,0:T(8,128)} %shard_map.110.h_ref), custom_call_target="tpu_custom_call" | custom-call | tf_op jit(solution)/shard_map/pallas_call | solution.py:279
  200.2 3.3 %rel_update1.1 = (f32[1345,200]{1,0:T(8,128)}, f32[1,1408]{1,0:T(1,128)}) custom-call(f32[200,1408]{1,0:T(8,128)} %get-tuple-element.30.rt_ref, f32[1,1408]{1,0:T(1,128)} %get-tuple-element.36.state_ref, f32[2,16,9,8,128]{4,3,2,1,0:T(8,128)} %shard_map.111.h_ref), custom_call_target="tpu_custom_call" | custom-call | tf_op jit(solution)/shard_map/rel_update1/pallas_call | solution.py:51
  203.5 2.8 %copy.20 = f32[1345,200]{0,1:T(8,128)} copy(f32[1345,200]{1,0:T(8,128)} %get-tuple-element.42) | data formatting | bytes 2152000
  206.2 0.6 slice_reduce_fusion
  206.9 0.7 copy-done.4
  207.6 3.9 %update1.1 = (f32[1024,200]{1,0:T(8,128)}, f32[1,1024]{1,0:T(1,128)}, f32[200,1024]{1,0:T(8,128)}) custom-call(f32[200,1024]{1,0:T(8,128)} %get-tuple-element.26.et_ref.refs_0_, f32[1,1024]{1,0:T(1,128)} %get-tuple-element.27.refs_1_, f32[200,1024]{1,0:T(8,128)} %get-tuple-element.32.refs_2_, f32[200,512]{1,0:T(8,128)} %copy-done.4, ...), custom_call_target="tpu_custom_call" | custom-call | tf_op jit(solution)/shard_map/update1/pallas_call | solution.py:51
  211.5 2.4 %copy.19 = f32[1024,200]{0,1:T(8,128)} copy(f32[1024,200]{1,0:T(8,128)} %get-tuple-element.40) | data formatting | bytes 1638400
  (31 shorter events, 0.1 us)
Async XLA Ops:
  1.9 13.1 %copy-start.1 = (s32[2,3,512]{2,1,0:T(4,128)S(1)}, s32[2,3,512]{2,1,0:T(4,128)}, u32[]{:S(2)}) copy-start(s32[2,3,512]{2,1,0:T(4,128)} %copy.12.edges_ref.refs_4_) | copy-start | bytes 36868
  1.9 13.2 %copy-start.6 = (s32[2,4,1000]{2,1,0:T(4,128)S(1)}, s32[2,4,1000]{2,1,0:T(4,128)}, u32[]{:S(2)}) copy-start(s32[2,4,1000]{2,1,0:T(4,128)} %param.12) | copy-start | bytes 96004
  1.9 18.5 %copy-start.13 = (s32[2,1]{0,1:T(1,128)S(1)}, s32[2,1]{0,1:T(1,128)}, u32[]{:S(2)}) copy-start(s32[2,1]{0,1:T(1,128)} %param.13) | copy-start | bytes 28
  1.9 19.2 %copy-start = (f32[1345,200]{0,1:T(8,128)S(1)}, f32[1345,200]{0,1:T(8,128)}, u32[]{:S(2)}) copy-start(f32[1345,200]{0,1:T(8,128)} %param.9) | copy-start | bytes 3228004
  7.3 23.2 %collective-permute-start = (f32[200,512]{1,0:T(8,128)}, f32[200,512]{1,0:T(8,128)S(1)}, u32[]{:S(2)}, u32[]{:S(2)}) collective-permute-start(f32[200,512]{1,0:T(8,128)} %get-tuple-element.23), channel_id=1, source_target_pairs={{0,128},{1,129},{2,130},{3,131},{4,132},{5,133},{6,134},{7,135},{8... | collective-permute-start | bytes 1228808 | tf_op jit(solution)/shard_map/ppermute | solution.py:318
  15.1 15.5 %collective-permute-start.1 = (s32[3,512]{1,0:T(4,128)S(1)}, s32[3,512]{1,0:T(4,128)S(1)}, u32[]{:S(2)}, u32[]{:S(2)}) collective-permute-start(s32[3,512]{1,0:T(4,128)S(1)} %get-tuple-element.47), channel_id=1, source_target_pairs={{0,128},{1,129},{2,130},{3,131},{4,132},{5,133},{6,134},{7,135},{8... | collective-permute-start | bytes 18440 | tf_op jit(solution)/shard_map/ppermute | solution.py:318
  15.2 10.4 %collective-permute-start.2 = (s32[4,1000]{1,0:T(4,128)S(1)}, s32[4,1000]{1,0:T(4,128)S(1)}, u32[]{:S(2)}, u32[]{:S(2)}) collective-permute-start(s32[4,1000]{1,0:T(4,128)S(1)} %get-tuple-element.45), channel_id=1, source_target_pairs={{0,128},{1,129},{2,130},{3,131},{4,132},{5,133},{6,134},{7,135},{8... | collective-permute-start | bytes 48008 | tf_op jit(solution)/shard_map/ppermute | solution.py:318
  21.0 9.5 %collective-permute-start.3 = (s32[1]{0:T(128)}, s32[1]{0:T(128)}, u32[]{:S(2)}, u32[]{:S(2)}) collective-permute-start(s32[1]{0:T(128)} %bitcast.3), channel_id=1, source_target_pairs={{0,128},{1,129},{2,130},{3,131},{4,132},{5,133},{6,134},{7,135},{8... | collective-permute-start | bytes 20 | tf_op jit(solution)/shard_map/ppermute | solution.py:318
  25.6 0.6 copy-start.8
  30.6 0.6 copy-start.10
  30.6 0.8 copy-start.3
  40.9 33.8 %copy-start.11 = (f32[1345]{0:T(1024)S(1)}, f32[1345]{0:T(1024)}, u32[]{:S(2)}) copy-start(f32[1345]{0:T(1024)} %param.10) | copy-start | bytes 16144
  40.9 11.1 %collective-permute-start.4 = (f32[200,512]{1,0:T(8,128)}, f32[200,512]{1,0:T(8,128)S(1)}, u32[]{:S(2)}, u32[]{:S(2)}) collective-permute-start(f32[200,512]{1,0:T(8,128)} %get-tuple-element.25), channel_id=1, source_target_pairs={{0,128},{1,129},{2,130},{3,131},{4,132},{5,133},{6,134},{7,135},{8... | collective-permute-start | bytes 1228808 | tf_op jit(solution)/shard_map/ppermute | solution.py:318
  52.1 0.8 copy-start.5
  57.1 82.4 %collective-permute-start.5 = (f32[200,512]{1,0:T(8,128)}, f32[200,512]{1,0:T(8,128)S(1)}, u32[]{:S(2)}, u32[]{:S(2)}) collective-permute-start(f32[200,512]{1,0:T(8,128)} %get-tuple-element.31), channel_id=1, source_target_pairs={{0,1},{1,0},{2,3},{3,2},{4,5},{5,4},{6,7},{7,6},{8,9},{9,8},{10,11... | collective-permute-start | bytes 1228808 | tf_op jit(solution)/shard_map/ppermute | solution.py:318
  74.2 1.6 collective-permute-start.7
  74.2 65.3 %collective-permute-start.6 = (s32[3,512]{1,0:T(4,128)S(1)}, s32[3,512]{1,0:T(4,128)S(1)}, u32[]{:S(2)}, u32[]{:S(2)}) collective-permute-start(s32[3,512]{1,0:T(4,128)S(1)} %get-tuple-element.46), channel_id=1, source_target_pairs={{0,1},{1,0},{2,3},{3,2},{4,5},{5,4},{6,7},{7,6},{8,9},{9,8},{10,11... | collective-permute-start | bytes 18440 | tf_op jit(solution)/shard_map/ppermute | solution.py:318
  74.7 64.8 %collective-permute-start.8 = (s32[1]{0:T(128)}, s32[1]{0:T(128)}, u32[]{:S(2)}, u32[]{:S(2)}) collective-permute-start(s32[1]{0:T(128)} %bitcast.6), channel_id=1, source_target_pairs={{0,1},{1,0},{2,3},{3,2},{4,5},{5,4},{6,7},{7,6},{8,9},{9,8},{10,11... | collective-permute-start | bytes 20 | tf_op jit(solution)/shard_map/ppermute | solution.py:318
  75.8 0.6 copy-start.7
  139.5 0.6 copy-start.9
  139.5 0.8 copy-start.2
  149.9 56.9 %collective-permute-start.9 = (f32[200,512]{1,0:T(8,128)}, f32[200,512]{1,0:T(8,128)S(1)}, u32[]{:S(2)}, u32[]{:S(2)}) collective-permute-start(f32[200,512]{1,0:T(8,128)} %get-tuple-element.33), channel_id=1, source_target_pairs={{0,1},{1,0},{2,3},{3,2},{4,5},{5,4},{6,7},{7,6},{8,9},{9,8},{10,11... | collective-permute-start | bytes 1228808 | tf_op jit(solution)/shard_map/ppermute | solution.py:318
  203.5 2.8 %copy-start.12 = (f32[1,1408]{1,0:T(1,128)S(1)}, f32[1,1408]{1,0:T(1,128)}, u32[]{:S(2)}) copy-start(f32[1,1408]{1,0:T(1,128)} %get-tuple-element.39) | copy-start | bytes 16900
  206.9 0.7 copy-start.4

commit v3 on v2

--- a/solution.py
+++ b/solution.py
@@ -185,29 +185,29 @@
     return [device((z + k) % ZS, x, y, c) for k in range(ZS)]
 
 
-def core_sum_kernel(h_ref, out_ref, got, *sems):
+def spread_sum_kernel(h_ref, out_ref, *more):
+    s0, r0, s1, r1 = more[-4:]
+    acc, got0, got1 = (more[i * PLANE : (i + 1) * PLANE] for i in range(3))
     other = other_core()
+    plane = in_plane()
     c = places_of()[0]
-    meet([other])
-    one = remote(h_ref.at[1 - c], got, sems, 0, other)
-    one.start()
-    one.wait()
-    out_ref[...] = h_ref[c] + got[...]
-
-
-def plane_sum_kernel(h_ref, out_ref, *more):
-    got, sems = more[:-2], more[-2:]
-    plane = in_plane()
-    meet([p[0] for p in plane[1:]])
-    sends = [remote(h_ref.at[plane[k][1]], got[k], sems, k, plane[k][0]) for k in range(1, PLANE)]
-    for one in sends[::-1]:
-        one.start()
-    total = h_ref[plane[0][1]]
-    for k in range(PLANE - 1, 0, -1):
-        sends[k - 1].wait_recv()
-        total = total + got[k][...]
+    meet([other] + [p[0] for p in plane[1:]])
+    order = range(PLANE - 1, -1, -1)
+    first = [remote(h_ref.at[1 - c, plane[k][1]], got0[k], (s0, r0), k, other) for k in range(PLANE)]
+    second = [remote(acc[k], got1[k], (s1, r1), k, plane[k][0]) for k in range(PLANE)]
+    for k in order:
+        first[k].start()
+    for k in order:
+        first[k].wait_recv()
+        acc[k][...] = h_ref[c, plane[k][1]] + got0[k][...]
+        if k < PLANE - 1:
+            second[k + 1].start()
+    total = acc[0][...]
+    for k in order[:-1]:
+        second[k].wait_recv()
+        total = total + got1[k][...]
     out_ref[...] = total
-    for one in sends:
+    for one in first + second[1:]:
         one.wait_send()
 
 
@@ -231,52 +231,50 @@
         one.wait_send()
 
 
-def plane_share_kernel(h_ref, out_ref, *more):
-    got, sems = more[:-2], more[-2:]
+def spread_share_kernel(h_ref, out_ref, *more):
+    s3, r3, s4, r4 = more[-4:]
+    got3, got4 = (more[i * PLANE : (i + 1) * PLANE] for i in range(2))
+    other = other_core()
     plane = in_plane()
-    meet([p[0] for p in plane[1:]])
-    sends = [remote(h_ref, got[k], sems, k, plane[k][0]) for k in range(1, PLANE)]
-    for one in sends[::-1]:
-        one.start()
-    out_ref[plane[0][1]] = h_ref[...]
-    for k in range(PLANE - 1, 0, -1):
-        sends[k - 1].wait_recv()
-        out_ref[plane[k][2]] = got[k][...]
-    for one in sends:
+    c = places_of()[0]
+    meet([other] + [p[0] for p in plane[1:]])
+    order = range(PLANE - 1, 0, -1)
+    fourth = [remote(h_ref, got3[k], (s3, r3), k, plane[k][0]) for k in range(PLANE)]
+    fifth = [remote(got3[k] if k else h_ref, got4[k], (s4, r4), k, other) for k in range(PLANE)]
+    for k in order:
+        fourth[k].start()
+    fifth[0].start()
+    out_ref[c, plane[0][1]] = h_ref[...]
+    for k in order:
+        fourth[k].wait_recv()
+        fifth[k].start()
+        out_ref[c, plane[k][2]] = got3[k][...]
+    for k in [0, *order]:
+        fifth[k].wait_recv()
+        out_ref[1 - c, plane[k][2]] = got4[k][...]
+    for one in fourth[1:] + fifth:
         one.wait_send()
 
 
-def core_share_kernel(h_ref, out_ref, got, *sems):
-    other = other_core()
-    c = places_of()[0]
-    meet([other])
-    one = remote(h_ref, got, sems, 0, other)
-    one.start()
-    out_ref[c] = h_ref[...]
-    one.wait()
-    out_ref[1 - c] = got[...]
-
-
-def settings(shape, scratch, count, number):
+def settings(shape, scratch, counts, number):
+    dma = pltpu.SemaphoreType.DMA
     return dict(
         out_shape=jax.ShapeDtypeStruct(shape, F32),
         in_specs=[VMEM],
         out_specs=VMEM,
-        scratch_shapes=[*scratch, pltpu.SemaphoreType.DMA((count,)), pltpu.SemaphoreType.DMA((count,))],
+        scratch_shapes=[*scratch, *(dma((count,)) for count in counts for _ in range(2))],
         compiler_params=pltpu.CompilerParams(collective_id=number, has_side_effects=True),
     )
 
 
 def reduced(h, number):
     pieces = h.shape
-    half, piece = pieces[1:], pieces[2:]
-    base = 5 * number
+    piece = pieces[2:]
+    base = 3 * number
     one = pltpu.VMEM(piece, F32)
-    h = pl.pallas_call(core_sum_kernel, **settings(half, [pltpu.VMEM(half, F32)], 1, base))(h)
-    h = pl.pallas_call(plane_sum_kernel, **settings(piece, [one] * PLANE, PLANE, base + 1))(h)
-    h = pl.pallas_call(column_sum_kernel, **settings(piece, [pltpu.VMEM((ZS, *piece), F32)] + [one] * ZS, ZS, base + 2))(h)
-    h = pl.pallas_call(plane_share_kernel, **settings(half, [one] * PLANE, PLANE, base + 3))(h)
-    return pl.pallas_call(core_share_kernel, **settings(pieces, [pltpu.VMEM(half, F32)], 1, base + 4))(h)
+    h = pl.pallas_call(spread_sum_kernel, **settings(piece, [one] * (3 * PLANE), (PLANE, PLANE), base))(h)
+    h = pl.pallas_call(column_sum_kernel, **settings(piece, [pltpu.VMEM((ZS, *piece), F32)] + [one] * ZS, (ZS,), base + 1))(h)
+    return pl.pallas_call(spread_share_kernel, **settings(pieces, [one] * (2 * PLANE), (PLANE, PLANE), base + 2))(h)
 
 
 def stepped(param, state, grad):

time: 215 us -> 207 us (0.963)
  Pallas kernels: 154 us -> 146 us
    pallas_call x8 -> x4, Pallas kernels: 75.2 us -> 67.8 us  [the longest x2 34.9 us: reduced(): pl.pallas_call(spread_sum_kernel, **settings(piece, [one] * (3 * PLANE),...]
  transfers between devices with their start and end apart: 10 -> 10, of which waited for: 3 -> 3; matrix products, arithmetic and copies ran while one was open for 3% -> 3% of each run, Pallas kernels for 58% -> 56%
where the time goes in v3:
time: 207 us; the launch traced here: 206 us
  Pallas kernels  146 us (71%)
  starting transfers between devices  36.5 us (18%)
  local copies, waits for them, and re-layouts  16.6 us (8%)
  waiting for transfers between devices  6.11 us (3%)
    pallas_call x10, Pallas kernels, call(): pl.pallas_call(kernel, out_shape=[jax.ShapeDtypeStruct(*out) for out in o...  47.9 us
    ppermute x10, starting transfers between devices, swapped(): lax.ppermute(value, 'dom', [(low, low ^ 1 << apart) for low in range(coun...  36.5 us
    pallas_call x2, Pallas kernels, reduced(): pl.pallas_call(spread_sum_kernel, **settings(piece, [one] * (3 * PLANE),...  34.9 us
    pallas_call x2, Pallas kernels, reduced(): pl.pallas_call(spread_share_kernel, **settings(pieces, [one] * (2 * PLANE...  32.9 us
    pallas_call x2, Pallas kernels, reduced(): pl.pallas_call(column_sum_kernel, **settings(piece, [pltpu.VMEM((ZS, *pie...  30.3 us
    unnamed x33, local copies, waits for them, and re-layouts  14.8 us
    ppermute x10, waiting for transfers between devices, swapped(): lax.ppermute(value, 'dom', [(low, low ^ 1 << apart) for low in range(coun...  6.11 us
  transfers between devices with their start and end apart: 10, of which 3 were waited for; matrix products, arithmetic and copies ran while one was open for 3% of the time, Pallas kernels for 56%

profile of v3, /device:TPU:1, one launch (start us, length us, event | category | flops | bytes accessed | tf_op | source)
XLA Modules:
  0.0 206.1 jit_solution(663968754638651683)
XLA Ops:
  0.6 1.3 copy.12.edges_ref.refs_4_
  1.9 2.6 %copy.11.e_ref = f32[1024,200]{1,0:T(8,128)} copy(f32[1024,200]{0,1:T(8,128)} %param.7) | data formatting | bytes 1638400 | tf_op args[0]
  4.5 2.8 %prep.1 = (f32[200,1024]{1,0:T(8,128)}, f32[200,512]{1,0:T(8,128)}) custom-call(f32[1024,200]{1,0:T(8,128)} %copy.11.e_ref, s32[2,3,512]{2,1,0:T(4,128)} %copy.12.edges_ref.refs_4_), custom_call_target="tpu_custom_call" | custom-call | tf_op jit(solution)/shard_map/prep/pallas_call | solution.py:51
  7.3 7.7 %collective-permute-start = (f32[200,512]{1,0:T(8,128)}, f32[200,512]{1,0:T(8,128)S(1)}, u32[]{:S(2)}, u32[]{:S(2)}) collective-permute-start(f32[200,512]{1,0:T(8,128)} %get-tuple-element.23), channel_id=1, source_target_pairs={{0,128},{1,129},{2,130},{3,131},{4,132},{5,133},{6,134},{7,135},{8... | collective-permute-start | bytes 1228808 | tf_op jit(solution)/shard_map/ppermute | solution.py:316
  15.1 0.1 collective-permute-start.1
  15.2 5.3 %collective-permute-start.2 = (s32[4,1000]{1,0:T(4,128)S(1)}, s32[4,1000]{1,0:T(4,128)S(1)}, u32[]{:S(2)}, u32[]{:S(2)}) collective-permute-start(s32[4,1000]{1,0:T(4,128)S(1)} %get-tuple-element.45), channel_id=1, source_target_pairs={{0,128},{1,129},{2,130},{3,131},{4,132},{5,133},{6,134},{7,135},{8... | collective-permute-start | bytes 48008 | tf_op jit(solution)/shard_map/ppermute | solution.py:316
  20.5 0.6 fusion
  21.0 0.1 collective-permute-start.3
  21.2 1.5 copy.13.r_ref
  22.7 2.8 %rel_prep.1.rt_ref = f32[200,1408]{1,0:T(8,128)} custom-call(f32[1345,200]{1,0:T(8,128)} %copy.13.r_ref), custom_call_target="tpu_custom_call" | custom-call | tf_op jit(solution)/shard_map/rel_prep/pallas_call | solution.py:51
  25.5 0.1 collective-permute-done.2.neg_ref
  25.6 0.6 copy-done.8
  26.2 4.4 %hist0.1.c_ref = f32[1024,512]{1,0:T(8,128)} custom-call(s32[4,1000]{1,0:T(4,128)} %copy-done.8), custom_call_target="tpu_custom_call" | custom-call | tf_op jit(solution)/shard_map/hist0/pallas_call | solution.py:51
  30.6 0.0 collective-permute-done.3.count_ref
  30.6 0.0 collective-permute-done.1.edges_ref
  30.6 0.6 copy-done.10
  31.2 0.2 copy-done.3
  31.4 9.5 %main0.1 = (f32[200,1024]{1,0:T(8,128)}, f32[200,512]{1,0:T(8,128)}, f32[2,16,9,8,128]{4,3,2,1,0:T(8,128)}) custom-call(f32[1024,200]{1,0:T(8,128)} %copy.11.e_ref, f32[200,1024]{1,0:T(8,128)} %get-tuple-element.22.et_ref.refs_0_, f32[200,1408]{1,0:T(8,128)} %rel_prep.1.rt_ref, f32[200,512]{1,0:T(8,128)} %copy-done.3, s32[3,512]{1,0:T(4,128)} %copy-done.10, ...), custom_call_target="tpu_custom_call" | custom-call | tf_op jit(solution)/shard_map/main0/pallas_call | solution.py:51
  40.9 5.6 %collective-permute-start.4 = (f32[200,512]{1,0:T(8,128)}, f32[200,512]{1,0:T(8,128)S(1)}, u32[]{:S(2)}, u32[]{:S(2)}) collective-permute-start(f32[200,512]{1,0:T(8,128)} %get-tuple-element.25), channel_id=1, source_target_pairs={{0,128},{1,129},{2,130},{3,131},{4,132},{5,133},{6,134},{7,135},{8... | collective-permute-start | bytes 1228808 | tf_op jit(solution)/shard_map/ppermute | solution.py:316
  46.5 5.5 %collective-permute-done.4.refs_3_ = f32[200,512]{1,0:T(8,128)S(1)} collective-permute-done((f32[200,512]{1,0:T(8,128)}, f32[200,512]{1,0:T(8,128)S(1)}, u32[]{:S(2)}, u32[]{:S(2)}) %collective-permute-start.4) | collective-permute-done | bytes 409632 | tf_op jit(solution)/shard_map/ppermute | solution.py:316
  52.0 0.8 copy-done.5
  52.8 4.3 %update0.1 = (f32[1024,200]{1,0:T(8,128)}, f32[1,1024]{1,0:T(1,128)}, f32[200,1024]{1,0:T(8,128)}, f32[200,512]{1,0:T(8,128)}) custom-call(f32[200,1024]{1,0:T(8,128)} %get-tuple-element.22.et_ref.refs_0_, f32[1,1024]{1,0:T(1,128)} %bitcast.12, f32[200,1024]{1,0:T(8,128)} %get-tuple-element.24.refs_2_, f32[200,512]{1,0:T(8,128)} %copy-done.5, ...), custom_call_target="tpu_custom_call" | custom-call | tf_op jit(solution)/shard_map/update0/pallas_call | solution.py:51
  57.1 17.1 %collective-permute-start.5 = (f32[200,512]{1,0:T(8,128)}, f32[200,512]{1,0:T(8,128)S(1)}, u32[]{:S(2)}, u32[]{:S(2)}) collective-permute-start(f32[200,512]{1,0:T(8,128)} %get-tuple-element.31), channel_id=1, source_target_pairs={{0,1},{1,0},{2,3},{3,2},{4,5},{5,4},{6,7},{7,6},{8,9},{9,8},{10,11... | collective-permute-start | bytes 1228808 | tf_op jit(solution)/shard_map/ppermute | solution.py:316
  74.2 0.0 collective-permute-start.7
  74.2 0.5 collective-permute-start.6
  74.7 0.6 pad.4.state_ref
  75.3 0.5 collective-permute-done.7.neg_ref
  75.8 0.6 copy-done.7
  76.4 4.4 %hist1.1.c_ref = f32[1024,512]{1,0:T(8,128)} custom-call(s32[4,1000]{1,0:T(4,128)} %copy-done.7), custom_call_target="tpu_custom_call" | custom-call | tf_op jit(solution)/shard_map/hist1/pallas_call | solution.py:51
  80.8 18.4 %shard_map.102.h_ref = f32[9,8,128]{2,1,0:T(8,128)} custom-call(f32[2,16,9,8,128]{4,3,2,1,0:T(8,128)} %get-tuple-element.29.h_ref), custom_call_target="tpu_custom_call" | custom-call | tf_op jit(solution)/shard_map/pallas_call | solution.py:275
  99.2 17.3 %shard_map.103.h_ref = f32[9,8,128]{2,1,0:T(8,128)} custom-call(f32[9,8,128]{2,1,0:T(8,128)} %shard_map.102.h_ref), custom_call_target="tpu_custom_call" | custom-call | tf_op jit(solution)/shard_map/pallas_call | solution.py:276
  116.5 16.4 %shard_map.104.h_ref = f32[2,16,9,8,128]{4,3,2,1,0:T(8,128)} custom-call(f32[9,8,128]{2,1,0:T(8,128)} %shard_map.103.h_ref), custom_call_target="tpu_custom_call" | custom-call | tf_op jit(solution)/shard_map/pallas_call | solution.py:277
  133.0 2.9 %rel_update0.1 = (f32[200,1408]{1,0:T(8,128)}, f32[1,1408]{1,0:T(1,128)}) custom-call(f32[200,1408]{1,0:T(8,128)} %rel_prep.1.rt_ref, f32[1,1408]{1,0:T(1,128)} %pad.4.state_ref, f32[2,16,9,8,128]{4,3,2,1,0:T(8,128)} %shard_map.104.h_ref), custom_call_target="tpu_custom_call" | custom-call | tf_op jit(solution)/shard_map/rel_update0/pallas_call | solution.py:51
  135.8 0.0 copy-start.9
  135.9 0.0 copy-start.2
  135.9 0.6 copy-done.9
  136.4 0.2 copy-done.2
  136.6 9.6 %main1.1 = (f32[200,1024]{1,0:T(8,128)}, f32[200,512]{1,0:T(8,128)}, f32[2,16,9,8,128]{4,3,2,1,0:T(8,128)}) custom-call(f32[1024,200]{1,0:T(8,128)} %get-tuple-element.28.e_ref, f32[200,1024]{1,0:T(8,128)} %get-tuple-element.26.et_ref.refs_0_, f32[200,1408]{1,0:T(8,128)} %get-tuple-element.30.rt_ref, f32[200,512]{1,0:T(8,128)} %copy-done.2, ...), custom_call_target="tpu_custom_call" | custom-call | tf_op jit(solution)/shard_map/main1/pallas_call | solution.py:51
  146.2 0.1 collective-permute-start.9
  146.3 16.5 %shard_map.105.h_ref = f32[9,8,128]{2,1,0:T(8,128)} custom-call(f32[2,16,9,8,128]{4,3,2,1,0:T(8,128)} %get-tuple-element.37.h_ref), custom_call_target="tpu_custom_call" | custom-call | tf_op jit(solution)/shard_map/pallas_call | solution.py:275
  162.8 13.0 %shard_map.106.h_ref = f32[9,8,128]{2,1,0:T(8,128)} custom-call(f32[9,8,128]{2,1,0:T(8,128)} %shard_map.105.h_ref), custom_call_target="tpu_custom_call" | custom-call | tf_op jit(solution)/shard_map/pallas_call | solution.py:276
  175.9 16.5 %shard_map.107.h_ref = f32[2,16,9,8,128]{4,3,2,1,0:T(8,128)} custom-call(f32[9,8,128]{2,1,0:T(8,128)} %shard_map.106.h_ref), custom_call_target="tpu_custom_call" | custom-call | tf_op jit(solution)/shard_map/pallas_call | solution.py:277
  192.4 3.3 %rel_update1.1 = (f32[1345,200]{1,0:T(8,128)}, f32[1,1408]{1,0:T(1,128)}) custom-call(f32[200,1408]{1,0:T(8,128)} %get-tuple-element.30.rt_ref, f32[1,1408]{1,0:T(1,128)} %get-tuple-element.36.state_ref, f32[2,16,9,8,128]{4,3,2,1,0:T(8,128)} %shard_map.107.h_ref), custom_call_target="tpu_custom_call" | custom-call | tf_op jit(solution)/shard_map/rel_update1/pallas_call | solution.py:51
  195.6 2.8 %copy.20 = f32[1345,200]{0,1:T(8,128)} copy(f32[1345,200]{1,0:T(8,128)} %get-tuple-element.42) | data formatting | bytes 2152000
  198.4 0.6 slice_reduce_fusion
  199.0 0.7 copy-done.4
  199.8 3.8 %update1.1 = (f32[1024,200]{1,0:T(8,128)}, f32[1,1024]{1,0:T(1,128)}, f32[200,1024]{1,0:T(8,128)}) custom-call(f32[200,1024]{1,0:T(8,128)} %get-tuple-element.26.et_ref.refs_0_, f32[1,1024]{1,0:T(1,128)} %get-tuple-element.27.refs_1_, f32[200,1024]{1,0:T(8,128)} %get-tuple-element.32.refs_2_, f32[200,512]{1,0:T(8,128)} %copy-done.4, ...), custom_call_target="tpu_custom_call" | custom-call | tf_op jit(solution)/shard_map/update1/pallas_call | solution.py:51
  203.6 2.4 %copy.19 = f32[1024,200]{0,1:T(8,128)} copy(f32[1024,200]{1,0:T(8,128)} %get-tuple-element.40) | data formatting | bytes 1638400
  (27 shorter events, 0.1 us)
Async XLA Ops:
  1.9 13.1 %copy-start.1 = (s32[2,3,512]{2,1,0:T(4,128)S(1)}, s32[2,3,512]{2,1,0:T(4,128)}, u32[]{:S(2)}) copy-start(s32[2,3,512]{2,1,0:T(4,128)} %copy.12.edges_ref.refs_4_) | copy-start | bytes 36868
  1.9 13.2 %copy-start.6 = (s32[2,4,1000]{2,1,0:T(4,128)S(1)}, s32[2,4,1000]{2,1,0:T(4,128)}, u32[]{:S(2)}) copy-start(s32[2,4,1000]{2,1,0:T(4,128)} %param.12) | copy-start | bytes 96004
  1.9 18.5 %copy-start.13 = (s32[2,1]{0,1:T(1,128)S(1)}, s32[2,1]{0,1:T(1,128)}, u32[]{:S(2)}) copy-start(s32[2,1]{0,1:T(1,128)} %param.13) | copy-start | bytes 28
  1.9 19.2 %copy-start = (f32[1345,200]{0,1:T(8,128)S(1)}, f32[1345,200]{0,1:T(8,128)}, u32[]{:S(2)}) copy-start(f32[1345,200]{0,1:T(8,128)} %param.9) | copy-start | bytes 3228004
  7.3 23.2 %collective-permute-start = (f32[200,512]{1,0:T(8,128)}, f32[200,512]{1,0:T(8,128)S(1)}, u32[]{:S(2)}, u32[]{:S(2)}) collective-permute-start(f32[200,512]{1,0:T(8,128)} %get-tuple-element.23), channel_id=1, source_target_pairs={{0,128},{1,129},{2,130},{3,131},{4,132},{5,133},{6,134},{7,135},{8... | collective-permute-start | bytes 1228808 | tf_op jit(solution)/shard_map/ppermute | solution.py:316
  15.1 15.5 %collective-permute-start.1 = (s32[3,512]{1,0:T(4,128)S(1)}, s32[3,512]{1,0:T(4,128)S(1)}, u32[]{:S(2)}, u32[]{:S(2)}) collective-permute-start(s32[3,512]{1,0:T(4,128)S(1)} %get-tuple-element.47), channel_id=1, source_target_pairs={{0,128},{1,129},{2,130},{3,131},{4,132},{5,133},{6,134},{7,135},{8... | collective-permute-start | bytes 18440 | tf_op jit(solution)/shard_map/ppermute | solution.py:316
  15.2 10.4 %collective-permute-start.2 = (s32[4,1000]{1,0:T(4,128)S(1)}, s32[4,1000]{1,0:T(4,128)S(1)}, u32[]{:S(2)}, u32[]{:S(2)}) collective-permute-start(s32[4,1000]{1,0:T(4,128)S(1)} %get-tuple-element.45), channel_id=1, source_target_pairs={{0,128},{1,129},{2,130},{3,131},{4,132},{5,133},{6,134},{7,135},{8... | collective-permute-start | bytes 48008 | tf_op jit(solution)/shard_map/ppermute | solution.py:316
  21.0 9.5 %collective-permute-start.3 = (s32[1]{0:T(128)}, s32[1]{0:T(128)}, u32[]{:S(2)}, u32[]{:S(2)}) collective-permute-start(s32[1]{0:T(128)} %bitcast.3), channel_id=1, source_target_pairs={{0,128},{1,129},{2,130},{3,131},{4,132},{5,133},{6,134},{7,135},{8... | collective-permute-start | bytes 20 | tf_op jit(solution)/shard_map/ppermute | solution.py:316
  25.6 0.6 copy-start.8
  30.6 0.6 copy-start.10
  30.6 0.8 copy-start.3
  40.9 33.8 %copy-start.11 = (f32[1345]{0:T(1024)S(1)}, f32[1345]{0:T(1024)}, u32[]{:S(2)}) copy-start(f32[1345]{0:T(1024)} %param.10) | copy-start | bytes 16144
  40.9 11.1 %collective-permute-start.4 = (f32[200,512]{1,0:T(8,128)}, f32[200,512]{1,0:T(8,128)S(1)}, u32[]{:S(2)}, u32[]{:S(2)}) collective-permute-start(f32[200,512]{1,0:T(8,128)} %get-tuple-element.25), channel_id=1, source_target_pairs={{0,128},{1,129},{2,130},{3,131},{4,132},{5,133},{6,134},{7,135},{8... | collective-permute-start | bytes 1228808 | tf_op jit(solution)/shard_map/ppermute | solution.py:316
  52.0 0.8 copy-start.5
  57.1 78.7 %collective-permute-start.5 = (f32[200,512]{1,0:T(8,128)}, f32[200,512]{1,0:T(8,128)S(1)}, u32[]{:S(2)}, u32[]{:S(2)}) collective-permute-start(f32[200,512]{1,0:T(8,128)} %get-tuple-element.31), channel_id=1, source_target_pairs={{0,1},{1,0},{2,3},{3,2},{4,5},{5,4},{6,7},{7,6},{8,9},{9,8},{10,11... | collective-permute-start | bytes 1228808 | tf_op jit(solution)/shard_map/ppermute | solution.py:316
  74.2 1.6 collective-permute-start.7
  74.2 61.6 %collective-permute-start.6 = (s32[3,512]{1,0:T(4,128)S(1)}, s32[3,512]{1,0:T(4,128)S(1)}, u32[]{:S(2)}, u32[]{:S(2)}) collective-permute-start(s32[3,512]{1,0:T(4,128)S(1)} %get-tuple-element.46), channel_id=1, source_target_pairs={{0,1},{1,0},{2,3},{3,2},{4,5},{5,4},{6,7},{7,6},{8,9},{9,8},{10,11... | collective-permute-start | bytes 18440 | tf_op jit(solution)/shard_map/ppermute | solution.py:316
  74.7 61.1 %collective-permute-start.8 = (s32[1]{0:T(128)}, s32[1]{0:T(128)}, u32[]{:S(2)}, u32[]{:S(2)}) collective-permute-start(s32[1]{0:T(128)} %bitcast.6), channel_id=1, source_target_pairs={{0,1},{1,0},{2,3},{3,2},{4,5},{5,4},{6,7},{7,6},{8,9},{9,8},{10,11... | collective-permute-start | bytes 20 | tf_op jit(solution)/shard_map/ppermute | solution.py:316
  75.8 0.6 copy-start.7
  135.8 0.6 copy-start.9
  135.9 0.8 copy-start.2
  146.2 52.9 %collective-permute-start.9 = (f32[200,512]{1,0:T(8,128)}, f32[200,512]{1,0:T(8,128)S(1)}, u32[]{:S(2)}, u32[]{:S(2)}) collective-permute-start(f32[200,512]{1,0:T(8,128)} %get-tuple-element.33), channel_id=1, source_target_pairs={{0,1},{1,0},{2,3},{3,2},{4,5},{5,4},{6,7},{7,6},{8,9},{9,8},{10,11... | collective-permute-start | bytes 1228808 | tf_op jit(solution)/shard_map/ppermute | solution.py:316
  195.6 2.8 %copy-start.12 = (f32[1,1408]{1,0:T(1,128)S(1)}, f32[1,1408]{1,0:T(1,128)}, u32[]{:S(2)}) copy-start(f32[1,1408]{1,0:T(1,128)} %get-tuple-element.39) | copy-start | bytes 16900
  199.0 0.7 copy-start.4

commit v4 on v3

v4 whole, which is shorter than its diff:
```python
import functools

import jax
import jax.numpy as jnp
from jax import lax
from jax.experimental import pallas as pl
from jax.experimental.pallas import tpu as pltpu
from jax.sharding import PartitionSpec as P

RATE = 0.2
F32 = jnp.float32
BF16 = jnp.bfloat16
VMEM = pl.BlockSpec(memory_space=pltpu.VMEM)
SMEM = pl.BlockSpec(memory_space=pltpu.SMEM)
NN = (((1,), (0,)), ((), ()))
NT = (((1,), (1,)), ((), ()))
LANES = 128
SUBLANES = 8
ZS, XS, YS, CORES = 8, 4, 4, 2
PLANE = XS * YS
MESH = pl.DeviceIdType.MESH


def split(value):
    high = value.astype(BF16)
    return high, (value - high.astype(F32)).astype(BF16)


def dot(left, right, dims=NN):
    return lax.dot_general(left, right, dims, preferred_element_type=F32)


def dot3(left, right, dims=NN):
    return (
        dot(left[0], right[0], dims) + dot(left[0], right[1], dims) + dot(left[1], right[0], dims)
    )


def dot_exact(left, right, dims=NN):
    return dot(left[0], right, dims) + dot(left[1], right, dims)


def spots(ids, count):
    rows = lax.broadcasted_iota(jnp.int32, (count, ids.shape[1]), 0)
    return jnp.where(rows == ids, 1.0, 0.0).astype(BF16)


def call(kernel, outs, args, scratch=(), name=None, collective=None):
    params = None
    if collective is not None:
        params = pltpu.CompilerParams(collective_id=collective, has_side_effects=True)
    return pl.pallas_call(
        kernel,
        out_shape=[jax.ShapeDtypeStruct(*out) for out in outs],
        in_specs=[VMEM] * len(args),
        out_specs=[VMEM] * len(outs),
        scratch_shapes=list(scratch),
        compiler_params=params,
        name=name,
    )(*args)


def pairs(*counts):
    return [pltpu.SemaphoreType.DMA((count,)) for count in counts for _ in range(2)]


def prep_kernel(e_ref, edges_ref, neg_ref, counts_ref, et_ref, st_ref, meta_ref, wide):
    rows, dim = e_ref.shape
    rounds, kinds, slots = edges_ref.shape
    blocks, draws = neg_ref.shape[1:]
    wide[...] = jnp.zeros_like(wide)
    wide[:, :dim] = e_ref[...]
    et_ref[...] = wide[...].T[:dim]
    source = edges_ref[0, 0:1, :]
    st_ref[...] = dot_exact(split(et_ref[...]), spots(source, rows))
    meta_ref[...] = jnp.full(meta_ref.shape, -1, jnp.int32)
    for r in range(rounds):
        meta_ref[r, 0:kinds, 0:slots] = edges_ref[r]
        meta_ref[r, kinds : kinds + 1, :] = jnp.broadcast_to(counts_ref[r : r + 1, :], (1, rows))
        meta_ref[r, kinds + 1 : kinds + 1 + blocks, 0:draws] = neg_ref[r]


def hist(meta_ref, c_ref, blocks, draws):
    ones = jnp.ones((meta_ref.shape[1], LANES), BF16)
    for b in range(blocks):
        hits = spots(meta_ref[4 + b : 5 + b, :], c_ref.shape[0])
        c_ref[:, b * LANES : (b + 1) * LANES] = dot(hits, ones) * (1.0 / draws)


def exchange_kernel(
    draws, st_ref, meta_ref, r_ref, rows_ref, meta0_ref, meta1_ref, rt_ref, c0_ref, c1_ref, wide, ss, rs
):
    c, y, x, z = places_of()
    far, near = device((z + ZS // 2) % ZS, x, y, c), other_core()
    meet([far, near])
    sends = [
        remote(meta_ref.at[0], meta0_ref, (ss, rs), 0, far),
        remote(meta_ref.at[1], meta1_ref, (ss, rs), 1, near),
        remote(st_ref, rows_ref, (ss, rs), 2, far),
    ]
    for one in sends:
        one.start()
    rels, dim = r_ref.shape
    blocks = c0_ref.shape[1] // LANES
    wide[...] = jnp.zeros_like(wide)
    wide[:rels, :dim] = r_ref[...]
    rt_ref[...] = wide[...].T[:dim]
    sends[1].wait_recv()
    hist(meta1_ref, c1_ref, blocks, draws)
    sends[0].wait_recv()
    hist(meta0_ref, c0_ref, blocks, draws)
    sends[2].wait_recv()
    for one in sends:
        one.wait_send()


def main_kernel(
    e_ref, et_ref, rt_ref, st_ref, meta_ref, c_ref, gt_ref, gs_ref, h_ref, q, tmp
):
    rows, dim = e_ref.shape
    half = dim // 2
    wide = st_ref.shape[1]
    rels = rt_ref.shape[1]
    relation = meta_ref[1:2, 0:wide]
    live = lax.broadcasted_iota(jnp.int32, (1, wide), 1) < meta_ref[3:4, 0:wide]
    target = jnp.where(live, meta_ref[2:3, 0:wide], -1)
    alive = live.astype(F32)
    rel_spots = spots(relation, rels)
    tmp[...] = dot_exact(split(rt_ref[...]), rel_spots)
    s_re, s_im = st_ref[0:half, :], st_ref[half:dim, :]
    w_re, w_im = tmp[0:half, :], tmp[half:dim, :]
    q[0:half, :] = s_re * w_re - s_im * w_im
    q[half:dim, :] = s_re * w_im + s_im * w_re
    q_parts = split(q[...])
    up = jnp.zeros((dim, wide), F32)
    step = 256
    for j in range(0, rows, step):
        scores = dot3(split(e_ref[j : j + step, :]), q_parts)
        sig = 0.5 * jnp.tanh(0.5 * scores) + 0.5
        number = lax.broadcasted_iota(jnp.int32, (step, wide), 0) + j
        mark = jnp.where(number == target, 1.0, 0.0)
        weight = split(sig * (c_ref[j : j + step, :] * alive + mark) - mark)
        up = up + dot3(split(et_ref[:, j : j + step]), weight)
        gt_ref[:, j : j + step] = dot3(q_parts, weight, NT)
    q[...] = up
    u_re, u_im = q[0:half, :], q[half:dim, :]
    gs_ref[0:half, :] = u_re * w_re + u_im * w_im
    gs_ref[half:dim, :] = u_im * w_re - u_re * w_im
    tmp[0:half, :] = u_re * s_re + u_im * s_im
    tmp[half:dim, :] = u_im * s_re - u_re * s_im
    total = dot_exact(split(tmp[...]), rel_spots, NT)
    places, tiles = tile_places(h_ref.shape, total.shape)
    for place, (row, lane) in zip(places, tiles):
        h_ref[place] = total[row : row + SUBLANES, lane : lane + LANES]
    for place in places[len(tiles) :]:
        h_ref[place] = jnp.zeros((SUBLANES, LANES), F32)


def second_main_kernel(
    e_ref, et_ref, rt_ref, rel_state_ref, sum_ref, st_ref, meta_ref, c_ref,
    gt_ref, gs_ref, h_ref, rt_out, rel_state_out, q, tmp, whole,
):
    join_tiles(sum_ref, whole)
    rt_out[...], rel_state_out[...] = stepped(rt_ref[...], rel_state_ref[...], whole[...])
    main_kernel(e_ref, et_ref, rt_out, st_ref, meta_ref, c_ref, gt_ref, gs_ref, h_ref, q, tmp)


def tile_places(shape, flat):
    places = [(c, k, t) for c in range(shape[0]) for k in range(shape[1]) for t in range(shape[2])]
    tiles = [(r, l) for r in range(0, flat[0], SUBLANES) for l in range(0, flat[1], LANES)]
    return places, tiles


def join_tiles(h_ref, whole):
    places, tiles = tile_places(h_ref.shape, whole.shape)
    for place, (row, lane) in zip(places, tiles):
        whole[row : row + SUBLANES, lane : lane + LANES] = h_ref[place]


def places_of():
    me = lax.axis_index("dom")
    return me % CORES, me // CORES % YS, me // (CORES * YS) % XS, me // (CORES * YS * XS)


def device(z, x, y, c):
    return (((z * XS + x) * YS + y) * CORES + c,)


def remote(src, dst, sems, k, to):
    return pltpu.make_async_remote_copy(
        src_ref=src,
        dst_ref=dst,
        send_sem=sems[0].at[k],
        recv_sem=sems[1].at[k],
        device_id=to,
        device_id_type=MESH,
    )


def meet(peers):
    barrier = pltpu.get_barrier_semaphore()
    for peer in peers:
        pl.semaphore_signal(barrier, inc=1, device_id=peer, device_id_type=MESH)
    pl.semaphore_wait(barrier, len(peers))


def other_core():
    c, y, x, z = places_of()
    return device(z, x, y, 1 - c)


def in_plane():
    c, y, x, z = places_of()
    plane = []
    for k in range(PLANE):
        px, py = (x + k // YS) % XS, (y + k % YS) % YS
        fx, fy = (x + XS - k // YS) % XS, (y + YS - k % YS) % YS
        plane.append((device(z, px, py, c), px * YS + py, fx * YS + fy))
    return plane


def in_column():
    c, y, x, z = places_of()
    return [device((z + k) % ZS, x, y, c) for k in range(ZS)]


def spread_sum(h_ref, out_ref, *more, beside=None):
    s0, r0, s1, r1 = more[-4:]
    acc, got0, got1 = (more[i * PLANE : (i + 1) * PLANE] for i in range(3))
    other = other_core()
    plane = in_plane()
    c = places_of()[0]
    meet([other] + [p[0] for p in plane[1:]])
    order = range(PLANE - 1, -1, -1)
    first = [remote(h_ref.at[1 - c, plane[k][1]], got0[k], (s0, r0), k, other) for k in range(PLANE)]
    second = [None] + [remote(acc[k], got1[k], (s1, r1), k, plane[k][0]) for k in range(1, PLANE)]
    for k in order:
        first[k].start()
    if beside is not None:
        beside.start()
    for k in order:
        first[k].wait_recv()
        acc[k][...] = h_ref[c, plane[k][1]] + got0[k][...]
        if k < PLANE - 1:
            second[k + 1].start()
    total = acc[0][...]
    for k in order[:-1]:
        second[k].wait_recv()
        total = total + got1[k][...]
    out_ref[...] = total
    for one in first + second[1:]:
        one.wait_send()
    if beside is not None:
        beside.wait()


def spread_sum_kernel(h_ref, out_ref, *more):
    spread_sum(h_ref, out_ref, *more)


def second_spread_sum_kernel(h_ref, gs_ref, out_ref, gs_out, sx, rx, *more):
    spread_sum(h_ref, out_ref, *more, beside=remote(gs_ref, gs_out, (sx, rx), 0, other_core()))


def column_sum_kernel(h_ref, out_ref, level, *more, beside=None):
    got, sems = more[:-2], more[-2:]
    column = in_column()
    z = places_of()[3]
    meet(column[1:])
    sends = [remote(h_ref, got[k], sems, k, column[k]) for k in range(1, ZS)]
    for k in (4, 3, 5, 2, 6, 1, 7):
        sends[k - 1].start()
    level[z] = h_ref[...]
    if beside is not None:
        beside()
    for k in range(1, ZS):
        sends[k - 1].wait_recv()
        level[(z + ZS - k) % ZS] = got[k][...]
    total = level[0]
    for k in range(1, ZS):
        total = total + level[k]
    out_ref[...] = total
    for one in sends:
        one.wait_send()


def last_column_sum_kernel(
    h_ref, et_ref, state_ref, gt_ref, gs_ref, meta_ref, out_ref, e_out, state_out, wide, *more
):
    def beside():
        after = entity_step(1, et_ref, state_ref, gt_ref, gs_ref, meta_ref, state_out)
        e_out[...] = turned(after, wide)

    column_sum_kernel(h_ref, out_ref, *more, beside=beside)


def spread_share(h_ref, out_ref, *more, beside=None):
    s3, r3, s4, r4 = more[-4:]
    got3, got4 = (more[i * PLANE : (i + 1) * PLANE] for i in range(2))
    other = other_core()
    plane = in_plane()
    c = places_of()[0]
    meet([other] + [p[0] for p in plane[1:]])
    order = range(PLANE - 1, 0, -1)
    fourth = [None] + [remote(h_ref, got3[k], (s3, r3), k, plane[k][0]) for k in range(1, PLANE)]
    fifth = [remote(got3[k] if k else h_ref, got4[k], (s4, r4), k, other) for k in range(PLANE)]
    for k in order:
        fourth[k].start()
    fifth[0].start()
    extra = beside() if beside is not None else None
    out_ref[c, plane[0][1]] = h_ref[...]
    for k in order:
        fourth[k].wait_recv()
        fifth[k].start()
        out_ref[c, plane[k][2]] = got3[k][...]
    for k in [0, *order]:
        fifth[k].wait_recv()
        out_ref[1 - c, plane[k][2]] = got4[k][...]
    for one in fourth[1:] + fifth:
        one.wait_send()
    if extra is not None:
        extra.wait()


def spread_share_kernel(
    h_ref, et_ref, state_ref, gt_ref, gs_ref, meta_ref,
    out_ref, e_out, state_out, et_out, rows_out, mine, wide, sx, rx, *more,
):
    def beside():
        after = entity_step(0, et_ref, state_ref, gt_ref, gs_ref, meta_ref, state_out)
        source = meta_ref[1, 0:1, 0 : mine.shape[1]]
        mine[...] = dot_exact(split(after), spots(source, after.shape[1]))
        send = remote(mine, rows_out, (sx, rx), 0, other_core())
        et_out[...] = after
        e_out[...] = turned(after, wide)
        send.start()
        return send

    spread_share(h_ref, out_ref, *more, beside=beside)


def last_spread_share_kernel(
    h_ref, rt_ref, rel_state_ref, r_out, rel_state_out, sums, whole, wide, *more
):
    spread_share(h_ref, sums, *more)
    join_tiles(sums, whole)
    after, rel_state_out[...] = stepped(rt_ref[...], rel_state_ref[...], whole[...])
    r_out[...] = turned(after, wide)[: r_out.shape[0]]


def turned(value, wide):
    dim = value.shape[0]
    wide[0:dim, :] = value
    wide[dim:, :] = jnp.zeros((wide.shape[0] - dim, wide.shape[1]), F32)
    return wide[...].T[:, :dim]


def entity_step(number, et_ref, state_ref, gt_ref, gs_ref, meta_ref, state_out):
    source = spots(meta_ref[number, 0:1, 0 : gs_ref.shape[1]], et_ref.shape[1])
    grad = gt_ref[...] + dot_exact(split(gs_ref[...]), source, NT)
    after, state_out[...] = stepped(et_ref[...], state_ref[...], grad)
    return after


def stepped(param, state, grad):
    new_state = state + jnp.sum(grad * grad, axis=0, keepdims=True) * (1.0 / grad.shape[0])
    return param - RATE * grad / jnp.sqrt(new_state), new_state


def swapped(value, apart):
    count = lax.axis_size("dom")
    return lax.ppermute(value, "dom", [(low, low ^ (1 << apart)) for low in range(count)])


def body(entities, entity_state, relations, relation_state, edges, negatives, counts):
    rows, dim = entities.shape
    rels = relations.shape[0]
    rels_pad = -(-rels // LANES) * LANES
    slots = edges.shape[2]
    blocks, draws = negatives.shape[1:]
    dim_pad = -(-dim // LANES) * LANES
    tiles = dim // SUBLANES * (rels_pad // LANES)
    piece = (-(-tiles // (CORES * PLANE)), SUBLANES, LANES)
    pieces = (CORES, PLANE, *piece)
    one = pltpu.VMEM(piece, F32)

    def array(*shape):
        return (shape, F32)

    def space(*shape):
        return pltpu.VMEM(shape, F32)

    meta_shape = (2, 4 + blocks, rows)
    et, st, meta = call(
        prep_kernel,
        [array(dim, rows), array(dim, slots), (meta_shape, jnp.int32)],
        [entities, edges, negatives, counts],
        [space(rows, dim_pad)],
        name="prep",
    )
    state = entity_state.reshape(1, rows)
    rel_state = jnp.pad(relation_state.reshape(1, rels), ((0, 0), (0, rels_pad - rels)), constant_values=1.0)
    their_rows, meta0, meta1, rt, c0, c1 = call(
        functools.partial(exchange_kernel, draws),
        [
            array(dim, slots),
            (meta_shape[1:], jnp.int32),
            (meta_shape[1:], jnp.int32),
            array(dim, rels_pad),
            array(rows, slots),
            array(rows, slots),
        ],
        [st, meta, relations],
        [space(rels_pad, dim_pad), *pairs(3)],
        name="exchange",
        collective=0,
    )
    gt, gs, h = call(
        main_kernel,
        [array(dim, rows), array(dim, slots), (pieces, F32)],
        [entities, et, rt, their_rows, meta0, c0],
        [space(dim, slots), space(dim, slots)],
        name="main",
    )
    levels = lax.axis_size("dom").bit_length() - 1
    gs = swapped(gs, levels - 1)
    (h,) = call(
        spread_sum_kernel, [(piece, F32)], [h], [one] * (3 * PLANE) + pairs(PLANE, PLANE), name="spread_sum", collective=1
    )
    (h,) = call(
        column_sum_kernel, [(piece, F32)], [h], [space(ZS, *piece)] + [one] * ZS + pairs(ZS), name="column_sum", collective=2
    )
    h, table, state, et, their_rows = call(
        spread_share_kernel,
        [(pieces, F32), array(rows, dim), array(1, rows), array(dim, rows), array(dim, slots)],
        [h, et, state, gt, gs, meta],
        [space(dim, slots), space(dim_pad, rows), *pairs(1)] + [one] * (2 * PLANE) + pairs(PLANE, PLANE),
        name="spread_share",
        collective=3,
    )
    gt, gs, h, rt, rel_state = call(
        second_main_kernel,
        [array(dim, rows), array(dim, slots), (pieces, F32), array(dim, rels_pad), array(1, rels_pad)],
        [table, et, rt, rel_state, h, their_rows, meta1, c1],
        [space(dim, slots), space(dim, slots), space(dim, rels_pad)],
        name="second_main",
    )
    h, gs = call(
        second_spread_sum_kernel,
        [(piece, F32), array(dim, slots)],
        [h, gs],
        pairs(1) + [one] * (3 * PLANE) + pairs(PLANE, PLANE),
        name="second_spread_sum",
        collective=4,
    )
    h, table, state = call(
        last_column_sum_kernel,
        [(piece, F32), array(rows, dim), array(1, rows)],
        [h, et, state, gt, gs, meta],
        [space(dim_pad, rows), space(ZS, *piece)] + [one] * ZS + pairs(ZS),
        name="last_column_sum",
        collective=5,
    )
    relations, rel_state = call(
        last_spread_share_kernel,
        [array(rels, dim), array(1, rels_pad)],
        [h, rt, rel_state],
        [space(*pieces), space(dim, rels_pad), space(dim_pad, rels_pad)] + [one] * (2 * PLANE) + pairs(PLANE, PLANE),
        name="last_spread_share",
        collective=6,
    )
    return table, state.reshape(rows), relations, rel_state[0, :rels]


def solution(mesh):
    return jax.shard_map(
        body,
        mesh=mesh,
        in_specs=(
            P("dom", None),
            P("dom"),
            P(),
            P(),
            P(None, None, "dom"),
            P(None, "dom", None),
            P(None, "dom"),
        ),
        out_specs=(P("dom", None), P("dom"), P(), P()),
        check_vma=False,
    )
```

time: 207 us -> 171 us (0.83)
  starting transfers between devices: 36.5 us -> 5.27 us
  waiting for transfers between devices: 6.11 us -> 0.01 us
  Pallas kernels: 146 us -> 150 us
  local copies, waits for them, and re-layouts: 16.6 us -> 14.5 us
    pallas_call x10, Pallas kernels: 47.9 us -> 150 us  [call(): pl.pallas_call(kernel, out_shape=[jax.ShapeDtypeStruct(*out) for out in o...]
    pallas_call x6 -> x0, Pallas kernels: 98.2 us -> none  [the longest x2 34.9 us: reduced(): pl.pallas_call(spread_sum_kernel, **settings(piece, [one] * (3 * PLANE),...]
    ppermute x10 -> x1, starting transfers between devices: 36.5 us -> 5.27 us  [swapped(): lax.ppermute(value, 'dom', [(low, low ^ 1 << apart) for low in range(coun...]
    ppermute x10 -> x1, waiting for transfers between devices: 6.11 us -> 0.01 us  [swapped(): lax.ppermute(value, 'dom', [(low, low ^ 1 << apart) for low in range(coun...]
    unnamed x33 -> x17, local copies, waits for them, and re-layouts: 14.8 us -> 13.3 us
  transfers between devices with their start and end apart: 10 -> 1, of which waited for: 3 -> 0; matrix products, arithmetic and copies ran while one was open for 3% -> 0% of each run, Pallas kernels for 56% -> 21%
where the time goes in v4:
time: 171 us; the launch traced here: 170 us
  Pallas kernels  150 us (88%)
  local copies, waits for them, and re-layouts  14.5 us (8%)
  starting transfers between devices  5.27 us (3%)
    pallas_call x10, Pallas kernels, call(): pl.pallas_call(kernel, out_shape=[jax.ShapeDtypeStruct(*out) for out in o...  150 us
    unnamed x17, local copies, waits for them, and re-layouts  13.3 us
    ppermute x1, starting transfers between devices, swapped(): lax.ppermute(value, 'dom', [(low, low ^ 1 << apart) for low in range(coun...  5.27 us
  transfers between devices with their start and end apart: 1, of which 0 were waited for; matrix products, arithmetic and copies ran while one was open for 0% of the time, Pallas kernels for 21%

profile of v4, /device:TPU:1, one launch (start us, length us, event | category | flops | bytes accessed | tf_op | source)
XLA Modules:
  0.0 170.0 jit_solution(9567857758659004830)
XLA Ops:
  0.6 0.0 copy-start
  0.6 1.4 copy.13.counts_ref
  2.0 1.3 copy.12.edges_ref
  3.3 2.5 %copy.15.e_ref = f32[1024,200]{1,0:T(8,128)} copy(f32[1024,200]{0,1:T(8,128)} %param.7) | data formatting | bytes 1638400 | tf_op args[0]
  5.8 0.0 copy-done
  5.8 1.6 copy.14.r_ref
  7.4 2.8 %prep.1 = (f32[200,1024]{1,0:T(8,128)}, f32[200,512]{1,0:T(8,128)}, s32[2,8,1024]{2,1,0:T(8,128)}) custom-call(f32[1024,200]{1,0:T(8,128)} %copy.15.e_ref, s32[2,3,512]{2,1,0:T(4,128)} %copy.12.edges_ref, s32[2,4,1000]{2,1,0:T(4,128)} %neg_ref.1, s32[2,1]{1,0:T(2,128)} %copy.13.counts_ref), custom_call_target="tpu_custom_call" | custom-call | tf_op jit(solution)/shard_map/prep/pallas_call | solution.py:52
  10.2 25.6 %exchange.1 = (f32[200,512]{1,0:T(8,128)}, s32[8,1024]{1,0:T(8,128)}, s32[8,1024]{1,0:T(8,128)}, f32[200,1408]{1,0:T(8,128)}, f32[1024,512]{1,0:T(8,128)}, /*index=5*/f32[1024,512]{1,0:T(8,128)}) custom-call(f32[200,512]{1,0:T(8,128)} %get-tuple-element.34.st_ref, s32[2,8,1024]{2,1,0:T(8,128)} %get-tuple-element.35.meta_ref, f32[1345,200]{1,0:T(8,128)} %copy.14.r_ref), custom_call_target="tpu_custom_call" | custom-call | tf_op jit(solution)/shard_map/exchange/pallas_call | solution.py:52
  35.8 0.0 copy-start.2
  35.9 8.9 %main.1 = (f32[200,1024]{1,0:T(8,128)}, f32[200,512]{1,0:T(8,128)}, f32[2,16,9,8,128]{4,3,2,1,0:T(8,128)}) custom-call(f32[1024,200]{1,0:T(8,128)} %copy.15.e_ref, f32[200,1024]{1,0:T(8,128)} %get-tuple-element.33.et_ref, f32[200,1408]{1,0:T(8,128)} %get-tuple-element.36.rt_ref, f32[200,512]{1,0:T(8,128)} %get-tuple-element.37.st_ref, ...), custom_call_target="tpu_custom_call" | custom-call | tf_op jit(solution)/shard_map/main/pallas_call | solution.py:52
  44.8 5.3 %collective-permute-start = (f32[200,512]{1,0:T(8,128)}, f32[200,512]{1,0:T(8,128)S(1)}, u32[]{:S(2)}, u32[]{:S(2)}) collective-permute-start(f32[200,512]{1,0:T(8,128)} %get-tuple-element.42), channel_id=1, source_target_pairs={{0,128},{1,129},{2,130},{3,131},{4,132},{5,133},{6,134},{7,135},{8... | collective-permute-start | bytes 1228808 | tf_op jit(solution)/shard_map/ppermute | solution.py:372
  50.0 0.0 copy-done.2
  50.0 18.4 %spread_sum.1.h_ref = f32[9,8,128]{2,1,0:T(8,128)} custom-call(f32[2,16,9,8,128]{4,3,2,1,0:T(8,128)} %get-tuple-element.40.h_ref), custom_call_target="tpu_custom_call" | custom-call | tf_op jit(solution)/shard_map/spread_sum/pallas_call | solution.py:52
  68.4 17.5 %column_sum.1.h_ref = f32[9,8,128]{2,1,0:T(8,128)} custom-call(f32[9,8,128]{2,1,0:T(8,128)} %spread_sum.1.h_ref), custom_call_target="tpu_custom_call" | custom-call | tf_op jit(solution)/shard_map/column_sum/pallas_call | solution.py:52
  85.9 0.6 pad.4.rel_state_ref
  86.5 0.0 collective-permute-done.gs_ref
  86.5 0.0 copy-start.1
  86.5 0.8 copy-done.1
  87.3 18.3 %spread_share.1 = (f32[2,16,9,8,128]{4,3,2,1,0:T(8,128)}, f32[1024,200]{1,0:T(8,128)}, f32[1,1024]{1,0:T(1,128)}, f32[200,1024]{1,0:T(8,128)}, f32[200,512]{1,0:T(8,128)}) custom-call(f32[9,8,128]{2,1,0:T(8,128)} %column_sum.1.h_ref, f32[200,1024]{1,0:T(8,128)} %get-tuple-element.33.et_ref, f32[1,1024]{1,0:T(1,128)} %bitcast.2, ...), custom_call_target="tpu_custom_call" | custom-call | tf_op jit(solution)/shard_map/spread_share/pallas_call | solution.py:52
  105.6 9.7 %second_main.1 = (f32[200,1024]{1,0:T(8,128)}, f32[200,512]{1,0:T(8,128)}, f32[2,16,9,8,128]{4,3,2,1,0:T(8,128)}, f32[200,1408]{1,0:T(8,128)}, f32[1,1408]{1,0:T(1,128)}) custom-call(f32[1024,200]{1,0:T(8,128)} %get-tuple-element.43.e_ref, f32[200,1024]{1,0:T(8,128)} %get-tuple-element.44.et_ref, f32[200,1408]{1,0:T(8,128)} %get-tuple-element.36.rt_ref, ...), custom_call_target="tpu_custom_call" | custom-call | tf_op jit(solution)/shard_map/second_main/pallas_call | solution.py:52
  115.3 16.6 %second_spread_sum.1 = (f32[9,8,128]{2,1,0:T(8,128)}, f32[200,512]{1,0:T(8,128)}) custom-call(f32[2,16,9,8,128]{4,3,2,1,0:T(8,128)} %get-tuple-element.49.h_ref, f32[200,512]{1,0:T(8,128)} %get-tuple-element.50.gs_ref), custom_call_target="tpu_custom_call" | custom-call | tf_op jit(solution)/shard_map/second_spread_sum/pallas_call | solution.py:52
  131.9 14.3 %last_column_sum.1 = (f32[9,8,128]{2,1,0:T(8,128)}, f32[1024,200]{1,0:T(8,128)}, f32[1,1024]{1,0:T(1,128)}) custom-call(f32[9,8,128]{2,1,0:T(8,128)} %get-tuple-element.51.h_ref, f32[200,1024]{1,0:T(8,128)} %get-tuple-element.44.et_ref, f32[1,1024]{1,0:T(1,128)} %get-tuple-element.52.state_ref, f32[200,1024]{1,0:T(8,128)} %get-tuple-element.53.gt_ref, ...), custom_call_target="tpu_custom_call" | custom-call | tf_op jit(solution)/shard_map/last_column_sum/pallas_call | solution.py:52
  146.2 2.4 %copy.16 = f32[1024,200]{0,1:T(8,128)} copy(f32[1024,200]{1,0:T(8,128)} %get-tuple-element.62) | data formatting | bytes 1638400
  148.6 17.4 %last_spread_share.1 = (f32[1345,200]{1,0:T(8,128)}, f32[1,1408]{1,0:T(1,128)}) custom-call(f32[9,8,128]{2,1,0:T(8,128)} %get-tuple-element.57.h_ref, f32[200,1408]{1,0:T(8,128)} %get-tuple-element.58.rt_ref, f32[1,1408]{1,0:T(1,128)} %get-tuple-element.59.rel_state_ref), custom_call_target="tpu_custom_call" | custom-call | tf_op jit(solution)/shard_map/last_spread_share/pallas_call | solution.py:52
  166.0 0.0 copy-start.3
  166.0 0.0 copy-start.4
  166.0 2.8 %copy.17 = f32[1345,200]{0,1:T(8,128)} copy(f32[1345,200]{1,0:T(8,128)} %get-tuple-element.64) | data formatting | bytes 2152000
  168.8 0.0 copy-done.3
  168.8 0.6 slice_reduce_fusion
  169.4 0.0 copy-done.4
  169.4 0.6 copy.19
  (1 shorter events, 0.0 us)
Async XLA Ops:
  0.6 5.2 %copy-start = (f32[1345,200]{0,1:T(8,128)S(1)}, f32[1345,200]{0,1:T(8,128)}, u32[]{:S(2)}) copy-start(f32[1345,200]{0,1:T(8,128)} %param.9) | copy-start | bytes 3228004
  35.8 14.2 %copy-start.2 = (f32[1345]{0:T(1024)S(1)}, f32[1345]{0:T(1024)}, u32[]{:S(2)}) copy-start(f32[1345]{0:T(1024)} %param.10) | copy-start | bytes 16144
  44.8 41.7 %collective-permute-start = (f32[200,512]{1,0:T(8,128)}, f32[200,512]{1,0:T(8,128)S(1)}, u32[]{:S(2)}, u32[]{:S(2)}) collective-permute-start(f32[200,512]{1,0:T(8,128)} %get-tuple-element.42), channel_id=1, source_target_pairs={{0,128},{1,129},{2,130},{3,131},{4,132},{5,133},{6,134},{7,135},{8... | collective-permute-start | bytes 1228808 | tf_op jit(solution)/shard_map/ppermute | solution.py:372
  86.5 0.8 copy-start.1
  166.0 2.8 %copy-start.3 = (f32[1,1408]{1,0:T(1,128)S(1)}, f32[1,1408]{1,0:T(1,128)}, u32[]{:S(2)}) copy-start(f32[1,1408]{1,0:T(1,128)} %get-tuple-element.61) | copy-start | bytes 16900
  166.0 3.4 %copy-start.4 = (f32[1,1024]{1,0:T(1,128)S(1)}, f32[1,1024]{1,0:T(1,128)}, u32[]{:S(2)}) copy-start(f32[1,1024]{1,0:T(1,128)} %get-tuple-element.56) | copy-start | bytes 12292

commit v5 on v4

--- a/solution.py
+++ b/solution.py
@@ -224,13 +224,13 @@
     return [device((z + k) % ZS, x, y, c) for k in range(ZS)]
 
 
-def spread_sum(h_ref, out_ref, *more, beside=None):
+def spread_sum(h_ref, out_ref, *more, beside=None, also=()):
     s0, r0, s1, r1 = more[-4:]
     acc, got0, got1 = (more[i * PLANE : (i + 1) * PLANE] for i in range(3))
     other = other_core()
     plane = in_plane()
     c = places_of()[0]
-    meet([other] + [p[0] for p in plane[1:]])
+    meet([other, *(p[0] for p in plane[1:]), *also])
     order = range(PLANE - 1, -1, -1)
     first = [remote(h_ref.at[1 - c, plane[k][1]], got0[k], (s0, r0), k, other) for k in range(PLANE)]
     second = [None] + [remote(acc[k], got1[k], (s1, r1), k, plane[k][0]) for k in range(1, PLANE)]
@@ -281,6 +281,27 @@
         total = total + level[k]
     out_ref[...] = total
     for one in sends:
+        one.wait_send()
+
+
+def spread_column_kernel(h_ref, out_ref, level, part, *more):
+    s2, r2, *more = more
+    got2, more = more[:ZS], more[ZS:]
+    c, y, x, z = places_of()
+    column = in_column()
+    spread_sum(h_ref, part, *more, also=column[1:])
+    third = [None] + [remote(part, got2[k], (s2, r2), k, column[k]) for k in range(1, ZS)]
+    for k in (4, 3, 5, 2, 6, 1, 7):
+        third[k].start()
+    level[z] = part[...]
+    for k in range(1, ZS):
+        third[k].wait_recv()
+        level[(z + ZS - k) % ZS] = got2[k][...]
+    total = level[0]
+    for k in range(1, ZS):
+        total = total + level[k]
+    out_ref[...] = total
+    for one in third[1:]:
         one.wait_send()
 
 
@@ -425,10 +446,12 @@
     levels = lax.axis_size("dom").bit_length() - 1
     gs = swapped(gs, levels - 1)
     (h,) = call(
-        spread_sum_kernel, [(piece, F32)], [h], [one] * (3 * PLANE) + pairs(PLANE, PLANE), name="spread_sum", collective=1
-    )
-    (h,) = call(
-        column_sum_kernel, [(piece, F32)], [h], [space(ZS, *piece)] + [one] * ZS + pairs(ZS), name="column_sum", collective=2
+        spread_column_kernel,
+        [(piece, F32)],
+        [h],
+        [space(ZS, *piece), one, *pairs(ZS)] + [one] * (ZS + 3 * PLANE) + pairs(PLANE, PLANE),
+        name="spread_column",
+        collective=1,
     )
     h, table, state, et, their_rows = call(
         spread_share_kernel,

time: 171 us -> 167 us (0.977)
  Pallas kernels: 150 us -> 146 us
    pallas_call x10 -> x9, Pallas kernels: 150 us -> 146 us  [call(): pl.pallas_call(kernel, out_shape=[jax.ShapeDtypeStruct(*out) for out in o...]
  transfers between devices with their start and end apart: 1 -> 1, of which waited for: 0 -> 0; matrix products, arithmetic and copies ran while one was open for 0% -> 0% of each run, Pallas kernels for 21% -> 20%
where the time goes in v5:
time: 167 us; the launch traced here: 166 us
  Pallas kernels  146 us (87%)
  local copies, waits for them, and re-layouts  14.5 us (9%)
  starting transfers between devices  5.26 us (3%)
    pallas_call x9, Pallas kernels, call(): pl.pallas_call(kernel, out_shape=[jax.ShapeDtypeStruct(*out) for out in o...  146 us
    unnamed x17, local copies, waits for them, and re-layouts  13.2 us
    ppermute x1, starting transfers between devices, swapped(): lax.ppermute(value, 'dom', [(low, low ^ 1 << apart) for low in range(coun...  5.26 us
  transfers between devices with their start and end apart: 1, of which 0 were waited for; matrix products, arithmetic and copies ran while one was open for 0% of the time, Pallas kernels for 20%

profile of v5, /device:TPU:1, one launch (start us, length us, event | category | flops | bytes accessed | tf_op | source)
XLA Modules:
  0.0 166.1 jit_solution(972091857682012576)
XLA Ops:
  0.6 0.0 copy-start
  0.6 1.4 copy.13.counts_ref
  2.0 1.3 copy.12.edges_ref
  3.3 2.5 %copy.15.e_ref = f32[1024,200]{1,0:T(8,128)} copy(f32[1024,200]{0,1:T(8,128)} %param.7) | data formatting | bytes 1638400 | tf_op args[0]
  5.8 0.0 copy-done
  5.8 1.5 copy.14.r_ref
  7.3 2.9 %prep.1 = (f32[200,1024]{1,0:T(8,128)}, f32[200,512]{1,0:T(8,128)}, s32[2,8,1024]{2,1,0:T(8,128)}) custom-call(f32[1024,200]{1,0:T(8,128)} %copy.15.e_ref, s32[2,3,512]{2,1,0:T(4,128)} %copy.12.edges_ref, s32[2,4,1000]{2,1,0:T(4,128)} %neg_ref.1, s32[2,1]{1,0:T(2,128)} %copy.13.counts_ref), custom_call_target="tpu_custom_call" | custom-call | tf_op jit(solution)/shard_map/prep/pallas_call | solution.py:52
  10.2 25.6 %exchange.1 = (f32[200,512]{1,0:T(8,128)}, s32[8,1024]{1,0:T(8,128)}, s32[8,1024]{1,0:T(8,128)}, f32[200,1408]{1,0:T(8,128)}, f32[1024,512]{1,0:T(8,128)}, /*index=5*/f32[1024,512]{1,0:T(8,128)}) custom-call(f32[200,512]{1,0:T(8,128)} %get-tuple-element.34.st_ref, s32[2,8,1024]{2,1,0:T(8,128)} %get-tuple-element.35.meta_ref, f32[1345,200]{1,0:T(8,128)} %copy.14.r_ref), custom_call_target="tpu_custom_call" | custom-call | tf_op jit(solution)/shard_map/exchange/pallas_call | solution.py:52
  35.8 0.0 copy-start.2
  35.8 8.9 %main.1 = (f32[200,1024]{1,0:T(8,128)}, f32[200,512]{1,0:T(8,128)}, f32[2,16,9,8,128]{4,3,2,1,0:T(8,128)}) custom-call(f32[1024,200]{1,0:T(8,128)} %copy.15.e_ref, f32[200,1024]{1,0:T(8,128)} %get-tuple-element.33.et_ref, f32[200,1408]{1,0:T(8,128)} %get-tuple-element.36.rt_ref, f32[200,512]{1,0:T(8,128)} %get-tuple-element.37.st_ref, ...), custom_call_target="tpu_custom_call" | custom-call | tf_op jit(solution)/shard_map/main/pallas_call | solution.py:52
  44.7 5.3 %collective-permute-start = (f32[200,512]{1,0:T(8,128)}, f32[200,512]{1,0:T(8,128)S(1)}, u32[]{:S(2)}, u32[]{:S(2)}) collective-permute-start(f32[200,512]{1,0:T(8,128)} %get-tuple-element.42), channel_id=1, source_target_pairs={{0,128},{1,129},{2,130},{3,131},{4,132},{5,133},{6,134},{7,135},{8... | collective-permute-start | bytes 1228808 | tf_op jit(solution)/shard_map/ppermute | solution.py:393
  50.0 0.0 copy-done.2
  50.0 33.7 %spread_column.1.h_ref = f32[9,8,128]{2,1,0:T(8,128)} custom-call(f32[2,16,9,8,128]{4,3,2,1,0:T(8,128)} %get-tuple-element.40.h_ref), custom_call_target="tpu_custom_call" | custom-call | tf_op jit(solution)/shard_map/spread_column/pallas_call | solution.py:52
  83.6 0.6 pad.4.rel_state_ref
  84.2 0.0 collective-permute-done.gs_ref
  84.3 0.0 copy-start.1
  84.3 0.8 copy-done.1
  85.0 17.2 %spread_share.1 = (f32[2,16,9,8,128]{4,3,2,1,0:T(8,128)}, f32[1024,200]{1,0:T(8,128)}, f32[1,1024]{1,0:T(1,128)}, f32[200,1024]{1,0:T(8,128)}, f32[200,512]{1,0:T(8,128)}) custom-call(f32[9,8,128]{2,1,0:T(8,128)} %spread_column.1.h_ref, f32[200,1024]{1,0:T(8,128)} %get-tuple-element.33.et_ref, f32[1,1024]{1,0:T(1,128)} %bitcast.2, ...), custom_call_target="tpu_custom_call" | custom-call | tf_op jit(solution)/shard_map/spread_share/pallas_call | solution.py:52
  102.3 9.6 %second_main.1 = (f32[200,1024]{1,0:T(8,128)}, f32[200,512]{1,0:T(8,128)}, f32[2,16,9,8,128]{4,3,2,1,0:T(8,128)}, f32[200,1408]{1,0:T(8,128)}, f32[1,1408]{1,0:T(1,128)}) custom-call(f32[1024,200]{1,0:T(8,128)} %get-tuple-element.43.e_ref, f32[200,1024]{1,0:T(8,128)} %get-tuple-element.44.et_ref, f32[200,1408]{1,0:T(8,128)} %get-tuple-element.36.rt_ref, ...), custom_call_target="tpu_custom_call" | custom-call | tf_op jit(solution)/shard_map/second_main/pallas_call | solution.py:52
  111.8 16.3 %second_spread_sum.1 = (f32[9,8,128]{2,1,0:T(8,128)}, f32[200,512]{1,0:T(8,128)}) custom-call(f32[2,16,9,8,128]{4,3,2,1,0:T(8,128)} %get-tuple-element.49.h_ref, f32[200,512]{1,0:T(8,128)} %get-tuple-element.50.gs_ref), custom_call_target="tpu_custom_call" | custom-call | tf_op jit(solution)/shard_map/second_spread_sum/pallas_call | solution.py:52
  128.1 14.4 %last_column_sum.1 = (f32[9,8,128]{2,1,0:T(8,128)}, f32[1024,200]{1,0:T(8,128)}, f32[1,1024]{1,0:T(1,128)}) custom-call(f32[9,8,128]{2,1,0:T(8,128)} %get-tuple-element.51.h_ref, f32[200,1024]{1,0:T(8,128)} %get-tuple-element.44.et_ref, f32[1,1024]{1,0:T(1,128)} %get-tuple-element.52.state_ref, f32[200,1024]{1,0:T(8,128)} %get-tuple-element.53.gt_ref, ...), custom_call_target="tpu_custom_call" | custom-call | tf_op jit(solution)/shard_map/last_column_sum/pallas_call | solution.py:52
  142.5 2.4 %copy.16 = f32[1024,200]{0,1:T(8,128)} copy(f32[1024,200]{1,0:T(8,128)} %get-tuple-element.62) | data formatting | bytes 1638400
  144.9 17.2 %last_spread_share.1 = (f32[1345,200]{1,0:T(8,128)}, f32[1,1408]{1,0:T(1,128)}) custom-call(f32[9,8,128]{2,1,0:T(8,128)} %get-tuple-element.57.h_ref, f32[200,1408]{1,0:T(8,128)} %get-tuple-element.58.rt_ref, f32[1,1408]{1,0:T(1,128)} %get-tuple-element.59.rel_state_ref), custom_call_target="tpu_custom_call" | custom-call | tf_op jit(solution)/shard_map/last_spread_share/pallas_call | solution.py:52
  162.1 0.0 copy-start.3
  162.1 0.0 copy-start.4
  162.2 2.8 %copy.17 = f32[1345,200]{0,1:T(8,128)} copy(f32[1345,200]{1,0:T(8,128)} %get-tuple-element.64) | data formatting | bytes 2152000
  164.9 0.0 copy-done.3
  164.9 0.6 slice_reduce_fusion
  165.5 0.0 copy-done.4
  165.5 0.6 copy.19
  (1 shorter events, 0.0 us)
Async XLA Ops:
  0.6 5.2 %copy-start = (f32[1345,200]{0,1:T(8,128)S(1)}, f32[1345,200]{0,1:T(8,128)}, u32[]{:S(2)}) copy-start(f32[1345,200]{0,1:T(8,128)} %param.9) | copy-start | bytes 3228004
  35.8 14.2 %copy-start.2 = (f32[1345]{0:T(1024)S(1)}, f32[1345]{0:T(1024)}, u32[]{:S(2)}) copy-start(f32[1345]{0:T(1024)} %param.10) | copy-start | bytes 16144
  44.7 39.5 %collective-permute-start = (f32[200,512]{1,0:T(8,128)}, f32[200,512]{1,0:T(8,128)S(1)}, u32[]{:S(2)}, u32[]{:S(2)}) collective-permute-start(f32[200,512]{1,0:T(8,128)} %get-tuple-element.42), channel_id=1, source_target_pairs={{0,128},{1,129},{2,130},{3,131},{4,132},{5,133},{6,134},{7,135},{8... | collective-permute-start | bytes 1228808 | tf_op jit(solution)/shard_map/ppermute | solution.py:393
  84.3 0.8 copy-start.1
  162.1 2.8 %copy-start.3 = (f32[1,1408]{1,0:T(1,128)S(1)}, f32[1,1408]{1,0:T(1,128)}, u32[]{:S(2)}) copy-start(f32[1,1408]{1,0:T(1,128)} %get-tuple-element.61) | copy-start | bytes 16900
  162.1 3.4 %copy-start.4 = (f32[1,1024]{1,0:T(1,128)S(1)}, f32[1,1024]{1,0:T(1,128)}, u32[]{:S(2)}) copy-start(f32[1,1024]{1,0:T(1,128)} %get-tuple-element.56) | copy-start | bytes 12292

commit v6 on v5

--- a/solution.py
+++ b/solution.py
@@ -254,46 +254,18 @@
         beside.wait()
 
 
-def spread_sum_kernel(h_ref, out_ref, *more):
-    spread_sum(h_ref, out_ref, *more)
-
-
-def second_spread_sum_kernel(h_ref, gs_ref, out_ref, gs_out, sx, rx, *more):
-    spread_sum(h_ref, out_ref, *more, beside=remote(gs_ref, gs_out, (sx, rx), 0, other_core()))
-
-
-def column_sum_kernel(h_ref, out_ref, level, *more, beside=None):
-    got, sems = more[:-2], more[-2:]
-    column = in_column()
-    z = places_of()[3]
-    meet(column[1:])
-    sends = [remote(h_ref, got[k], sems, k, column[k]) for k in range(1, ZS)]
-    for k in (4, 3, 5, 2, 6, 1, 7):
-        sends[k - 1].start()
-    level[z] = h_ref[...]
-    if beside is not None:
-        beside()
-    for k in range(1, ZS):
-        sends[k - 1].wait_recv()
-        level[(z + ZS - k) % ZS] = got[k][...]
-    total = level[0]
-    for k in range(1, ZS):
-        total = total + level[k]
-    out_ref[...] = total
-    for one in sends:
-        one.wait_send()
-
-
-def spread_column_kernel(h_ref, out_ref, level, part, *more):
+def spread_column(h_ref, out_ref, level, part, *more, near=None, during=None):
     s2, r2, *more = more
     got2, more = more[:ZS], more[ZS:]
     c, y, x, z = places_of()
     column = in_column()
-    spread_sum(h_ref, part, *more, also=column[1:])
+    spread_sum(h_ref, part, *more, beside=near, also=column[1:])
     third = [None] + [remote(part, got2[k], (s2, r2), k, column[k]) for k in range(1, ZS)]
     for k in (4, 3, 5, 2, 6, 1, 7):
         third[k].start()
     level[z] = part[...]
+    if during is not None:
+        during()
     for k in range(1, ZS):
         third[k].wait_recv()
         level[(z + ZS - k) % ZS] = got2[k][...]
@@ -305,23 +277,14 @@
         one.wait_send()
 
 
-def last_column_sum_kernel(
-    h_ref, et_ref, state_ref, gt_ref, gs_ref, meta_ref, out_ref, e_out, state_out, wide, *more
-):
-    def beside():
-        after = entity_step(1, et_ref, state_ref, gt_ref, gs_ref, meta_ref, state_out)
-        e_out[...] = turned(after, wide)
-
-    column_sum_kernel(h_ref, out_ref, *more, beside=beside)
-
-
-def spread_share(h_ref, out_ref, *more, beside=None):
+def spread_share(h_ref, out_ref, *more, beside=None, greet=True):
     s3, r3, s4, r4 = more[-4:]
     got3, got4 = (more[i * PLANE : (i + 1) * PLANE] for i in range(2))
     other = other_core()
     plane = in_plane()
     c = places_of()[0]
-    meet([other] + [p[0] for p in plane[1:]])
+    if greet:
+        meet([other] + [p[0] for p in plane[1:]])
     order = range(PLANE - 1, 0, -1)
     fourth = [None] + [remote(h_ref, got3[k], (s3, r3), k, plane[k][0]) for k in range(1, PLANE)]
     fifth = [remote(got3[k] if k else h_ref, got4[k], (s4, r4), k, other) for k in range(PLANE)]
@@ -343,6 +306,27 @@
         extra.wait()
 
 
+def total_kernel(
+    h_ref, et_ref, state_ref, gt_ref, gs_ref, meta_ref, rt_ref, rel_state_ref,
+    e_out, state_out, r_out, rel_state_out, gs_in, both, sums, whole, wide, wide_rels, sx, rx, *more,
+):
+    def during():
+        after = entity_step(1, et_ref, state_ref, gt_ref, gs_in, meta_ref, state_out)
+        e_out[...] = turned(after, wide)
+
+    near = remote(gs_ref, gs_in, (sx, rx), 0, other_core())
+    more, share = more[: -2 * PLANE - 4], more[-2 * PLANE - 4 :]
+    spread_column(h_ref, both, *more, near=near, during=during)
+    spread_share(both, sums, *share, greet=False)
+    join_tiles(sums, whole)
+    after, rel_state_out[...] = stepped(rt_ref[...], rel_state_ref[...], whole[...])
+    r_out[...] = turned(after, wide_rels)[: r_out.shape[0]]
+
+
+def spread_column_kernel(h_ref, out_ref, *more):
+    spread_column(h_ref, out_ref, *more)
+
+
 def spread_share_kernel(
     h_ref, et_ref, state_ref, gt_ref, gs_ref, meta_ref,
     out_ref, e_out, state_out, et_out, rows_out, mine, wide, sx, rx, *more,
@@ -358,15 +342,6 @@
         return send
 
     spread_share(h_ref, out_ref, *more, beside=beside)
-
-
-def last_spread_share_kernel(
-    h_ref, rt_ref, rel_state_ref, r_out, rel_state_out, sums, whole, wide, *more
-):
-    spread_share(h_ref, sums, *more)
-    join_tiles(sums, whole)
-    after, rel_state_out[...] = stepped(rt_ref[...], rel_state_ref[...], whole[...])
-    r_out[...] = turned(after, wide)[: r_out.shape[0]]
 
 
 def turned(value, wide):
@@ -459,7 +434,7 @@
         [h, et, state, gt, gs, meta],
         [space(dim, slots), space(dim_pad, rows), *pairs(1)] + [one] * (2 * PLANE) + pairs(PLANE, PLANE),
         name="spread_share",
-        collective=3,
+        collective=2,
     )
     gt, gs, h, rt, rel_state = call(
         second_main_kernel,
@@ -468,29 +443,18 @@
         [space(dim, slots), space(dim, slots), space(dim, rels_pad)],
         name="second_main",
     )
-    h, gs = call(
-        second_spread_sum_kernel,
-        [(piece, F32), array(dim, slots)],
-        [h, gs],
-        pairs(1) + [one] * (3 * PLANE) + pairs(PLANE, PLANE),
-        name="second_spread_sum",
-        collective=4,
-    )
-    h, table, state = call(
-        last_column_sum_kernel,
-        [(piece, F32), array(rows, dim), array(1, rows)],
-        [h, et, state, gt, gs, meta],
-        [space(dim_pad, rows), space(ZS, *piece)] + [one] * ZS + pairs(ZS),
-        name="last_column_sum",
-        collective=5,
-    )
-    relations, rel_state = call(
-        last_spread_share_kernel,
-        [array(rels, dim), array(1, rels_pad)],
-        [h, rt, rel_state],
-        [space(*pieces), space(dim, rels_pad), space(dim_pad, rels_pad)] + [one] * (2 * PLANE) + pairs(PLANE, PLANE),
-        name="last_spread_share",
-        collective=6,
+    table, state, relations, rel_state = call(
+        total_kernel,
+        [array(rows, dim), array(1, rows), array(rels, dim), array(1, rels_pad)],
+        [h, et, state, gt, gs, meta, rt, rel_state],
+        [space(dim, slots), one, space(*pieces), space(dim, rels_pad), space(dim_pad, rows)]
+        + [space(dim_pad, rels_pad), *pairs(1), space(ZS, *piece), one, *pairs(ZS)]
+        + [one] * (ZS + 3 * PLANE)
+        + pairs(PLANE, PLANE)
+        + [one] * (2 * PLANE)
+        + pairs(PLANE, PLANE),
+        name="total",
+        collective=3,
     )
     return table, state.reshape(rows), relations, rel_state[0, :rels]
 

time: 167 us -> 156 us (0.934)
  Pallas kernels: 146 us -> 136 us
    pallas_call x9 -> x7, Pallas kernels: 146 us -> 136 us  [call(): pl.pallas_call(kernel, out_shape=[jax.ShapeDtypeStruct(*out) for out in o...]
    unnamed x17 -> x19, local copies, waits for them, and re-layouts: 13.2 us -> 12 us
  transfers between devices with their start and end apart: 1 -> 1, of which waited for: 0 -> 0; matrix products, arithmetic and copies ran while one was open for 0% -> 0% of each run, Pallas kernels for 20% -> 22%
where the time goes in v6:
time: 156 us; the launch traced here: 155 us
  Pallas kernels  136 us (87%)
  local copies, waits for them, and re-layouts  13.3 us (9%)
  starting transfers between devices  5.28 us (3%)
    pallas_call x7, Pallas kernels, call(): pl.pallas_call(kernel, out_shape=[jax.ShapeDtypeStruct(*out) for out in o...  136 us
    unnamed x19, local copies, waits for them, and re-layouts  12 us
    ppermute x1, starting transfers between devices, swapped(): lax.ppermute(value, 'dom', [(low, low ^ 1 << apart) for low in range(coun...  5.28 us
  transfers between devices with their start and end apart: 1, of which 0 were waited for; matrix products, arithmetic and copies ran while one was open for 0% of the time, Pallas kernels for 22%

profile of v6, /device:TPU:1, one launch (start us, length us, event | category | flops | bytes accessed | tf_op | source)
XLA Modules:
  0.0 155.2 jit_solution(5304927633242675336)
XLA Ops:
  0.6 0.0 copy-start.1
  0.6 1.4 copy.13.counts_ref
  2.0 1.3 copy.12.edges_ref
  3.3 2.5 %copy.15.e_ref = f32[1024,200]{1,0:T(8,128)} copy(f32[1024,200]{0,1:T(8,128)} %param.7) | data formatting | bytes 1638400 | tf_op args[0]
  5.8 0.0 copy-done.1
  5.8 1.6 copy.14.r_ref
  7.3 2.9 %prep.1 = (f32[200,1024]{1,0:T(8,128)}, f32[200,512]{1,0:T(8,128)}, s32[2,8,1024]{2,1,0:T(8,128)}) custom-call(f32[1024,200]{1,0:T(8,128)} %copy.15.e_ref, s32[2,3,512]{2,1,0:T(4,128)} %copy.12.edges_ref, s32[2,4,1000]{2,1,0:T(4,128)} %neg_ref.1, s32[2,1]{1,0:T(2,128)} %copy.13.counts_ref), custom_call_target="tpu_custom_call" | custom-call | tf_op jit(solution)/shard_map/prep/pallas_call | solution.py:52
  10.2 25.6 %exchange.1 = (f32[200,512]{1,0:T(8,128)}, s32[8,1024]{1,0:T(8,128)}, s32[8,1024]{1,0:T(8,128)}, f32[200,1408]{1,0:T(8,128)}, f32[1024,512]{1,0:T(8,128)}, /*index=5*/f32[1024,512]{1,0:T(8,128)}) custom-call(f32[200,512]{1,0:T(8,128)} %get-tuple-element.31.st_ref, s32[2,8,1024]{2,1,0:T(8,128)} %get-tuple-element.32.meta_ref, f32[1345,200]{1,0:T(8,128)} %copy.14.r_ref), custom_call_target="tpu_custom_call" | custom-call | tf_op jit(solution)/shard_map/exchange/pallas_call | solution.py:52
  35.8 0.0 copy-start.3
  35.8 8.9 %main.1 = (f32[200,1024]{1,0:T(8,128)}, f32[200,512]{1,0:T(8,128)}, f32[2,16,9,8,128]{4,3,2,1,0:T(8,128)}) custom-call(f32[1024,200]{1,0:T(8,128)} %copy.15.e_ref, f32[200,1024]{1,0:T(8,128)} %get-tuple-element.30.et_ref, f32[200,1408]{1,0:T(8,128)} %get-tuple-element.33.rt_ref, f32[200,512]{1,0:T(8,128)} %get-tuple-element.34.st_ref, ...), custom_call_target="tpu_custom_call" | custom-call | tf_op jit(solution)/shard_map/main/pallas_call | solution.py:52
  44.7 5.3 %collective-permute-start = (f32[200,512]{1,0:T(8,128)}, f32[200,512]{1,0:T(8,128)S(1)}, u32[]{:S(2)}, u32[]{:S(2)}) collective-permute-start(f32[200,512]{1,0:T(8,128)} %get-tuple-element.39), channel_id=1, source_target_pairs={{0,128},{1,129},{2,130},{3,131},{4,132},{5,133},{6,134},{7,135},{8... | collective-permute-start | bytes 1228808 | tf_op jit(solution)/shard_map/ppermute | solution.py:368
  50.0 0.0 copy-done.3
  50.0 33.7 %spread_column.1.h_ref = f32[9,8,128]{2,1,0:T(8,128)} custom-call(f32[2,16,9,8,128]{4,3,2,1,0:T(8,128)} %get-tuple-element.37.h_ref), custom_call_target="tpu_custom_call" | custom-call | tf_op jit(solution)/shard_map/spread_column/pallas_call | solution.py:52
  83.6 0.6 pad.4.rel_state_ref
  84.2 0.0 collective-permute-done.gs_ref
  84.2 0.0 copy-start.2
  84.2 0.8 copy-done.2
  85.0 17.3 %spread_share.1 = (f32[2,16,9,8,128]{4,3,2,1,0:T(8,128)}, f32[1024,200]{1,0:T(8,128)}, f32[1,1024]{1,0:T(1,128)}, f32[200,1024]{1,0:T(8,128)}, f32[200,512]{1,0:T(8,128)}) custom-call(f32[9,8,128]{2,1,0:T(8,128)} %spread_column.1.h_ref, f32[200,1024]{1,0:T(8,128)} %get-tuple-element.30.et_ref, f32[1,1024]{1,0:T(1,128)} %bitcast.2, ...), custom_call_target="tpu_custom_call" | custom-call | tf_op jit(solution)/shard_map/spread_share/pallas_call | solution.py:52
  102.3 9.6 %second_main.1 = (f32[200,1024]{1,0:T(8,128)}, f32[200,512]{1,0:T(8,128)}, f32[2,16,9,8,128]{4,3,2,1,0:T(8,128)}, f32[200,1408]{1,0:T(8,128)}, f32[1,1408]{1,0:T(1,128)}) custom-call(f32[1024,200]{1,0:T(8,128)} %get-tuple-element.40.e_ref, f32[200,1024]{1,0:T(8,128)} %get-tuple-element.41.et_ref, f32[200,1408]{1,0:T(8,128)} %get-tuple-element.33.rt_ref, ...), custom_call_target="tpu_custom_call" | custom-call | tf_op jit(solution)/shard_map/second_main/pallas_call | solution.py:52
  111.9 38.1 %total.1 = (f32[1024,200]{1,0:T(8,128)}, f32[1,1024]{1,0:T(1,128)}, f32[1345,200]{1,0:T(8,128)}, f32[1,1408]{1,0:T(1,128)}) custom-call(f32[2,16,9,8,128]{4,3,2,1,0:T(8,128)} %get-tuple-element.46.h_ref, f32[200,1024]{1,0:T(8,128)} %get-tuple-element.41.et_ref, f32[1,1024]{1,0:T(1,128)} %get-tuple-element.47.state_ref, ...), custom_call_target="tpu_custom_call" | custom-call | tf_op jit(solution)/shard_map/total/pallas_call | solution.py:52
  150.0 0.0 copy-start.4
  150.0 0.0 copy-start
  150.0 2.5 %copy.16 = f32[1024,200]{0,1:T(8,128)} copy(f32[1024,200]{1,0:T(8,128)} %get-tuple-element.56) | data formatting | bytes 1638400
  152.5 0.0 copy-done.4
  152.5 0.6 slice_reduce_fusion
  153.2 0.0 copy-done
  153.2 0.0 copy-start.5
  153.2 1.4 copy.17
  154.6 0.0 copy-done.5
  154.6 0.6 copy.19
  (1 shorter events, 0.0 us)
Async XLA Ops:
  0.6 5.2 %copy-start.1 = (f32[1345,200]{0,1:T(8,128)S(1)}, f32[1345,200]{0,1:T(8,128)}, u32[]{:S(2)}) copy-start(f32[1345,200]{0,1:T(8,128)} %param.9) | copy-start | bytes 3228004
  35.8 14.2 %copy-start.3 = (f32[1345]{0:T(1024)S(1)}, f32[1345]{0:T(1024)}, u32[]{:S(2)}) copy-start(f32[1345]{0:T(1024)} %param.10) | copy-start | bytes 16144
  44.7 39.6 %collective-permute-start = (f32[200,512]{1,0:T(8,128)}, f32[200,512]{1,0:T(8,128)S(1)}, u32[]{:S(2)}, u32[]{:S(2)}) collective-permute-start(f32[200,512]{1,0:T(8,128)} %get-tuple-element.39), channel_id=1, source_target_pairs={{0,128},{1,129},{2,130},{3,131},{4,132},{5,133},{6,134},{7,135},{8... | collective-permute-start | bytes 1228808 | tf_op jit(solution)/shard_map/ppermute | solution.py:368
  84.2 0.8 copy-start.2
  150.0 2.6 %copy-start.4 = (f32[1,1408]{1,0:T(1,128)S(1)}, f32[1,1408]{1,0:T(1,128)}, u32[]{:S(2)}) copy-start(f32[1,1408]{1,0:T(1,128)} %get-tuple-element.55) | copy-start | bytes 16900
  150.0 3.2 %copy-start = (f32[1345,200]{1,0:T(8,128)S(1)}, f32[1345,200]{1,0:T(8,128)}, u32[]{:S(2)}) copy-start(f32[1345,200]{1,0:T(8,128)} %get-tuple-element.58) | copy-start | bytes 3228004
  153.2 1.4 copy-start.5

commit v7 on v6

v7 whole, which is shorter than its diff:
```python
import functools

import jax
import jax.numpy as jnp
from jax import lax
from jax.experimental import pallas as pl
from jax.experimental.pallas import tpu as pltpu
from jax.sharding import PartitionSpec as P

RATE = 0.2
F32 = jnp.float32
BF16 = jnp.bfloat16
VMEM = pl.BlockSpec(memory_space=pltpu.VMEM)
SMEM = pl.BlockSpec(memory_space=pltpu.SMEM)
NN = (((1,), (0,)), ((), ()))
NT = (((1,), (1,)), ((), ()))
LANES = 128
SUBLANES = 8
ZS, XS, YS, CORES = 8, 4, 4, 2
PLANE = XS * YS
MESH = pl.DeviceIdType.MESH


def split(value):
    high = value.astype(BF16)
    return high, (value - high.astype(F32)).astype(BF16)


def dot(left, right, dims=NN):
    return lax.dot_general(left, right, dims, preferred_element_type=F32)


def dot3(left, right, dims=NN):
    return (
        dot(left[0], right[0], dims) + dot(left[0], right[1], dims) + dot(left[1], right[0], dims)
    )


def dot_exact(left, right, dims=NN):
    return dot(left[0], right, dims) + dot(left[1], right, dims)


def spots(ids, count):
    rows = lax.broadcasted_iota(jnp.int32, (count, ids.shape[1]), 0)
    return jnp.where(rows == ids, 1.0, 0.0).astype(BF16)


def call(kernel, outs, args, scratch=(), name=None, collective=None):
    params = None
    if collective is not None:
        params = pltpu.CompilerParams(collective_id=collective, has_side_effects=True)
    return pl.pallas_call(
        kernel,
        out_shape=[jax.ShapeDtypeStruct(*out) for out in outs],
        in_specs=[VMEM] * len(args),
        out_specs=[VMEM] * len(outs),
        scratch_shapes=list(scratch),
        compiler_params=params,
        name=name,
    )(*args)


def pairs(*counts):
    return [pltpu.SemaphoreType.DMA((count,)) for count in counts for _ in range(2)]


def hist(meta_ref, c_ref, blocks, draws):
    ones = jnp.ones((meta_ref.shape[1], LANES), BF16)
    for b in range(blocks):
        hits = spots(meta_ref[4 + b : 5 + b, :], c_ref.shape[0])
        c_ref[:, b * LANES : (b + 1) * LANES] = dot(hits, ones) * (1.0 / draws)


def table_parts(et_ref, wide, e_parts, et_parts):
    dim = et_ref.shape[0]
    wide[0:dim, :] = et_ref[...]
    wide[dim:, :] = jnp.zeros((wide.shape[0] - dim, wide.shape[1]), F32)
    e_parts[0][...], e_parts[1][...] = split(wide[...].T)
    et_parts[0][...], et_parts[1][...] = split(et_ref[...])


def relation_rows(rt_ref, meta_ref, picks, w):
    picks[...] = spots(meta_ref[1:2, 0 : w.shape[1]], rt_ref.shape[1])
    w[...] = dot_exact(split(rt_ref[...]), picks[...])


def edge_part(part, e_parts, et_parts, st, meta_ref, c_ref, picks, w, gt_ref, gs_ref, h_sum, q, tmp):
    dim, rows = et_parts[0].shape
    half = dim // 2
    wide = st.shape[1]
    lanes = slice(part * wide, (part + 1) * wide)
    number = lax.broadcasted_iota(jnp.int32, (1, wide), 1) + part * wide
    live = number < meta_ref[3:4, lanes]
    target = jnp.where(live, meta_ref[2:3, lanes], -1)
    alive = live.astype(F32)
    s_re, s_im = st[0:half, :], st[half:dim, :]
    w_re, w_im = w[0:half, lanes], w[half:dim, lanes]
    q[0:half, :] = s_re * w_re - s_im * w_im
    q[half:dim, :] = s_re * w_im + s_im * w_re
    q_parts = split(q[...])
    up = jnp.zeros((dim, wide), F32)
    step = 256
    for j in range(0, rows, step):
        e_part = [one[j : j + step, 0:dim] for one in e_parts]
        scores = dot3(e_part, q_parts)
        sig = 0.5 * jnp.tanh(0.5 * scores) + 0.5
        row = lax.broadcasted_iota(jnp.int32, (step, wide), 0) + j
        mark = jnp.where(row == target, 1.0, 0.0)
        weight = split(sig * (c_ref[j : j + step, lanes] * alive + mark) - mark)
        up = up + dot3([one[:, j : j + step] for one in et_parts], weight)
        grad = dot3(q_parts, weight, NT)
        gt_ref[:, j : j + step] = grad if part == 0 else gt_ref[:, j : j + step] + grad
    q[...] = up
    u_re, u_im = q[0:half, :], q[half:dim, :]
    gs_ref[0:half, lanes] = u_re * w_re + u_im * w_im
    gs_ref[half:dim, lanes] = u_im * w_re - u_re * w_im
    tmp[0:half, :] = u_re * s_re + u_im * s_im
    tmp[half:dim, :] = u_im * s_re - u_re * s_im
    total = dot_exact(split(tmp[...]), picks[:, lanes], NT)
    h_sum[...] = total if part == 0 else h_sum[...] + total


def cut_tiles(h_sum, h_ref):
    places, tiles = tile_places(h_ref.shape, h_sum.shape)
    for place, (row, lane) in zip(places, tiles):
        h_ref[place] = h_sum[row : row + SUBLANES, lane : lane + LANES]
    for place in places[len(tiles) :]:
        h_ref[place] = jnp.zeros((SUBLANES, LANES), F32)


def front_kernel(
    et_ref, r_ref, edges_ref, neg_ref, counts_ref,
    gt_ref, gs_ref, h_ref, rt_ref, meta_ref, meta1_ref, c1_ref,
    meta0, c0, st, rows, wide, eh, el, eth, etl, picks, w, h_sum, q, tmp, ss, rs,
):
    dim, count = et_ref.shape
    kinds, rounds, slots = edges_ref.shape
    blocks, draws = neg_ref.shape[1:]
    parts, _, width = st.shape
    c, y, x, z = places_of()
    far, near = device((z + ZS // 2) % ZS, x, y, c), other_core()
    greet([far, near])
    eth[...], etl[...] = split(et_ref[...])
    meta_ref[...] = jnp.full(meta_ref.shape, -1, jnp.int32)
    for r in range(rounds):
        for kind in range(kinds):
            meta_ref[r, kind : kind + 1, 0:slots] = edges_ref[kind, r : r + 1, :]
        meta_ref[r, kinds : kinds + 1, :] = jnp.broadcast_to(counts_ref[0:1, r : r + 1], (1, count))
        meta_ref[r, kinds + 1 : kinds + 1 + blocks, 0:draws] = neg_ref[r]
    sends = [remote(st.at[p], rows.at[p], (ss, rs), p, far) for p in range(parts)]
    sends.append(remote(meta_ref.at[0], meta0, (ss, rs), parts, far))
    sends.append(remote(meta_ref.at[1], meta1_ref, (ss, rs), parts + 1, near))
    for p in range(parts):
        source = meta_ref[0, 0:1, p * width : (p + 1) * width]
        st[p] = dot_exact((eth[...], etl[...]), spots(source, count))
        if p == 0:
            await_peers([far, near])
            sends[parts].start()
            sends[parts + 1].start()
        sends[p].start()
    wide[0:dim, :] = et_ref[...]
    wide[dim:, :] = jnp.zeros((wide.shape[0] - dim, count), F32)
    eh[...], el[...] = split(wide[...].T)
    rt_ref[...] = jnp.zeros_like(rt_ref)
    rt_ref[:, 0 : r_ref.shape[1]] = r_ref[...]
    sends[parts + 1].wait_recv()
    hist(meta1_ref, c1_ref, blocks, draws)
    sends[parts].wait_recv()
    hist(meta0, c0, blocks, draws)
    relation_rows(rt_ref, meta0, picks, w)
    for p in range(parts):
        sends[p].wait_recv()
        edge_part(
            p, (eh, el), (eth, etl), rows.at[p], meta0, c0, picks, w, gt_ref, gs_ref, h_sum, q, tmp
        )
    cut_tiles(h_sum, h_ref)
    for one in sends:
        one.wait_send()


def second_main_kernel(
    et_ref, rt_ref, rel_state_ref, sum_ref, rows, meta_ref, c_ref,
    gt_ref, gs_ref, h_ref, rt_out, rel_state_out,
    wide, eh, el, eth, etl, picks, w, h_sum, q, tmp, state,
):
    rels = rel_state_ref.shape[1]
    join_tiles(sum_ref, h_sum)
    state[...] = jnp.ones_like(state)
    state[:, 0:rels] = rel_state_ref[...]
    rt_out[...], rel_state_out[...] = stepped(rt_ref[...], state[...], h_sum[...])
    table_parts(et_ref, wide, (eh, el), (eth, etl))
    relation_rows(rt_out, meta_ref, picks, w)
    for p in range(rows.shape[0]):
        edge_part(
            p, (eh, el), (eth, etl), rows.at[p], meta_ref, c_ref, picks, w, gt_ref, gs_ref, h_sum, q, tmp
        )
    cut_tiles(h_sum, h_ref)


def tile_places(shape, flat):
    places = [(c, k, t) for c in range(shape[0]) for k in range(shape[1]) for t in range(shape[2])]
    tiles = [(r, l) for r in range(0, flat[0], SUBLANES) for l in range(0, flat[1], LANES)]
    return places, tiles


def join_tiles(h_ref, whole):
    places, tiles = tile_places(h_ref.shape, whole.shape)
    for place, (row, lane) in zip(places, tiles):
        whole[row : row + SUBLANES, lane : lane + LANES] = h_ref[place]


def places_of():
    me = lax.axis_index("dom")
    return me % CORES, me // CORES % YS, me // (CORES * YS) % XS, me // (CORES * YS * XS)


def device(z, x, y, c):
    return (((z * XS + x) * YS + y) * CORES + c,)


def remote(src, dst, sems, k, to):
    return pltpu.make_async_remote_copy(
        src_ref=src,
        dst_ref=dst,
        send_sem=sems[0].at[k],
        recv_sem=sems[1].at[k],
        device_id=to,
        device_id_type=MESH,
    )


def greet(peers):
    for peer in peers:
        pl.semaphore_signal(
            pltpu.get_barrier_semaphore(), inc=1, device_id=peer, device_id_type=MESH
        )


def await_peers(peers):
    pl.semaphore_wait(pltpu.get_barrier_semaphore(), len(peers))


def meet(peers):
    greet(peers)
    await_peers(peers)


def other_core():
    c, y, x, z = places_of()
    return device(z, x, y, 1 - c)


def in_plane():
    c, y, x, z = places_of()
    plane = []
    for k in range(PLANE):
        px, py = (x + k // YS) % XS, (y + k % YS) % YS
        fx, fy = (x + XS - k // YS) % XS, (y + YS - k % YS) % YS
        plane.append((device(z, px, py, c), px * YS + py, fx * YS + fy))
    return plane


def in_column():
    c, y, x, z = places_of()
    return [device((z + k) % ZS, x, y, c) for k in range(ZS)]


def spread_sum(h_ref, out_ref, *more, beside=(), also=()):
    s0, r0, s1, r1 = more[-4:]
    acc, got0, got1 = (more[i * PLANE : (i + 1) * PLANE] for i in range(3))
    other = other_core()
    plane = in_plane()
    c = places_of()[0]
    meet([other, *(p[0] for p in plane[1:]), *also])
    order = range(PLANE - 1, -1, -1)
    first = [remote(h_ref.at[1 - c, plane[k][1]], got0[k], (s0, r0), k, other) for k in range(PLANE)]
    second = [None] + [remote(acc[k], got1[k], (s1, r1), k, plane[k][0]) for k in range(1, PLANE)]
    for k in order:
        first[k].start()
    for one in beside:
        one.start()
    for k in order:
        first[k].wait_recv()
        acc[k][...] = h_ref[c, plane[k][1]] + got0[k][...]
        if k < PLANE - 1:
            second[k + 1].start()
    total = acc[0][...]
    for k in order[:-1]:
        second[k].wait_recv()
        total = total + got1[k][...]
    out_ref[...] = total
    for one in first + second[1:]:
        one.wait_send()


def spread_column(h_ref, out_ref, level, part, *more, early=(), late=(), during=None):
    s2, r2, *more = more
    got2, more = more[:ZS], more[ZS:]
    c, y, x, z = places_of()
    column = in_column()
    spread_sum(h_ref, part, *more, beside=early, also=column[1:])
    third = [None] + [remote(part, got2[k], (s2, r2), k, column[k]) for k in range(1, ZS)]
    for k in (4, 3, 5, 2, 6, 1, 7):
        third[k].start()
    for one in late:
        one.start()
    level[z] = part[...]
    if during is not None:
        during()
    for k in range(1, ZS):
        third[k].wait_recv()
        level[(z + ZS - k) % ZS] = got2[k][...]
    total = level[0]
    for k in range(1, ZS):
        total = total + level[k]
    out_ref[...] = total
    for one in third[1:]:
        one.wait_send()


def spread_share(h_ref, out_ref, *more, beside=None):
    s3, r3, s4, r4 = more[-4:]
    got3, got4 = (more[i * PLANE : (i + 1) * PLANE] for i in range(2))
    other = other_core()
    plane = in_plane()
    c = places_of()[0]
    order = range(PLANE - 1, 0, -1)
    fourth = [None] + [remote(h_ref, got3[k], (s3, r3), k, plane[k][0]) for k in range(1, PLANE)]
    fifth = [remote(got3[k] if k else h_ref, got4[k], (s4, r4), k, other) for k in range(PLANE)]
    for k in order:
        fourth[k].start()
    fifth[0].start()
    out_ref[c, plane[0][1]] = h_ref[...]
    for k in order:
        fourth[k].wait_recv()
        fifth[k].start()
        out_ref[c, plane[k][2]] = got3[k][...]
    if beside is not None:
        beside()
    for k in [0, *order]:
        fifth[k].wait_recv()
        out_ref[1 - c, plane[k][2]] = got4[k][...]
    for one in fourth[1:] + fifth:
        one.wait_send()


def first_total_kernel(
    h_ref, et_ref, state_ref, gt_ref, gs_ref, meta_ref,
    sums_ref, et_out, state_out, rows_out,
    gs_in, mine, both, sx, rx, *more,
):
    c, y, x, z = places_of()
    far = device((z + ZS // 2) % ZS, x, y, c)
    dim = gs_ref.shape[0]
    parts, _, width = mine.shape
    cut = dim // 2 // SUBLANES * SUBLANES
    ends = [(0, cut), (cut, dim)]
    back = [remote(gs_ref.at[a:b], gs_in.at[a:b], (sx, rx), i, far) for i, (a, b) in enumerate(ends)]
    on = [remote(mine.at[p], rows_out.at[p], (sx, rx), 2 + p, other_core()) for p in range(parts)]
    more, share = more[: -2 * PLANE - 4], more[-2 * PLANE - 4 :]
    spread_column(h_ref, both, *more, early=back[:1], late=back[1:])

    def beside():
        for one in back:
            one.wait()
        after = entity_step(0, et_ref, state_ref, gt_ref, gs_in, meta_ref, state_out)
        et_out[...] = after
        pieces = split(after)
        for p in range(parts):
            source = meta_ref[1, 0:1, p * width : (p + 1) * width]
            mine[p] = dot_exact(pieces, spots(source, after.shape[1]))
            on[p].start()

    spread_share(both, sums_ref, *share, beside=beside)
    for one in on:
        one.wait()


def last_total_kernel(
    h_ref, et_ref, state_ref, gt_ref, gs_ref, meta_ref, rt_ref, rel_state_ref,
    et_out, state_out, rt_out, rel_state_out,
    gs_in, both, sums, whole, sx, rx, *more,
):
    near = remote(gs_ref, gs_in, (sx, rx), 0, other_core())

    def during():
        near.wait()
        et_out[...] = entity_step(1, et_ref, state_ref, gt_ref, gs_in, meta_ref, state_out)

    more, share = more[: -2 * PLANE - 4], more[-2 * PLANE - 4 :]
    spread_column(h_ref, both, *more, early=[near], during=during)
    spread_share(both, sums, *share)
    join_tiles(sums, whole)
    after, state = stepped(rt_ref[...], rel_state_ref[...], whole[...])
    rt_out[...] = after[:, 0 : rt_out.shape[1]]
    rel_state_out[...] = state[:, 0 : rt_out.shape[1]]


def entity_step(number, et_ref, state_ref, gt_ref, gs_ref, meta_ref, state_out):
    source = spots(meta_ref[number, 0:1, 0 : gs_ref.shape[1]], et_ref.shape[1])
    grad = gt_ref[...] + dot_exact(split(gs_ref[...]), source, NT)
    after, state_out[...] = stepped(et_ref[...], state_ref[...], grad)
    return after


def stepped(param, state, grad):
    new_state = state + jnp.sum(grad * grad, axis=0, keepdims=True) * (1.0 / grad.shape[0])
    return param - RATE * grad / jnp.sqrt(new_state), new_state


def body(entities, entity_state, relations, relation_state, edges, negatives, counts):
    rows, dim = entities.shape
    rels = relations.shape[0]
    rels_pad = -(-rels // LANES) * LANES
    slots = edges.shape[2]
    blocks, draws = negatives.shape[1:]
    dim_pad = -(-dim // LANES) * LANES
    tiles = dim // SUBLANES * (rels_pad // LANES)
    piece = (-(-tiles // (CORES * PLANE)), SUBLANES, LANES)
    pieces = (CORES, PLANE, *piece)
    halves = (2, dim, slots // 2)
    one = pltpu.VMEM(piece, F32)

    def array(*shape, kind=F32):
        return (shape, kind)

    def space(*shape, kind=F32):
        return pltpu.VMEM(shape, kind)

    def table_spaces():
        return [
            space(dim_pad, rows),
            space(rows, dim_pad, kind=BF16),
            space(rows, dim_pad, kind=BF16),
            space(dim, rows, kind=BF16),
            space(dim, rows, kind=BF16),
            space(rels_pad, slots, kind=BF16),
            space(dim, slots),
            space(dim, rels_pad),
            space(*halves[1:]),
            space(*halves[1:]),
        ]

    def total_spaces():
        return (
            [space(ZS, *piece), one, *pairs(ZS)]
            + [one] * (ZS + 3 * PLANE)
            + pairs(PLANE, PLANE)
            + [one] * (2 * PLANE)
            + pairs(PLANE, PLANE)
        )

    meta_shape = (2, 4 + blocks, rows)
    grads = [array(dim, rows), array(dim, slots), array(*pieces)]
    et = entities.T
    state = entity_state.reshape(1, rows)
    rel_state = relation_state.reshape(1, rels)
    gt, gs, h, rt, meta, meta1, c1 = call(
        front_kernel,
        grads
        + [
            array(dim, rels_pad),
            array(*meta_shape, kind=jnp.int32),
            array(*meta_shape[1:], kind=jnp.int32),
            array(rows, slots),
        ],
        [et, relations.T, edges.transpose(1, 0, 2), negatives, counts.T],
        [space(*meta_shape[1:], kind=jnp.int32), space(rows, slots), space(*halves), space(*halves)]
        + table_spaces()
        + pairs(4),
        name="front",
        collective=0,
    )
    h, et, state, their_rows = call(
        first_total_kernel,
        [array(*pieces), array(dim, rows), array(1, rows), array(*halves)],
        [h, et, state, gt, gs, meta],
        [space(dim, slots), space(*halves), one, *pairs(4)] + total_spaces(),
        name="first_total",
        collective=1,
    )
    gt, gs, h, rt, rel_state = call(
        second_main_kernel,
        grads + [array(dim, rels_pad), array(1, rels_pad)],
        [et, rt, rel_state, h, their_rows, meta1, c1],
        table_spaces() + [space(1, rels_pad)],
        name="second_main",
    )
    et, state, rt, rel_state = call(
        last_total_kernel,
        [array(dim, rows), array(1, rows), array(dim, rels), array(1, rels)],
        [h, et, state, gt, gs, meta, rt, rel_state],
        [space(dim, slots), one, space(*pieces), space(dim, rels_pad), *pairs(1)] + total_spaces(),
        name="last_total",
        collective=2,
    )
    return et.T, state.reshape(rows), rt.T, rel_state.reshape(rels)


def solution(mesh):
    return jax.shard_map(
        body,
        mesh=mesh,
        in_specs=(
            P("dom", None),
            P("dom"),
            P(),
            P(),
            P(None, None, "dom"),
            P(None, "dom", None),
            P(None, "dom"),
        ),
        out_specs=(P("dom", None), P("dom"), P(), P()),
        check_vma=False,
    )
```

time: 156 us -> 136 us (0.87)
  local copies, waits for them, and re-layouts: 13.3 us -> 5.01 us
  Pallas kernels: 136 us -> 128 us
  starting transfers between devices: 5.28 us -> 0 us
    unnamed x19 -> x7, local copies, waits for them, and re-layouts: 12 us -> 3.71 us
    pallas_call x7 -> x4, Pallas kernels: 136 us -> 128 us  [call(): pl.pallas_call(kernel, out_shape=[jax.ShapeDtypeStruct(*out) for out in o...]
    ppermute x1 -> x0, starting transfers between devices: 5.28 us -> none  [swapped(): lax.ppermute(value, 'dom', [(low, low ^ 1 << apart) for low in range(coun...]
  transfers between devices with their start and end apart: 1 -> 0, of which waited for: 0 -> 0; matrix products, arithmetic and copies ran while one was open for 0% -> 0% of each run, Pallas kernels for 22% -> 0%
where the time goes in v7:
time: 136 us; the launch traced here: 135 us
  Pallas kernels  128 us (94%)
  local copies, waits for them, and re-layouts  5.01 us (4%)
  other arithmetic  1.4 us (1%)
    pallas_call x4, Pallas kernels, call(): pl.pallas_call(kernel, out_shape=[jax.ShapeDtypeStruct(*out) for out in o...  128 us
    unnamed x7, local copies, waits for them, and re-layouts  3.71 us

profile of v7, /device:TPU:1, one launch (start us, length us, event | category | flops | bytes accessed | tf_op | source)
XLA Modules:
  0.0 135.2 jit_solution(3049850741130694660)
XLA Ops:
  0.6 1.3 reshape.21.rel_state_ref
  1.9 28.1 %front.1 = (f32[200,1024]{1,0:T(8,128)}, f32[200,512]{1,0:T(8,128)}, f32[2,16,9,8,128]{4,3,2,1,0:T(8,128)}, f32[200,1408]{1,0:T(8,128)}, s32[2,8,1024]{2,1,0:T(8...) custom-call(f32[200,1024]{1,0:T(8,128)} %bitcast.8, f32[200,1345]{1,0:T(8,128)} %bitcast.10, s32[3,2,512]{2,1,0:T(2,128)} %bitcast.13, ...), custom_call_target="tpu_custom_call" | custom-call | tf_op jit(solution)/shard_map/front/pallas_call | solution.py:52
  30.1 51.2 %first_total.1 = (f32[2,16,9,8,128]{4,3,2,1,0:T(8,128)}, f32[200,1024]{1,0:T(8,128)}, f32[1,1024]{1,0:T(1,128)}, f32[2,200,256]{2,1,0:T(8,128)}) custom-call(f32[2,16,9,8,128]{4,3,2,1,0:T(8,128)} %get-tuple-element.24.h_ref, f32[200,1024]{1,0:T(8,128)} %bitcast.9, f32[1,1024]{1,0:T(1,128)} %bitcast.14, f32[200,1024]{1,0:T(8,128)} %get-tuple-element.25.gt_ref, ...), custom_call_target="tpu_custom_call" | custom-call | tf_op jit(solution)/shard_map/first_total/pallas_call | solution.py:52
  81.3 10.0 %second_main.1 = (f32[200,1024]{1,0:T(8,128)}, f32[200,512]{1,0:T(8,128)}, f32[2,16,9,8,128]{4,3,2,1,0:T(8,128)}, f32[200,1408]{1,0:T(8,128)}, f32[1,1408]{1,0:T(1,128)}) custom-call(f32[200,1024]{1,0:T(8,128)} %get-tuple-element.28.et_ref, f32[200,1408]{1,0:T(8,128)} %get-tuple-element.29.rt_ref, f32[1,1345]{1,0:T(1,128)} %reshape.21.rel_state_ref, ...), custom_call_target="tpu_custom_call" | custom-call | tf_op jit(solution)/shard_map/second_main/pallas_call | solution.py:52
  91.3 38.8 %last_total.1 = (f32[200,1024]{1,0:T(8,128)}, f32[1,1024]{1,0:T(1,128)}, f32[200,1345]{1,0:T(8,128)}, f32[1,1345]{1,0:T(1,128)}) custom-call(f32[2,16,9,8,128]{4,3,2,1,0:T(8,128)} %get-tuple-element.34.h_ref, f32[200,1024]{1,0:T(8,128)} %get-tuple-element.28.et_ref, f32[1,1024]{1,0:T(1,128)} %get-tuple-element.35.state_ref, ...), custom_call_target="tpu_custom_call" | custom-call | tf_op jit(solution)/shard_map/last_total/pallas_call | solution.py:52
  130.1 0.0 copy-start.1
  130.1 0.0 copy-start
  130.1 1.4 %reduce = f32[1345]{0:T(1024)} reduce(f32[1,1345]{1,0:T(1,128)} %get-tuple-element.43, f32[]{:T(128)} %constant.2), dimensions={0}, to_apply=%get-tuple-element.43.reduce_sub_computation | reduce | bytes 10764 | tf_op jit(solution)/shard_map/last_total/pallas_call | solution.py:52
  131.5 2.1 %copy.14 = f32[1024,200]{0,1:T(8,128)} copy(f32[1024,200]{0,1:T(8,128)} %bitcast.12) | data formatting | bytes 1638400
  133.6 0.0 copy-done.1
  133.6 0.6 copy.15
  134.2 0.0 copy-done
  134.2 1.0 copy.16
Async XLA Ops:
  130.1 3.5 %copy-start.1 = (f32[1,1024]{1,0:T(1,128)S(1)}, f32[1,1024]{1,0:T(1,128)}, u32[]{:S(2)}) copy-start(f32[1,1024]{1,0:T(1,128)} %get-tuple-element.41) | copy-start | bytes 12292
  130.1 4.1 %copy-start = (f32[200,1345]{1,0:T(8,128)S(1)}, f32[200,1345]{1,0:T(8,128)}, u32[]{:S(2)}) copy-start(f32[200,1345]{1,0:T(8,128)} %get-tuple-element.42) | copy-start | bytes 3228004

commit v8 on v7

--- a/solution.py
+++ b/solution.py
@@ -128,8 +128,8 @@
         h_ref[place] = jnp.zeros((SUBLANES, LANES), F32)
 
 
-def front_kernel(
-    et_ref, r_ref, edges_ref, neg_ref, counts_ref,
+def front(
+    everyone, et_ref, r_ref, edges_ref, neg_ref, counts_ref,
     gt_ref, gs_ref, h_ref, rt_ref, meta_ref, meta1_ref, c1_ref,
     meta0, c0, st, rows, wide, eh, el, eth, etl, picks, w, h_sum, q, tmp, ss, rs,
 ):
@@ -139,7 +139,7 @@
     parts, _, width = st.shape
     c, y, x, z = places_of()
     far, near = device((z + ZS // 2) % ZS, x, y, c), other_core()
-    greet([far, near])
+    greet(everyone)
     eth[...], etl[...] = split(et_ref[...])
     meta_ref[...] = jnp.full(meta_ref.shape, -1, jnp.int32)
     for r in range(rounds):
@@ -154,7 +154,7 @@
         source = meta_ref[0, 0:1, p * width : (p + 1) * width]
         st[p] = dot_exact((eth[...], etl[...]), spots(source, count))
         if p == 0:
-            await_peers([far, near])
+            await_peers(everyone)
             sends[parts].start()
             sends[parts + 1].start()
         sends[p].start()
@@ -178,16 +178,13 @@
         one.wait_send()
 
 
-def second_main_kernel(
+def second_main(
     et_ref, rt_ref, rel_state_ref, sum_ref, rows, meta_ref, c_ref,
     gt_ref, gs_ref, h_ref, rt_out, rel_state_out,
-    wide, eh, el, eth, etl, picks, w, h_sum, q, tmp, state,
+    wide, eh, el, eth, etl, picks, w, h_sum, q, tmp,
 ):
-    rels = rel_state_ref.shape[1]
     join_tiles(sum_ref, h_sum)
-    state[...] = jnp.ones_like(state)
-    state[:, 0:rels] = rel_state_ref[...]
-    rt_out[...], rel_state_out[...] = stepped(rt_ref[...], state[...], h_sum[...])
+    rt_out[...], rel_state_out[...] = stepped(rt_ref[...], rel_state_ref[...], h_sum[...])
     table_parts(et_ref, wide, (eh, el), (eth, etl))
     relation_rows(rt_out, meta_ref, picks, w)
     for p in range(rows.shape[0]):
@@ -240,11 +237,6 @@
     pl.semaphore_wait(pltpu.get_barrier_semaphore(), len(peers))
 
 
-def meet(peers):
-    greet(peers)
-    await_peers(peers)
-
-
 def other_core():
     c, y, x, z = places_of()
     return device(z, x, y, 1 - c)
@@ -265,13 +257,12 @@
     return [device((z + k) % ZS, x, y, c) for k in range(ZS)]
 
 
-def spread_sum(h_ref, out_ref, *more, beside=(), also=()):
+def spread_sum(h_ref, out_ref, *more, beside=()):
     s0, r0, s1, r1 = more[-4:]
     acc, got0, got1 = (more[i * PLANE : (i + 1) * PLANE] for i in range(3))
     other = other_core()
     plane = in_plane()
     c = places_of()[0]
-    meet([other, *(p[0] for p in plane[1:]), *also])
     order = range(PLANE - 1, -1, -1)
     first = [remote(h_ref.at[1 - c, plane[k][1]], got0[k], (s0, r0), k, other) for k in range(PLANE)]
     second = [None] + [remote(acc[k], got1[k], (s1, r1), k, plane[k][0]) for k in range(1, PLANE)]
@@ -298,7 +289,7 @@
     got2, more = more[:ZS], more[ZS:]
     c, y, x, z = places_of()
     column = in_column()
-    spread_sum(h_ref, part, *more, beside=early, also=column[1:])
+    spread_sum(h_ref, part, *more, beside=early)
     third = [None] + [remote(part, got2[k], (s2, r2), k, column[k]) for k in range(1, ZS)]
     for k in (4, 3, 5, 2, 6, 1, 7):
         third[k].start()
@@ -344,7 +335,7 @@
         one.wait_send()
 
 
-def first_total_kernel(
+def first_total(
     h_ref, et_ref, state_ref, gt_ref, gs_ref, meta_ref,
     sums_ref, et_out, state_out, rows_out,
     gs_in, mine, both, sx, rx, *more,
@@ -376,7 +367,7 @@
         one.wait()
 
 
-def last_total_kernel(
+def last_total(
     h_ref, et_ref, state_ref, gt_ref, gs_ref, meta_ref, rt_ref, rel_state_ref,
     et_out, state_out, rt_out, rel_state_out,
     gs_in, both, sums, whole, sx, rx, *more,
@@ -393,7 +384,42 @@
     join_tiles(sums, whole)
     after, state = stepped(rt_ref[...], rel_state_ref[...], whole[...])
     rt_out[...] = after[:, 0 : rt_out.shape[1]]
-    rel_state_out[...] = state[:, 0 : rt_out.shape[1]]
+    rel_state_out[...] = state
+
+
+def step_kernel(sizes, *refs):
+    refs = list(refs)
+
+    def take(count):
+        taken, refs[:count] = refs[:count], []
+        return taken
+
+    et, state, r, rel_state, edges, neg, counts = take(7)
+    et_out, state_out, rt_out, rel_state_out = take(4)
+    gt, gs, h, rt, meta, meta1, c1, meta0, c0, st, rows = take(11)
+    table = take(10)
+    front_sems = take(2)
+    sums, et1, state1, their_rows, gs_in, mine, both, sx, rx = take(9)
+    first_spaces = take(sizes)
+    gt1, gs1, h1, rt1, rel_state1 = take(5)
+    gs_in1, both1, sums1, sx1, rx1 = take(5)
+    last_spaces = take(sizes)
+    everyone = [other_core()] + [one[0] for one in in_plane()[1:]] + in_column()[1:]
+    front(
+        everyone, et, r, edges, neg, counts, gt, gs, h, rt, meta, meta1, c1, meta0, c0, st, rows,
+        *table, *front_sems,
+    )
+    first_total(
+        h, et, state, gt, gs, meta, sums, et1, state1, their_rows, gs_in, mine, both, sx, rx,
+        *first_spaces,
+    )
+    second_main(
+        et1, rt, rel_state, sums, their_rows, meta1, c1, gt1, gs1, h1, rt1, rel_state1, *table
+    )
+    last_total(
+        h1, et1, state1, gt1, gs1, meta, rt1, rel_state1, et_out, state_out, rt_out, rel_state_out,
+        gs_in1, both1, sums1, table[7], sx1, rx1, *last_spaces,
+    )
 
 
 def entity_step(number, et_ref, state_ref, gt_ref, gs_ref, meta_ref, state_out):
@@ -451,50 +477,32 @@
         )
 
     meta_shape = (2, 4 + blocks, rows)
-    grads = [array(dim, rows), array(dim, slots), array(*pieces)]
-    et = entities.T
-    state = entity_state.reshape(1, rows)
-    rel_state = relation_state.reshape(1, rels)
-    gt, gs, h, rt, meta, meta1, c1 = call(
-        front_kernel,
-        grads
-        + [
-            array(dim, rels_pad),
-            array(*meta_shape, kind=jnp.int32),
-            array(*meta_shape[1:], kind=jnp.int32),
-            array(rows, slots),
+    meta = space(*meta_shape, kind=jnp.int32)
+    one_meta = space(*meta_shape[1:], kind=jnp.int32)
+    grads = [space(dim, rows), space(dim, slots), space(*pieces)]
+    scratch = [*grads, space(dim, rels_pad), meta, one_meta, space(rows, slots), one_meta]
+    scratch += [space(rows, slots), space(*halves), space(*halves), *table_spaces(), *pairs(4)]
+    scratch += [space(*pieces), space(dim, rows), space(1, rows), space(*halves)]
+    scratch += [space(dim, slots), space(*halves), one, *pairs(4), *total_spaces()]
+    scratch += [*grads, space(dim, rels_pad), space(1, rels_pad)]
+    scratch += [space(dim, slots), one, space(*pieces), *pairs(1), *total_spaces()]
+    et, state, rt, rel_state = call(
+        functools.partial(step_kernel, len(total_spaces())),
+        [array(dim, rows), array(1, rows), array(dim, rels), array(1, rels_pad)],
+        [
+            entities.T,
+            entity_state.reshape(1, rows),
+            relations.T,
+            jnp.pad(relation_state, (0, rels_pad - rels), constant_values=1.0).reshape(1, rels_pad),
+            edges.transpose(1, 0, 2),
+            negatives,
+            counts.T,
         ],
-        [et, relations.T, edges.transpose(1, 0, 2), negatives, counts.T],
-        [space(*meta_shape[1:], kind=jnp.int32), space(rows, slots), space(*halves), space(*halves)]
-        + table_spaces()
-        + pairs(4),
-        name="front",
+        scratch,
+        name="step",
         collective=0,
     )
-    h, et, state, their_rows = call(
-        first_total_kernel,
-        [array(*pieces), array(dim, rows), array(1, rows), array(*halves)],
-        [h, et, state, gt, gs, meta],
-        [space(dim, slots), space(*halves), one, *pairs(4)] + total_spaces(),
-        name="first_total",
-        collective=1,
-    )
-    gt, gs, h, rt, rel_state = call(
-        second_main_kernel,
-        grads + [array(dim, rels_pad), array(1, rels_pad)],
-        [et, rt, rel_state, h, their_rows, meta1, c1],
-        table_spaces() + [space(1, rels_pad)],
-        name="second_main",
-    )
-    et, state, rt, rel_state = call(
-        last_total_kernel,
-        [array(dim, rows), array(1, rows), array(dim, rels), array(1, rels)],
-        [h, et, state, gt, gs, meta, rt, rel_state],
-        [space(dim, slots), one, space(*pieces), space(dim, rels_pad), *pairs(1)] + total_spaces(),
-        name="last_total",
-        collective=2,
-    )
-    return et.T, state.reshape(rows), rt.T, rel_state.reshape(rels)
+    return et.T, state.reshape(rows), rt.T, rel_state[0, :rels]
 
 
 def solution(mesh):

time: 136 us -> 119 us (0.88)
  Pallas kernels: 128 us -> 112 us
  local copies, waits for them, and re-layouts: 5.01 us -> 6.41 us
  other arithmetic: 1.4 us -> 0 us
    pallas_call x4 -> x1, Pallas kernels: 128 us -> 112 us  [call(): pl.pallas_call(kernel, out_shape=[jax.ShapeDtypeStruct(*out) for out in o...]
    pallas_call x1 -> x0, other arithmetic: 1.4 us -> none  [call(): pl.pallas_call(kernel, out_shape=[jax.ShapeDtypeStruct(*out) for out in o...]
    slice x0 -> x1, local copies, waits for them, and re-layouts: none -> 1.4 us  [body(): return (et.T, state.reshape(rows), rt.T, rel_state[0, :rels])]
where the time goes in v8:
time: 119 us
  Pallas kernels  112 us (94%)
  local copies, waits for them, and re-layouts  6.41 us (5%)
    pallas_call x1, Pallas kernels, call(): pl.pallas_call(kernel, out_shape=[jax.ShapeDtypeStruct(*out) for out in o...  112 us
    unnamed x7, local copies, waits for them, and re-layouts  3.71 us

profile of v8, /device:TPU:1, one launch (start us, length us, event | category | flops | bytes accessed | tf_op | source)
XLA Modules:
  0.0 119.3 jit_solution(6035762801401479406)
XLA Ops:
  0.6 0.7 pad.4
  1.3 0.6 reshape.18.refs_3_
  1.9 112.2 %step.1 = (f32[200,1024]{1,0:T(8,128)}, f32[1,1024]{1,0:T(1,128)}, f32[200,1345]{1,0:T(8,128)}, f32[1,1408]{1,0:T(1,128)}) custom-call(f32[200,1024]{1,0:T(8,128)} %bitcast.10, f32[1,1024]{1,0:T(1,128)} %bitcast.13, f32[200,1345]{1,0:T(8,128)} %bitcast.8, f32[1,1408]{1,0:T(1,128)} %reshape.18.refs_3_, s32[3,2,512]{2,1,0:T(2,128)} %bitcast.12, ...), custom_call_target="tpu_custom_call" | custom-call | tf_op jit(solution)/shard_map/step/pallas_call | solution.py:52
  114.2 0.0 copy-start.1
  114.2 0.0 copy-start
  114.2 1.4 %slice_reduce_fusion = f32[1345]{0:T(1024)} fusion(f32[1,1408]{1,0:T(1,128)} %get-tuple-element.11), kind=kLoop, calls=%fused_computation | loop fusion | bytes 10760 | tf_op jit(solution)/shard_map/slice | solution.py:505
  115.6 2.1 %copy.14 = f32[1024,200]{0,1:T(8,128)} copy(f32[1024,200]{0,1:T(8,128)} %bitcast.11) | data formatting | bytes 1638400
  117.7 0.0 copy-done.1
  117.7 0.6 copy.15
  118.3 0.0 copy-done
  118.3 1.0 copy.16
Async XLA Ops:
  114.2 3.5 %copy-start.1 = (f32[1,1024]{1,0:T(1,128)S(1)}, f32[1,1024]{1,0:T(1,128)}, u32[]{:S(2)}) copy-start(f32[1,1024]{1,0:T(1,128)} %get-tuple-element.9) | copy-start | bytes 12292
  114.2 4.1 %copy-start = (f32[200,1345]{1,0:T(8,128)S(1)}, f32[200,1345]{1,0:T(8,128)}, u32[]{:S(2)}) copy-start(f32[200,1345]{1,0:T(8,128)} %get-tuple-element.10) | copy-start | bytes 3228004

commit v9 on v8

--- a/solution.py
+++ b/solution.py
@@ -19,6 +19,14 @@
 ZS, XS, YS, CORES = 8, 4, 4, 2
 PLANE = XS * YS
 MESH = pl.DeviceIdType.MESH
+
+
+def ring(apart, count):
+    return min(apart, count - apart)
+
+
+BY_DEPTH = sorted(range(1, ZS), key=lambda k: -ring(k, ZS))
+BY_REACH = sorted(range(PLANE), key=lambda k: -ring(k // YS, XS) - ring(k % YS, YS))
 
 
 def split(value):
@@ -263,18 +271,20 @@
     other = other_core()
     plane = in_plane()
     c = places_of()[0]
-    order = range(PLANE - 1, -1, -1)
+    order = BY_REACH
     first = [remote(h_ref.at[1 - c, plane[k][1]], got0[k], (s0, r0), k, other) for k in range(PLANE)]
     second = [None] + [remote(acc[k], got1[k], (s1, r1), k, plane[k][0]) for k in range(1, PLANE)]
     for k in order:
         first[k].start()
     for one in beside:
         one.start()
+    last = 0
     for k in order:
         first[k].wait_recv()
         acc[k][...] = h_ref[c, plane[k][1]] + got0[k][...]
-        if k < PLANE - 1:
-            second[k + 1].start()
+        if last:
+            second[last].start()
+        last = k
     total = acc[0][...]
     for k in order[:-1]:
         second[k].wait_recv()
@@ -284,28 +294,44 @@
         one.wait_send()
 
 
-def spread_column(h_ref, out_ref, level, part, *more, early=(), late=(), during=None):
-    s2, r2, *more = more
-    got2, more = more[:ZS], more[ZS:]
-    c, y, x, z = places_of()
+def spread_column(
+    h_ref, out_ref, level, part, own, s2, r2, s5, r5, *more, early=(), middle=(), late=(), during=None
+):
+    pair, got2, got5 = (more[i * ZS : (i + 1) * ZS] for i in range(3))
+    more = more[3 * ZS :]
+    z = places_of()[3]
     column = in_column()
+    each = own.shape[0]
     spread_sum(h_ref, part, *more, beside=early)
-    third = [None] + [remote(part, got2[k], (s2, r2), k, column[k]) for k in range(1, ZS)]
-    for k in (4, 3, 5, 2, 6, 1, 7):
+    for k in range(ZS):
+        pair[k][0:each] = part[pl.ds((z + k) % ZS * each, each)]
+        pair[k][each:] = part[ZS * each :]
+    third = [None] + [remote(pair[k], got2[k], (s2, r2), k, column[k]) for k in range(1, ZS)]
+    for k in BY_DEPTH:
         third[k].start()
-    for one in late:
+    for one in middle:
         one.start()
-    level[z] = part[...]
-    if during is not None:
-        during()
-    for k in range(1, ZS):
+    level[z] = pair[0][...]
+    for k in BY_DEPTH:
         third[k].wait_recv()
         level[(z + ZS - k) % ZS] = got2[k][...]
     total = level[0]
     for k in range(1, ZS):
         total = total + level[k]
-    out_ref[...] = total
-    for one in third[1:]:
+    own[...] = total[0:each]
+    given = [None] + [remote(own, got5[k], (s5, r5), k, column[k]) for k in range(1, ZS)]
+    for k in BY_DEPTH:
+        given[k].start()
+    for one in late:
+        one.start()
+    out_ref[ZS * each :] = total[each:]
+    out_ref[pl.ds(z * each, each)] = total[0:each]
+    if during is not None:
+        during()
+    for k in BY_DEPTH:
+        given[k].wait_recv()
+        out_ref[pl.ds((z + ZS - k) % ZS * each, each)] = got5[k][...]
+    for one in third[1:] + given[1:]:
         one.wait_send()
 
 
@@ -315,7 +341,7 @@
     other = other_core()
     plane = in_plane()
     c = places_of()[0]
-    order = range(PLANE - 1, 0, -1)
+    order = BY_REACH[:-1]
     fourth = [None] + [remote(h_ref, got3[k], (s3, r3), k, plane[k][0]) for k in range(1, PLANE)]
     fifth = [remote(got3[k] if k else h_ref, got4[k], (s4, r4), k, other) for k in range(PLANE)]
     for k in order:
@@ -344,12 +370,12 @@
     far = device((z + ZS // 2) % ZS, x, y, c)
     dim = gs_ref.shape[0]
     parts, _, width = mine.shape
-    cut = dim // 2 // SUBLANES * SUBLANES
-    ends = [(0, cut), (cut, dim)]
+    cuts = [dim * share // 100 // SUBLANES * SUBLANES for share in (0, 45, 70)] + [dim]
+    ends = list(zip(cuts[:-1], cuts[1:]))
     back = [remote(gs_ref.at[a:b], gs_in.at[a:b], (sx, rx), i, far) for i, (a, b) in enumerate(ends)]
-    on = [remote(mine.at[p], rows_out.at[p], (sx, rx), 2 + p, other_core()) for p in range(parts)]
+    on = [remote(mine.at[p], rows_out.at[p], (sx, rx), 3 + p, other_core()) for p in range(parts)]
     more, share = more[: -2 * PLANE - 4], more[-2 * PLANE - 4 :]
-    spread_column(h_ref, both, *more, early=back[:1], late=back[1:])
+    spread_column(h_ref, both, *more, early=back[:1], middle=back[1:2], late=back[2:])
 
     def beside():
         for one in back:
@@ -394,14 +420,14 @@
         taken, refs[:count] = refs[:count], []
         return taken
 
-    et, state, r, rel_state, edges, neg, counts = take(7)
+    et, state, r, rel_state_flat, edges, neg, counts = take(7)
     et_out, state_out, rt_out, rel_state_out = take(4)
     gt, gs, h, rt, meta, meta1, c1, meta0, c0, st, rows = take(11)
     table = take(10)
     front_sems = take(2)
     sums, et1, state1, their_rows, gs_in, mine, both, sx, rx = take(9)
     first_spaces = take(sizes)
-    gt1, gs1, h1, rt1, rel_state1 = take(5)
+    gt1, gs1, h1, rt1, rel_state1, rel_state = take(6)
     gs_in1, both1, sums1, sx1, rx1 = take(5)
     last_spaces = take(sizes)
     everyone = [other_core()] + [one[0] for one in in_plane()[1:]] + in_column()[1:]
@@ -413,6 +439,8 @@
         h, et, state, gt, gs, meta, sums, et1, state1, their_rows, gs_in, mine, both, sx, rx,
         *first_spaces,
     )
+    rel_state[...] = jnp.ones_like(rel_state)
+    rel_state[0, 0 : rel_state_flat.shape[0]] = rel_state_flat[...]
     second_main(
         et1, rt, rel_state, sums, their_rows, meta1, c1, gt1, gs1, h1, rt1, rel_state1, *table
     )
@@ -420,6 +448,13 @@
         h1, et1, state1, gt1, gs1, meta, rt1, rel_state1, et_out, state_out, rt_out, rel_state_out,
         gs_in1, both1, sums1, table[7], sx1, rx1, *last_spaces,
     )
+
+
+def finish_kernel(et_ref, state_ref, rt_ref, rel_state_ref, et_out, state_out, rt_out, rel_state_out):
+    et_out[...] = et_ref[...]
+    rt_out[...] = rt_ref[...]
+    state_out[...] = state_ref[0]
+    rel_state_out[...] = rel_state_ref[0, 0 : rel_state_out.shape[0]]
 
 
 def entity_step(number, et_ref, state_ref, gt_ref, gs_ref, meta_ref, state_out):
@@ -445,7 +480,9 @@
     piece = (-(-tiles // (CORES * PLANE)), SUBLANES, LANES)
     pieces = (CORES, PLANE, *piece)
     halves = (2, dim, slots // 2)
-    one = pltpu.VMEM(piece, F32)
+    each = piece[0] // ZS
+    pair = (piece[0] - (ZS - 1) * each, SUBLANES, LANES)
+    one, own = pltpu.VMEM(piece, F32), pltpu.VMEM((each, SUBLANES, LANES), F32)
 
     def array(*shape, kind=F32):
         return (shape, kind)
@@ -469,8 +506,10 @@
 
     def total_spaces():
         return (
-            [space(ZS, *piece), one, *pairs(ZS)]
-            + [one] * (ZS + 3 * PLANE)
+            [space(ZS, *pair), one, own, *pairs(ZS, ZS)]
+            + [space(*pair)] * (2 * ZS)
+            + [own] * ZS
+            + [one] * (3 * PLANE)
             + pairs(PLANE, PLANE)
             + [one] * (2 * PLANE)
             + pairs(PLANE, PLANE)
@@ -483,8 +522,8 @@
     scratch = [*grads, space(dim, rels_pad), meta, one_meta, space(rows, slots), one_meta]
     scratch += [space(rows, slots), space(*halves), space(*halves), *table_spaces(), *pairs(4)]
     scratch += [space(*pieces), space(dim, rows), space(1, rows), space(*halves)]
-    scratch += [space(dim, slots), space(*halves), one, *pairs(4), *total_spaces()]
-    scratch += [*grads, space(dim, rels_pad), space(1, rels_pad)]
+    scratch += [space(dim, slots), space(*halves), one, *pairs(5), *total_spaces()]
+    scratch += [*grads, space(dim, rels_pad), space(1, rels_pad), space(1, rels_pad)]
     scratch += [space(dim, slots), one, space(*pieces), *pairs(1), *total_spaces()]
     et, state, rt, rel_state = call(
         functools.partial(step_kernel, len(total_spaces())),
@@ -493,7 +532,7 @@
             entities.T,
             entity_state.reshape(1, rows),
             relations.T,
-            jnp.pad(relation_state, (0, rels_pad - rels), constant_values=1.0).reshape(1, rels_pad),
+            relation_state,
             edges.transpose(1, 0, 2),
             negatives,
             counts.T,
@@ -502,7 +541,13 @@
         name="step",
         collective=0,
     )
-    return et.T, state.reshape(rows), rt.T, rel_state[0, :rels]
+    et, state, rt, rel_state = call(
+        finish_kernel,
+        [array(dim, rows), array(rows), array(dim, rels), array(rels)],
+        [et, state, rt, rel_state],
+        name="finish",
+    )
+    return et.T, state, rt.T, rel_state
 
 
 def solution(mesh):

time: 119 us -> 114 us (0.958)
  local copies, waits for them, and re-layouts: 6.41 us -> 0 us
    unnamed x7 -> x0, local copies, waits for them, and re-layouts: 3.71 us -> none
    slice x1 -> x0, local copies, waits for them, and re-layouts: 1.4 us -> none  [body(): return (et.T, state.reshape(rows), rt.T, rel_state[0, :rels])]
    pallas_call x1 -> x2, Pallas kernels: 112 us -> 113 us  [call(): pl.pallas_call(kernel, out_shape=[jax.ShapeDtypeStruct(*out) for out in o...]
where the time goes in v9:
time: 114 us
  Pallas kernels  113 us (99%)
    pallas_call x2, Pallas kernels, call(): pl.pallas_call(kernel, out_shape=[jax.ShapeDtypeStruct(*out) for out in o...  113 us

profile of v9, /device:TPU:1, one launch (start us, length us, event | category | flops | bytes accessed | tf_op | source)
XLA Modules:
  0.0 113.9 jit_solution(17501110234646723764)
XLA Ops:
  0.6 110.5 %step.1 = (f32[200,1024]{1,0:T(8,128)}, f32[1,1024]{1,0:T(1,128)}, f32[200,1345]{1,0:T(8,128)}, f32[1,1408]{1,0:T(1,128)}) custom-call(f32[200,1024]{1,0:T(8,128)} %bitcast.8, f32[1,1024]{1,0:T(1,128)} %bitcast.10, f32[200,1345]{1,0:T(8,128)} %bitcast.7, f32[1345]{0:T(1024)} %refs_3_.1, s32[3,2,512]{2,1,0:T(2,128)} %bitcast.9, s32[2,4,1000]{2,1,0:T(4,128)} %refs_5_.1, ...), custom_call_target="tpu_custom_call" | custom-call | tf_op jit(solution)/shard_map/step/pallas_call | solution.py:60
  111.1 2.8 %finish.1 = (f32[200,1024]{1,0:T(8,128)}, f32[1024]{0:T(1024)}, f32[200,1345]{1,0:T(8,128)}, f32[1345]{0:T(1024)}) custom-call(f32[200,1024]{1,0:T(8,128)} %get-tuple-element.12.et_ref, f32[1,1024]{1,0:T(1,128)} %get-tuple-element.13.state_ref, f32[200,1345]{1,0:T(8,128)} %get-tuple-element.14.rt_ref, f32[1,1408]{1,0:T(1,128)} %get-tuple-element.15.rel_state_ref), custom_call_target="tpu_custom_call" | custom-call | tf_op jit(solution)/shard_map/finish/pallas_call | solution.py:60

commit v10 on v9

--- a/solution.py
+++ b/solution.py
@@ -189,13 +189,13 @@
 def second_main(
     et_ref, rt_ref, rel_state_ref, sum_ref, rows, meta_ref, c_ref,
     gt_ref, gs_ref, h_ref, rt_out, rel_state_out,
-    wide, eh, el, eth, etl, picks, w, h_sum, q, tmp,
+    arriving, wide, eh, el, eth, etl, picks, w, h_sum, q, tmp,
 ):
     join_tiles(sum_ref, h_sum)
     rt_out[...], rel_state_out[...] = stepped(rt_ref[...], rel_state_ref[...], h_sum[...])
-    table_parts(et_ref, wide, (eh, el), (eth, etl))
     relation_rows(rt_out, meta_ref, picks, w)
     for p in range(rows.shape[0]):
+        arriving[p].wait_recv()
         edge_part(
             p, (eh, el), (eth, etl), rows.at[p], meta_ref, c_ref, picks, w, gt_ref, gs_ref, h_sum, q, tmp
         )
@@ -364,13 +364,13 @@
 def first_total(
     h_ref, et_ref, state_ref, gt_ref, gs_ref, meta_ref,
     sums_ref, et_out, state_out, rows_out,
-    gs_in, mine, both, sx, rx, *more,
+    gs_in, mine, both, sx, rx, *more, prepare,
 ):
     c, y, x, z = places_of()
     far = device((z + ZS // 2) % ZS, x, y, c)
     dim = gs_ref.shape[0]
     parts, _, width = mine.shape
-    cuts = [dim * share // 100 // SUBLANES * SUBLANES for share in (0, 45, 70)] + [dim]
+    cuts = [dim * share // 100 // SUBLANES * SUBLANES for share in (0, 55, 80)] + [dim]
     ends = list(zip(cuts[:-1], cuts[1:]))
     back = [remote(gs_ref.at[a:b], gs_in.at[a:b], (sx, rx), i, far) for i, (a, b) in enumerate(ends)]
     on = [remote(mine.at[p], rows_out.at[p], (sx, rx), 3 + p, other_core()) for p in range(parts)]
@@ -388,9 +388,10 @@
             mine[p] = dot_exact(pieces, spots(source, after.shape[1]))
             on[p].start()
 
+        prepare()
+
     spread_share(both, sums_ref, *share, beside=beside)
-    for one in on:
-        one.wait()
+    return on
 
 
 def last_total(
@@ -435,15 +436,19 @@
         everyone, et, r, edges, neg, counts, gt, gs, h, rt, meta, meta1, c1, meta0, c0, st, rows,
         *table, *front_sems,
     )
-    first_total(
+    arriving = first_total(
         h, et, state, gt, gs, meta, sums, et1, state1, their_rows, gs_in, mine, both, sx, rx,
         *first_spaces,
+        prepare=lambda: table_parts(et1, table[0], table[1:3], table[3:5]),
     )
     rel_state[...] = jnp.ones_like(rel_state)
     rel_state[0, 0 : rel_state_flat.shape[0]] = rel_state_flat[...]
     second_main(
-        et1, rt, rel_state, sums, their_rows, meta1, c1, gt1, gs1, h1, rt1, rel_state1, *table
-    )
+        et1, rt, rel_state, sums, their_rows, meta1, c1, gt1, gs1, h1, rt1, rel_state1,
+        arriving, *table,
+    )
+    for one in arriving:
+        one.wait_send()
     last_total(
         h1, et1, state1, gt1, gs1, meta, rt1, rel_state1, et_out, state_out, rt_out, rel_state_out,
         gs_in1, both1, sums1, table[7], sx1, rx1, *last_spaces,

time: 114 us -> 113 us (level)
  no operation moved by 1% of the time
where the time goes in v10:
time: 113 us
  Pallas kernels  112 us (99%)
    pallas_call x2, Pallas kernels, call(): pl.pallas_call(kernel, out_shape=[jax.ShapeDtypeStruct(*out) for out in o...  112 us

profile of v10, /device:TPU:1, one launch (start us, length us, event | category | flops | bytes accessed | tf_op | source)
XLA Modules:
  0.0 112.9 jit_solution(10864422943845679928)
XLA Ops:
  0.6 109.4 %step.1 = (f32[200,1024]{1,0:T(8,128)}, f32[1,1024]{1,0:T(1,128)}, f32[200,1345]{1,0:T(8,128)}, f32[1,1408]{1,0:T(1,128)}) custom-call(f32[200,1024]{1,0:T(8,128)} %bitcast.8, f32[1,1024]{1,0:T(1,128)} %bitcast.10, f32[200,1345]{1,0:T(8,128)} %bitcast.7, f32[1345]{0:T(1024)} %refs_3_.1, s32[3,2,512]{2,1,0:T(2,128)} %bitcast.9, s32[2,4,1000]{2,1,0:T(4,128)} %refs_5_.1, ...), custom_call_target="tpu_custom_call" | custom-call | tf_op jit(solution)/shard_map/step/pallas_call | solution.py:60
  110.0 2.8 %finish.1 = (f32[200,1024]{1,0:T(8,128)}, f32[1024]{0:T(1024)}, f32[200,1345]{1,0:T(8,128)}, f32[1345]{0:T(1024)}) custom-call(f32[200,1024]{1,0:T(8,128)} %get-tuple-element.12.et_ref, f32[1,1024]{1,0:T(1,128)} %get-tuple-element.13.state_ref, f32[200,1345]{1,0:T(8,128)} %get-tuple-element.14.rt_ref, f32[1,1408]{1,0:T(1,128)} %get-tuple-element.15.rel_state_ref), custom_call_target="tpu_custom_call" | custom-call | tf_op jit(solution)/shard_map/finish/pallas_call | solution.py:60
